TPU v7x, 32 devices: a whole 2x2x4 slice. The times are simulated.
32 devices in a mesh: rep: 4 (over z), shard: 8 (over y, x, core).
Axes of the slice: x: 2, y: 2, z: 4, core: 2. Of those that a mesh axis runs over, the one named last changes fastest.
Arguments:
- tokens: bfloat16 [32, 1024, 768], P(('rep', 'shard')), may hold values from -6 to 6
- cotangent: bfloat16 [32, 1024, 768], P(('rep', 'shard')), may hold values from -6 to 6
- lengths: int32 [4, 8], P('rep'), may hold values from 1 to 1024, 5120 in all within a row
- dealing: int32 [4, 8], P('rep'), may hold values from 0 to 7, each once within a row
- drop_flags: int32 [4, 8], P('rep'), may hold values 0 or 1
- query_weight: float32 [768, 768], P('shard'), may hold values from -0.3125 to 0.3125
- key_weight: float32 [768, 768], P('shard'), may hold values from -0.21875 to 0.21875
- value_weight: float32 [768, 768], P('shard'), may hold values from -0.21875 to 0.21875
- out_weight: float32 [768, 768], P('shard'), may hold values from -0.875 to 0.875
- up_weight: float32 [768, 3072], P('shard'), may hold values from -0.21875 to 0.21875
- down_weight: float32 [3072, 768], P('shard'), may hold values from -0.109375 to 0.109375
- query_bias: float32 [768], P('shard'), may hold values from -3 to 3
- value_bias: float32 [768], P('shard'), may hold values from -3 to 3
- out_bias: float32 [768], P('shard'), may hold values from -3 to 3
- attn_gain: float32 [768], P('shard'), may hold values from 0.5 to 1.5
- attn_shift: float32 [768], P('shard'), may hold values from -2 to 2
- up_bias: float32 [3072], P('shard'), may hold values from -3 to 3
- down_bias: float32 [768], P('shard'), may hold values from -3 to 3
- final_gain: float32 [768], P('shard'), may hold values from 0.5 to 1.5
- final_shift: float32 [768], P('shard'), may hold values from -2 to 2
Outputs:
- output: bfloat16 [32, 1024, 768], P(('rep', 'shard'))
- input_grad: bfloat16 [32, 1024, 768], P(('rep', 'shard'))
- grad_query_weight: float32 [768, 768], P('shard')
- grad_key_weight: float32 [768, 768], P('shard')
- grad_value_weight: float32 [768, 768], P('shard')
- grad_out_weight: float32 [768, 768], P('shard')
- grad_up_weight: float32 [768, 3072], P('shard')
- grad_down_weight: float32 [3072, 768], P('shard')
- grad_query_bias: float32 [768], P('shard')
- grad_value_bias: float32 [768], P('shard')
- grad_out_bias: float32 [768], P('shard')
- grad_attn_gain: float32 [768], P('shard')
- grad_attn_shift: float32 [768], P('shard')
- grad_up_bias: float32 [3072], P('shard')
- grad_down_bias: float32 [768], P('shard')
- grad_final_gain: float32 [768], P('shard')
- grad_final_shift: float32 [768], P('shard')
Inputs may be any that keep to these rules, and one draw needn't show every extreme that they name: `lengths`: each row sums to 5120 and holds 1024 at least once. `dealing`: each row is a permutation.
All inputs are finite; a program needn't handle non-finite values. No bound on the sum of `drop_flags` on one device may be relied on, other than what follows from the above.
Results may differ from a plain program's by a relative error of at most 0.019.
Values may be sent and summed in bfloat16 or wider, within the bound.
A program may use at most 256 MiB of HBM per device.

v0:
```python
import math

import jax
import jax.numpy as jnp
from jax import lax
from jax.sharding import PartitionSpec as P

D = 768
HEADS = 12
HD = 64
LEN = 1024


def for_sending(value):
    return jax.tree.map(lambda a: a.astype(jnp.bfloat16) if a.dtype == jnp.float32 else a, value)


def layer_stats(summed):
    center = jnp.mean(summed, axis=-1, keepdims=True)
    offset = summed - center
    inverse = lax.rsqrt(jnp.mean(offset * offset, axis=-1, keepdims=True) + 1e-05)
    return (offset * inverse, inverse)


def norm_backward(upstream, normed, inverse, gain):
    scaled = upstream * gain
    return inverse * (
        scaled
        - jnp.mean(scaled, axis=-1, keepdims=True)
        - normed * jnp.mean(scaled * normed, axis=-1, keepdims=True)
    )


def contract(left, right):
    return lax.dot_general(
        left, right, (((0,), (0,)), ((), ())), preferred_element_type=jnp.float32
    )


def through(left, right):
    return lax.dot_general(
        left, right, (((1,), (1,)), ((), ())), preferred_element_type=jnp.float32
    )


def score_block(query_blk, keys_seq, key_valid):
    scores = jnp.einsum("qhd,khd->hqk", query_blk, keys_seq, preferred_element_type=jnp.float32) * (
        1.0 / math.sqrt(HD)
    )
    return jnp.where(key_valid[None, None, :], scores, -1e30)


def attend_forward(queries, keys_seq, values_seq, length):
    key_valid = jnp.arange(LEN) < length

    def per_block(query_blk):
        scores = score_block(query_blk, keys_seq, key_valid)
        peaks = jnp.max(scores, axis=-1, keepdims=True)
        expons = jnp.exp(scores - peaks)
        totals = jnp.sum(expons, axis=-1, keepdims=True)
        probs = (expons / totals).astype(jnp.bfloat16)
        context = jnp.einsum("hqk,khd->qhd", probs, values_seq, preferred_element_type=jnp.float32)
        return (context.astype(jnp.bfloat16), peaks + jnp.log(totals))

    return lax.map(per_block, queries)


def attend_backward(queries, keys_seq, values_seq, dcontext, lse_seq, length):
    key_valid = jnp.arange(LEN) < length

    def per_block(carry, inputs):
        query_blk, dctx_blk, lse_blk = inputs
        scores = score_block(query_blk, keys_seq, key_valid)
        probs = jnp.where(key_valid[None, None, :], jnp.exp(scores - lse_blk), 0.0)
        dprobs = jnp.einsum(
            "qhd,khd->hqk", dctx_blk, values_seq, preferred_element_type=jnp.float32
        )
        deltas = jnp.sum(dprobs * probs, axis=-1, keepdims=True)
        dscores = (probs * (dprobs - deltas) * (1.0 / math.sqrt(HD))).astype(jnp.bfloat16)
        dquery = jnp.einsum(
            "hqk,khd->qhd", dscores, keys_seq, preferred_element_type=jnp.float32
        ).astype(jnp.bfloat16)
        dkeys = carry[0] + jnp.einsum(
            "hqk,qhd->khd", dscores, query_blk, preferred_element_type=jnp.float32
        )
        dvalues = carry[1] + jnp.einsum(
            "hqk,qhd->khd", probs.astype(jnp.bfloat16), dctx_blk, preferred_element_type=jnp.float32
        )
        return ((dkeys, dvalues), dquery)

    zeros_kv = jnp.zeros(keys_seq.shape, jnp.float32)
    (dkeys, dvalues), dquery = lax.scan(
        per_block, (zeros_kv, zeros_kv), (queries, dcontext, lse_seq)
    )
    return (dquery, dkeys.astype(jnp.bfloat16), dvalues.astype(jnp.bfloat16))


def body(
    tokens,
    cotangent,
    lengths,
    dealing,
    drop_flags,
    query_weight,
    key_weight,
    value_weight,
    out_weight,
    up_weight,
    down_weight,
    query_bias,
    value_bias,
    out_bias,
    attn_gain,
    attn_shift,
    up_bias,
    down_bias,
    final_gain,
    final_shift,
):
    masters = (
        query_weight,
        key_weight,
        value_weight,
        out_weight,
        up_weight,
        down_weight,
        query_bias,
        value_bias,
        out_bias,
        attn_gain,
        attn_shift,
        up_bias,
        down_bias,
        final_gain,
        final_shift,
    )
    per_device = tokens.shape[0]
    row_count = per_device * LEN
    block_rows = min(512, LEN)
    group_order = dealing[0]
    pieces = (
        lax.all_to_all(tokens, "shard", split_axis=1, concat_axis=0, tiled=True),
        lax.all_to_all(cotangent, "shard", split_axis=1, concat_axis=0, tiled=True),
    )
    placed = (jnp.take(pieces[0], group_order, axis=0), jnp.take(pieces[1], group_order, axis=0))
    local_tokens, local_cotan = (
        lax.all_to_all(placed[0], "shard", split_axis=0, concat_axis=1, tiled=True),
        lax.all_to_all(placed[1], "shard", split_axis=0, concat_axis=1, tiled=True),
    )
    first_slot = lax.axis_index("shard") * per_device
    my_order = lax.dynamic_slice_in_dim(group_order, first_slot, per_device)
    my_lengths = jnp.take(lengths[0], my_order)
    my_flags = lax.dynamic_slice_in_dim(drop_flags[0], first_slot, per_device)
    positions = jnp.arange(LEN)
    row_live = ((positions[None, :] < my_lengths[:, None]) & (my_flags[:, None] == 0)).reshape(
        row_count, 1
    )
    lowered = tuple((master.astype(jnp.bfloat16) for master in masters))
    gathered = jax.tree.map(
        lambda part, own: part.astype(own.dtype),
        lax.all_gather(for_sending(lowered), "shard", axis=0, tiled=True),
        lowered,
    )
    (
        query_full,
        key_full,
        value_full,
        out_full,
        up_full,
        down_full,
        query_add,
        value_add,
        out_add,
        attn_scale,
        attn_add,
        up_add,
        down_add,
        final_scale,
        final_add,
    ) = gathered

    def as_blocks(matrix):
        return matrix.reshape(per_device, LEN // block_rows, block_rows, HEADS, HD)

    def as_sequences(matrix):
        return matrix.reshape(per_device, LEN, HEADS, HD)

    flat_tokens = local_tokens.reshape(row_count, D)
    token_float = flat_tokens.astype(jnp.float32)
    queries = (
        jnp.dot(flat_tokens, query_full, preferred_element_type=jnp.float32)
        + query_add.astype(jnp.float32)
    ).astype(jnp.bfloat16)
    keys_all = jnp.dot(flat_tokens, key_full, preferred_element_type=jnp.float32).astype(
        jnp.bfloat16
    )
    values_all = (
        jnp.dot(flat_tokens, value_full, preferred_element_type=jnp.float32)
        + value_add.astype(jnp.float32)
    ).astype(jnp.bfloat16)
    contexts, lse_all = lax.map(
        lambda packed: attend_forward(packed[0], packed[1], packed[2], packed[3]),
        (as_blocks(queries), as_sequences(keys_all), as_sequences(values_all), my_lengths),
    )
    context = contexts.reshape(row_count, D)
    attended = jnp.dot(context, out_full, preferred_element_type=jnp.float32) + out_add.astype(
        jnp.float32
    )
    normed_one, inverse_one = layer_stats(token_float + attended)
    first = normed_one * attn_scale.astype(jnp.float32) + attn_add.astype(jnp.float32)
    first_low = first.astype(jnp.bfloat16)
    hidden = jnp.dot(first_low, up_full, preferred_element_type=jnp.float32) + up_add.astype(
        jnp.float32
    )
    active = jax.nn.gelu(hidden, approximate=False).astype(jnp.bfloat16)
    branch = jnp.dot(active, down_full, preferred_element_type=jnp.float32) + down_add.astype(
        jnp.float32
    )
    normed_two, inverse_two = layer_stats(first + branch)
    final = normed_two * final_scale.astype(jnp.float32) + final_add.astype(jnp.float32)
    output = jnp.where(row_live, final, token_float).astype(jnp.bfloat16)
    weights_back = jax.tree.map(
        lambda part, own: part.astype(own.dtype),
        lax.all_gather(for_sending(lowered), "shard", axis=0, tiled=True),
        lowered,
    )
    (
        query_full,
        key_full,
        value_full,
        out_full,
        up_full,
        down_full,
        query_add,
        value_add,
        out_add,
        attn_scale,
        attn_add,
        up_add,
        down_add,
        final_scale,
        final_add,
    ) = weights_back
    cotan_float = local_cotan.reshape(row_count, D).astype(jnp.float32)
    upstream = jnp.where(row_live, cotan_float, 0.0)
    grad_final_scale = jnp.sum(upstream * normed_two, axis=0)
    grad_final_add = jnp.sum(upstream, axis=0)
    dsum_two = norm_backward(upstream, normed_two, inverse_two, final_scale.astype(jnp.float32))
    dbranch = dsum_two.astype(jnp.bfloat16)
    grad_down_add = jnp.sum(dbranch.astype(jnp.float32), axis=0)
    grad_down = contract(active, dbranch)
    dactive = through(dbranch, down_full)
    slope = 0.5 * (1.0 + lax.erf(hidden * (1.0 / math.sqrt(2.0)))) + hidden * jnp.exp(
        -0.5 * hidden * hidden
    ) * (1.0 / math.sqrt(2.0 * math.pi))
    dhidden = (dactive * slope).astype(jnp.bfloat16)
    grad_up_add = jnp.sum(dhidden.astype(jnp.float32), axis=0)
    grad_up = contract(first_low, dhidden)
    dfirst = dsum_two + through(dhidden, up_full)
    grad_attn_scale = jnp.sum(dfirst * normed_one, axis=0)
    grad_attn_add = jnp.sum(dfirst, axis=0)
    dsum_one = norm_backward(dfirst, normed_one, inverse_one, attn_scale.astype(jnp.float32))
    dattended = dsum_one.astype(jnp.bfloat16)
    grad_out_add = jnp.sum(dattended.astype(jnp.float32), axis=0)
    grad_out = contract(context, dattended)
    dcontext = through(dattended, out_full).astype(jnp.bfloat16)
    dqueries, dkeys, dvalues = lax.map(
        lambda packed: attend_backward(
            packed[0], packed[1], packed[2], packed[3], packed[4], packed[5]
        ),
        (
            as_blocks(queries),
            as_sequences(keys_all),
            as_sequences(values_all),
            as_blocks(dcontext),
            lse_all,
            my_lengths,
        ),
    )
    dqueries = dqueries.reshape(row_count, D)
    dkeys = dkeys.reshape(row_count, D)
    dvalues = dvalues.reshape(row_count, D)
    grad_query = contract(flat_tokens, dqueries)
    grad_key = contract(flat_tokens, dkeys)
    grad_value = contract(flat_tokens, dvalues)
    grad_query_add = jnp.sum(dqueries.astype(jnp.float32), axis=0)
    grad_value_add = jnp.sum(dvalues.astype(jnp.float32), axis=0)
    input_grad = (
        dsum_one
        + through(dqueries, query_full)
        + through(dkeys, key_full)
        + through(dvalues, value_full)
        + jnp.where(row_live, 0.0, cotan_float)
    ).astype(jnp.bfloat16)
    local_grads = (
        grad_query,
        grad_key,
        grad_value,
        grad_out,
        grad_up,
        grad_down,
        grad_query_add,
        grad_value_add,
        grad_out_add,
        grad_attn_scale,
        grad_attn_add,
        grad_up_add,
        grad_down_add,
        grad_final_scale,
        grad_final_add,
    )
    shares = (
        lax.psum_scatter(
            local_grads[0].astype(jnp.bfloat16), "shard", scatter_dimension=0, tiled=True
        ).astype(jnp.float32),
        lax.psum_scatter(
            local_grads[1].astype(jnp.bfloat16), "shard", scatter_dimension=0, tiled=True
        ).astype(jnp.float32),
        lax.psum_scatter(
            local_grads[2].astype(jnp.bfloat16), "shard", scatter_dimension=0, tiled=True
        ).astype(jnp.float32),
        lax.psum_scatter(
            local_grads[3].astype(jnp.bfloat16), "shard", scatter_dimension=0, tiled=True
        ).astype(jnp.float32),
        lax.psum_scatter(
            local_grads[4].astype(jnp.bfloat16), "shard", scatter_dimension=0, tiled=True
        ).astype(jnp.float32),
        lax.psum_scatter(
            local_grads[5].astype(jnp.bfloat16), "shard", scatter_dimension=0, tiled=True
        ).astype(jnp.float32),
        lax.psum_scatter(
            local_grads[6].astype(jnp.bfloat16), "shard", scatter_dimension=0, tiled=True
        ).astype(jnp.float32),
        lax.psum_scatter(
            local_grads[7].astype(jnp.bfloat16), "shard", scatter_dimension=0, tiled=True
        ).astype(jnp.float32),
        lax.psum_scatter(
            local_grads[8].astype(jnp.bfloat16), "shard", scatter_dimension=0, tiled=True
        ).astype(jnp.float32),
        lax.psum_scatter(
            local_grads[9].astype(jnp.bfloat16), "shard", scatter_dimension=0, tiled=True
        ).astype(jnp.float32),
        lax.psum_scatter(
            local_grads[10].astype(jnp.bfloat16), "shard", scatter_dimension=0, tiled=True
        ).astype(jnp.float32),
        lax.psum_scatter(
            local_grads[11].astype(jnp.bfloat16), "shard", scatter_dimension=0, tiled=True
        ).astype(jnp.float32),
        lax.psum_scatter(
            local_grads[12].astype(jnp.bfloat16), "shard", scatter_dimension=0, tiled=True
        ).astype(jnp.float32),
        lax.psum_scatter(
            local_grads[13].astype(jnp.bfloat16), "shard", scatter_dimension=0, tiled=True
        ).astype(jnp.float32),
        lax.psum_scatter(
            local_grads[14].astype(jnp.bfloat16), "shard", scatter_dimension=0, tiled=True
        ).astype(jnp.float32),
    )
    totals = (
        lax.psum(shares[0].astype(jnp.bfloat16), "rep").astype(jnp.float32),
        lax.psum(shares[1].astype(jnp.bfloat16), "rep").astype(jnp.float32),
        lax.psum(shares[2].astype(jnp.bfloat16), "rep").astype(jnp.float32),
        lax.psum(shares[3].astype(jnp.bfloat16), "rep").astype(jnp.float32),
        lax.psum(shares[4].astype(jnp.bfloat16), "rep").astype(jnp.float32),
        lax.psum(shares[5].astype(jnp.bfloat16), "rep").astype(jnp.float32),
        lax.psum(shares[6].astype(jnp.bfloat16), "rep").astype(jnp.float32),
        lax.psum(shares[7].astype(jnp.bfloat16), "rep").astype(jnp.float32),
        lax.psum(shares[8].astype(jnp.bfloat16), "rep").astype(jnp.float32),
        lax.psum(shares[9].astype(jnp.bfloat16), "rep").astype(jnp.float32),
        lax.psum(shares[10].astype(jnp.bfloat16), "rep").astype(jnp.float32),
        lax.psum(shares[11].astype(jnp.bfloat16), "rep").astype(jnp.float32),
        lax.psum(shares[12].astype(jnp.bfloat16), "rep").astype(jnp.float32),
        lax.psum(shares[13].astype(jnp.bfloat16), "rep").astype(jnp.float32),
        lax.psum(shares[14].astype(jnp.bfloat16), "rep").astype(jnp.float32),
    )
    returning = (output.reshape(per_device, LEN, D), input_grad.reshape(per_device, LEN, D))
    back_pieces = (
        lax.all_to_all(returning[0], "shard", split_axis=1, concat_axis=0, tiled=True),
        lax.all_to_all(returning[1], "shard", split_axis=1, concat_axis=0, tiled=True),
    )
    slot_ids = jnp.arange(group_order.shape[0], dtype=jnp.int32)
    inverse_order = jnp.sum(
        jnp.where(group_order[None, :] == slot_ids[:, None], slot_ids[None, :], 0), axis=1
    )
    restored = (
        jnp.take(back_pieces[0], inverse_order, axis=0),
        jnp.take(back_pieces[1], inverse_order, axis=0),
    )
    final_out, final_grad = (
        lax.all_to_all(restored[0], "shard", split_axis=0, concat_axis=1, tiled=True),
        lax.all_to_all(restored[1], "shard", split_axis=0, concat_axis=1, tiled=True),
    )
    return (
        final_out,
        final_grad,
        totals[0],
        totals[1],
        totals[2],
        totals[3],
        totals[4],
        totals[5],
        totals[6],
        totals[7],
        totals[8],
        totals[9],
        totals[10],
        totals[11],
        totals[12],
        totals[13],
        totals[14],
    )


def solution(mesh):
    placed = (
        P(("rep", "shard"), None, None),
        P(("rep", "shard"), None, None),
        P("rep", None),
        P("rep", None),
        P("rep", None),
        P("shard", None),
        P("shard", None),
        P("shard", None),
        P("shard", None),
        P("shard", None),
        P("shard", None),
        P("shard"),
        P("shard"),
        P("shard"),
        P("shard"),
        P("shard"),
        P("shard"),
        P("shard"),
        P("shard"),
        P("shard"),
    )
    return jax.shard_map(
        body,
        mesh=mesh,
        in_specs=placed,
        out_specs=(
            P(("rep", "shard"), None, None),
            P(("rep", "shard"), None, None),
            P("shard", None),
            P("shard", None),
            P("shard", None),
            P("shard", None),
            P("shard", None),
            P("shard", None),
            P("shard"),
            P("shard"),
            P("shard"),
            P("shard"),
            P("shard"),
            P("shard"),
            P("shard"),
            P("shard"),
            P("shard"),
        ),
        check_vma=False,
    )
```

profile of v0, /device:TPU:0, one launch (start us, length us, event | category | flops | bytes accessed | tf_op | source)
XLA Modules:
  0.0 956.5 jit_solution(16868999127353064278)
XLA Ops:
  43.8 11.6 %reduce.14 = bf16[1024,768]{1,0:T(8,128)(2,1)} reduce(bf16[1024,1,768]{2,1,0:T(2,128)(2,1)S(1)} %bitcast.169, bf16[]{:T(256)} %broadcast.290), dimensions={1}, to_apply=%bitcast.125.reduce_sub_computation | reduce | bytes 3145730
  74.2 15.3 %all-to-all-done.4 = bf16[8,2,49152]{2,1,0:T(2,128)(2,1)} async-done(((bf16[8,2,49152]{2,1,0:T(2,128)(2,1)}), bf16[8,2,49152]{2,1,0:T(2,128)(2,1)}, u32[]{:S(2)}, u32[]{:S(2)}) %all-to-all-start.4) | async-done | bytes 1572896 | tf_op jit(solution)/shard_map/all_to_all | solution.py:143
  101.2 26.8 %all_to_all.90 = bf16[8,128,768]{2,1,0:T(8,128)(2,1)S(1)} all-to-all(bf16[8,128,768]{2,1,0:T(8,128)(2,1)S(1)} %get-tuple-element.401), channel_id=1, replica_groups=mesh['rep'=4,'shard'=8] {'shard'}, dimensions={0} | all-to-all | bytes 3145728 | tf_op jit(solution)/shard_map/all_to_all | solution.py:148
  140.3 36.6 %all-reduce.18 = (bf16[768]{0:T(1024)(128)(2,1)S(1)}, bf16[768]{0:T(1024)(128)(2,1)S(1)}, bf16[768]{0:T(1024)(128)(2,1)S(1)}, bf16[768]{0:T(1024)(128)(2,1)S(1)}...) all-reduce(bf16[768]{0:T(1024)(128)(2,1)S(1)} %dynamic-update-slice, ...), channel_id=1, replica_groups=mesh['rep'=4,'shard'=8] {'shard'}, use_global_device_ids=true, to_apply=%add | all-reduce | flops 5376 | bytes 21504
  213.0 72.1 %while.49 = (s32[]{:T(128)}, bf16[2,512,12,64]{1,3,2,0:T(8,128)(2,1)}, f32[2,12,512,1]{2,1,3,0:T(8,128)S(1)}, bf16[2,512,12,64]{1,3,2,0:T(8,128)(2,1)}, bf16[102...) while((s32[]{:T(128)}, ...), condition=%wide.region_3.5_spmd.clone, body=%wide.region_0.4_spmd.clone.sunk | while | flops 1686498304 | bytes 93040808 | solution.py:65
  213.6 11.8 %fusion.150 = (f32[12,512]{1,0:T(8,128)S(1)}, f32[12,512,1024]{2,1,0:T(8,128)}) fusion(pred[1024]{0:T(1024)(128)(4,1)S(1)} %iota_compare_fusion.6, bf16[1024,12,64]{0,2,1:T(8,128)(2,1)S(1)} %get-tuple-element.544, bf16[2,512,12,64]{1,3,2,0:T(8,128)(2,1)} %get-tuple-element.543, s32[]{:T(128)S(6)} %copy.147), kind=kOutput, calls=%fused_computation.9.clone.1 | convolution fusion | flops 824174592 | bytes 27550724 | tf_op jit(solution)/shard_map/while/body/eval_jaxpr/while/body/eval_jaxpr/qhd,khd->hqk/dot_general | solution.py:47
  249.7 11.7 %fusion.150 = (f32[12,512]{1,0:T(8,128)S(1)}, f32[12,512,1024]{2,1,0:T(8,128)}) fusion(pred[1024]{0:T(1024)(128)(4,1)S(1)} %iota_compare_fusion.6, bf16[1024,12,64]{0,2,1:T(8,128)(2,1)S(1)} %get-tuple-element.544, bf16[2,512,12,64]{1,3,2,0:T(8,128)(2,1)} %get-tuple-element.543, s32[]{:T(128)S(6)} %copy.147), kind=kOutput, calls=%fused_computation.9.clone.1 | convolution fusion | flops 824174592 | bytes 27550724 | tf_op jit(solution)/shard_map/while/body/eval_jaxpr/while/body/eval_jaxpr/qhd,khd->hqk/dot_general | solution.py:47
  299.0 38.9 %fusion.60 = (bf16[1024,3072]{1,0:T(8,128)(2,1)}, f32[1024,3072]{1,0:T(8,128)}) fusion(f32[3072]{0:T(1024)S(1)} %bitcast.193, bf16[768,3072]{1,0:T(8,128)(2,1)} %all-gather.16.cloned.1.call-done, f32[1024,768]{0,1:T(8,128)} %copy-done.8, f32[768]{0:T(1024)S(1)} %copy-done.50, f32[768]{0:T(1024)S(1)} %copy-done.39, f32[1024]{0:T(1024)S(1)} %add_rsqrt_fusion.1, ...), kind=kOutput, calls=%fused_computation.60 | convolution fusion | flops 5043388416 | bytes 26765312 | tf_op jit(solution)/shard_map/dot_general | solution.py:212
  354.0 13.8 %fusion.93 = (bf16[3072]{0:T(1024)(128)(2,1)}, bf16[1024,3072]{1,0:T(8,128)(2,1)S(1)}) fusion(f32[1024,3072]{1,0:T(8,128)} %get-tuple-element.406, f32[3072]{0:T(1024)S(1)} %bitcast.194, bf16[3072,768]{1,0:T(8,128)(2,1)S(1)} %bitcast.199, f32[1024,768]{0,1:T(8,128)S(1)} %get-tuple-element.390), kind=kOutput, calls=%fused_computation.155 | convolution fusion | flops 4870370304 | bytes 26757120 | tf_op jit(solution)/shard_map/dot_general | solution.py:41
  392.3 209.7 %while.50 = (s32[]{:T(128)}, f32[1024,12,64]{0,2,1:T(8,128)}, f32[1024,12,64]{0,2,1:T(8,128)}, bf16[2,512,12,64]{1,3,2,0:T(8,128)(2,1)}, bf16[2,512,12,64]{1,3,2...) while((s32[]{:T(128)}, f32[1024,12,64]{0,2,1:T(8,128)}, ...), condition=%wide.region_15.17_spmd.clone, body=%wide.region_13.16_spmd.clone.sunk | while | flops 4124457984 | bytes 298133664 | solution.py:92
  393.0 13.6 %exponential_select_fusion.2 = f32[12,512,1024]{2,1,0:T(8,128)} fusion(f32[12,512]{1,0:T(8,128)S(1)} %dynamic-slice_bitcast_fusion.2, pred[1024]{0:T(1024)(128)(4,1)S(1)} %iota_compare_fusion.7, bf16[1024,12,64]{0,2,1:T(8,128)(2,1)} %get-tuple-element.577, bf16[2,512,12,64]{1,3,2,0:T(8,128)(2,1)} %get-tuple-element.576, s32[]{:T(128)S(6)} %copy.157), kind=kOutput, calls=%fused_computation.27.clone.1 | convolution fusion | flops 830472192 | bytes 27550724 | tf_op jit(solution)/shard_map/while/body/eval_jaxpr/while/body/eval_jaxpr/qhd,khd->hqk/dot_general | solution.py:47
  406.6 12.4 %bitcast_add_fusion.5 = f32[1024,12,64]{0,2,1:T(8,128)} fusion(f32[1024,12,64]{0,2,1:T(8,128)} %get-tuple-element.562, f32[12,512,1024]{2,1,0:T(8,128)} %exponential_select_fusion.2, pred[]{:T(512)S(6)} %compare.4, bf16[2,512,12,64]{1,3,2,0:T(8,128)(2,1)S(1)} %get-tuple-element.579, s32[]{:T(128)S(6)} %copy.157), kind=kOutput, calls=%fused_computation.32.clone.1 | convolution fusion | flops 813170688 | bytes 32243716 | tf_op jit(solution)/shard_map/while/body/eval_jaxpr/while/body/eval_jaxpr/hqk,qhd->khd/dot_general | solution.py:86
  429.0 33.1 %fusion.164 = bf16[2,512,12,64]{1,3,2,0:T(8,128)(2,1)} fusion(bf16[2,512,12,64]{1,3,2,0:T(8,128)(2,1)} %get-tuple-element.563, s32[]{:T(128)S(6)} %copy.157, bf16[1024,12,64]{0,2,1:T(8,128)(2,1)} %get-tuple-element.577, f32[12,512,1024]{2,1,0:T(8,128)} %exponential_select_fusion.2, f32[12,512,1024]{2,1,0:T(8,128)} %fusion.163), kind=kOutput, calls=%fused_computation.36.clone.1 | convolution fusion | flops 837164032 | bytes 103022592 | tf_op jit(solution)/shard_map/while/body/eval_jaxpr/while/body/eval_jaxpr/hqk,khd->qhd/dot_general | solution.py:80
  462.1 34.4 %bitcast_add_fusion.4 = f32[1024,12,64]{0,2,1:T(8,128)} fusion(f32[1024,12,64]{0,2,1:T(8,128)} %get-tuple-element.561, f32[12,512,1024]{2,1,0:T(8,128)} %exponential_select_fusion.2, f32[12,512,1024]{2,1,0:T(8,128)} %fusion.163, pred[]{:T(512)S(6)} %compare.4, bf16[2,512,12,64]{1,3,2,0:T(8,128)(2,1)} %get-tuple-element.576, s32[]{:T(128)S(6)} %copy.157), kind=kOutput, calls=%fused_computation.33.clone.1 | convolution fusion | flops 838343680 | bytes 107741192 | tf_op jit(solution)/shard_map/while/body/eval_jaxpr/while/body/eval_jaxpr/hqk,qhd->khd/dot_general | solution.py:83
  497.1 13.3 %exponential_select_fusion.2 = f32[12,512,1024]{2,1,0:T(8,128)} fusion(f32[12,512]{1,0:T(8,128)S(1)} %dynamic-slice_bitcast_fusion.2, pred[1024]{0:T(1024)(128)(4,1)S(1)} %iota_compare_fusion.7, bf16[1024,12,64]{0,2,1:T(8,128)(2,1)} %get-tuple-element.577, bf16[2,512,12,64]{1,3,2,0:T(8,128)(2,1)} %get-tuple-element.576, s32[]{:T(128)S(6)} %copy.157), kind=kOutput, calls=%fused_computation.27.clone.1 | convolution fusion | flops 830472192 | bytes 27550724 | tf_op jit(solution)/shard_map/while/body/eval_jaxpr/while/body/eval_jaxpr/qhd,khd->hqk/dot_general | solution.py:47
  510.5 13.1 %bitcast_add_fusion.5 = f32[1024,12,64]{0,2,1:T(8,128)} fusion(f32[1024,12,64]{0,2,1:T(8,128)} %get-tuple-element.562, f32[12,512,1024]{2,1,0:T(8,128)} %exponential_select_fusion.2, pred[]{:T(512)S(6)} %compare.4, bf16[2,512,12,64]{1,3,2,0:T(8,128)(2,1)S(1)} %get-tuple-element.579, s32[]{:T(128)S(6)} %copy.157), kind=kOutput, calls=%fused_computation.32.clone.1 | convolution fusion | flops 813170688 | bytes 32243716 | tf_op jit(solution)/shard_map/while/body/eval_jaxpr/while/body/eval_jaxpr/hqk,qhd->khd/dot_general | solution.py:86
  533.6 33.1 %fusion.164 = bf16[2,512,12,64]{1,3,2,0:T(8,128)(2,1)} fusion(bf16[2,512,12,64]{1,3,2,0:T(8,128)(2,1)} %get-tuple-element.563, s32[]{:T(128)S(6)} %copy.157, bf16[1024,12,64]{0,2,1:T(8,128)(2,1)} %get-tuple-element.577, f32[12,512,1024]{2,1,0:T(8,128)} %exponential_select_fusion.2, f32[12,512,1024]{2,1,0:T(8,128)} %fusion.163), kind=kOutput, calls=%fused_computation.36.clone.1 | convolution fusion | flops 837164032 | bytes 103022592 | tf_op jit(solution)/shard_map/while/body/eval_jaxpr/while/body/eval_jaxpr/hqk,khd->qhd/dot_general | solution.py:80
  566.7 35.1 %bitcast_add_fusion.4 = f32[1024,12,64]{0,2,1:T(8,128)} fusion(f32[1024,12,64]{0,2,1:T(8,128)} %get-tuple-element.561, f32[12,512,1024]{2,1,0:T(8,128)} %exponential_select_fusion.2, f32[12,512,1024]{2,1,0:T(8,128)} %fusion.163, pred[]{:T(512)S(6)} %compare.4, bf16[2,512,12,64]{1,3,2,0:T(8,128)(2,1)} %get-tuple-element.576, s32[]{:T(128)S(6)} %copy.157), kind=kOutput, calls=%fused_computation.33.clone.1 | convolution fusion | flops 838343680 | bytes 107741192 | tf_op jit(solution)/shard_map/while/body/eval_jaxpr/while/body/eval_jaxpr/hqk,qhd->khd/dot_general | solution.py:83
  645.7 24.0 %all-reduce.17 = (bf16[768]{0:T(1024)(128)(2,1)S(1)}, bf16[768]{0:T(1024)(128)(2,1)S(1)}, bf16[768]{0:T(1024)(128)(2,1)S(1)}, bf16[768]{0:T(1024)(128)(2,1)S(1)}...) all-reduce(bf16[768]{0:T(1024)(128)(2,1)S(1)} %dynamic-update-slice, ...), channel_id=1, replica_groups=mesh['rep'=4,'shard'=8] {'shard'}, use_global_device_ids=true, to_apply=%add.7 | all-reduce | flops 9984 | bytes 39936
  741.2 14.8 %all-to-all-done.6 = bf16[8,2,49152]{2,1,0:T(2,128)(2,1)} async-done(((bf16[8,2,49152]{2,1,0:T(2,128)(2,1)}), bf16[8,2,49152]{2,1,0:T(2,128)(2,1)}, u32[]{:S(2)}, u32[]{:S(2)}) %all-to-all-start.6) | async-done | bytes 1572896 | tf_op jit(solution)/shard_map/all_to_all | solution.py:379
  772.0 28.4 %reduce-scatter.17.cloned.1.call-done = bf16[384,768]{1,0:T(8,128)(2,1)} async-done(((bf16[3072,768]{1,0:T(8,128)(2,1)}), bf16[384,768]{1,0:T(8,128)(2,1)}) %reduce-scatter.17.cloned.1.call-update) | async-done | bytes 589840 | tf_op jit(solution)/shard_map/reduce_scatter | solution.py:328
  800.4 58.1 %reduce-scatter.15.cloned.1.call-done = bf16[96,3072]{1,0:T(8,128)(2,1)} async-done(((bf16[768,3072]{1,0:T(8,128)(2,1)}), bf16[96,3072]{1,0:T(8,128)(2,1)}) %reduce-scatter.15.cloned.1.call-update) | async-done | bytes 589840 | tf_op jit(solution)/shard_map/reduce_scatter | solution.py:325
  864.2 12.6 %all-reduce.19 = (bf16[96]{0:T(256)(128)(2,1)S(1)}, bf16[96]{0:T(256)(128)(2,1)S(1)}, bf16[96]{0:T(256)(128)(2,1)S(1)}, bf16[96]{0:T(256)(128)(2,1)S(1)}, bf16[9...) all-reduce(bf16[96]{0:T(256)(128)(2,1)S(1)} %dynamic-slice.16, ...), channel_id=1, replica_groups=mesh['rep'=4,'shard'=8] {'rep'}, use_global_device_ids=true, to_apply=%region_30.32 | all-reduce | flops 1152 | bytes 4608 | tf_op jit(solution)/shard_map/psum | solution.py:366
  883.1 54.5 %all-reduce.23.cloned.1.call-done = (bf16[96,768]{1,0:T(8,128)(2,1)}, bf16[96,768]{1,0:T(8,128)(2,1)}, bf16[96,768]{1,0:T(8,128)(2,1)}, bf16[96,768]{1,0:T(8,128...) async-done(((bf16[96,768]{1,0:T(8,128)(2,1)}, bf16[96,768]{1,0:T(8,128)(2,1)}, bf16[96,768]{1,0:T(8,128)(2,1)}, bf16[96,768]{1,0:T(8,128)(2,1)}, ...) | async-done | bytes 1769488 | tf_op jit(solution)/shard_map/psum | solution.py:360
  (384 shorter events, 390.1 us)
Async XLA Ops:
  7.2 189.5 %all-gather.8.cloned.1.call-start = ((), (), s32[]{:S(2)}) async-start(), calls=%async_computation.14 | async-start | bytes 1327104 | tf_op jit(solution)/shard_map/all_gather | solution.py:161
  9.0 196.5 %all-gather.10.cloned.1.call-start = ((), (), s32[]{:S(2)}) async-start(), calls=%async_computation.15 | async-start | bytes 1327104 | tf_op jit(solution)/shard_map/all_gather | solution.py:161
  10.7 197.8 %all-gather.12.cloned.1.call-start = ((), (), s32[]{:S(2)}) async-start(), calls=%async_computation.16 | async-start | bytes 1327104 | tf_op jit(solution)/shard_map/all_gather | solution.py:161
  12.4 281.0 %all-gather.14.cloned.1.call-start = ((), (), s32[]{:S(2)}) async-start(), calls=%async_computation.17 | async-start | bytes 1327104 | tf_op jit(solution)/shard_map/all_gather | solution.py:161
  14.1 284.8 %all-gather.16.cloned.1.call-start = ((), (), s32[]{:S(2)}) async-start(), calls=%async_computation.18 | async-start | bytes 5308416 | tf_op jit(solution)/shard_map/all_gather | solution.py:161
  34.7 27.9 %all-to-all-start = ((bf16[8,2,49152]{2,1,0:T(2,128)(2,1)}), bf16[8,2,49152]{2,1,0:T(2,128)(2,1)}, u32[]{:S(2)}, u32[]{:S(2)}) async-start(bf16[8,2,49152]{2,1,0:T(2,128)(2,1)} %reshape.367), calls=%async_computation | async-start | bytes 3145728 | tf_op jit(solution)/shard_map/all_to_all | solution.py:142
  62.6 26.9 %all-to-all-start.4 = ((bf16[8,2,49152]{2,1,0:T(2,128)(2,1)}), bf16[8,2,49152]{2,1,0:T(2,128)(2,1)}, u32[]{:S(2)}, u32[]{:S(2)}) async-start(bf16[8,2,49152]{2,1,0:T(2,128)(2,1)} %reshape.371), calls=%async_computation.4 | async-start | bytes 3145728 | tf_op jit(solution)/shard_map/all_to_all | solution.py:143
  128.0 66.0 %copy-start.5 = (bf16[8,128,768]{2,1,0:T(8,128)(2,1)}, bf16[8,128,768]{2,1,0:T(8,128)(2,1)S(1)}, u32[]{:S(2)}) copy-start(bf16[8,128,768]{2,1,0:T(8,128)(2,1)S(1)} %all_to_all.90) | copy-start | bytes 4718596
  128.1 60.8 %copy-start.61 = (s32[1,8]{1,0:T(1,128)S(1)}, s32[1,8]{1,0:T(1,128)}, u32[]{:S(2)}) copy-start(s32[1,8]{1,0:T(1,128)} %param.28) | copy-start | bytes 100
  128.1 66.5 %all-to-all-start.1 = ((bf16[8,128,768]{2,1,0:T(8,128)(2,1)}), bf16[8,128,768]{2,1,0:T(8,128)(2,1)S(1)}, u32[]{:S(2)}, u32[]{:S(2)}) async-start(bf16[8,128,768]{2,1,0:T(8,128)(2,1)} %get-tuple-element.402), calls=%async_computation.1 | async-start | bytes 3145728 | tf_op jit(solution)/shard_map/all_to_all | solution.py:147
  131.9 206.1 %all-gather.18.cloned.1.call-start = ((), (), s32[]{:S(2)}) async-start(), calls=%async_computation.19 | async-start | bytes 5308416 | tf_op jit(solution)/shard_map/all_gather | solution.py:161
  134.1 637.9 %reduce-scatter.13.cloned.1.call-start = ((), (), s32[]{:S(2)}) async-start(), calls=%async_computation.23 | async-start | bytes 1327104 | tf_op jit(solution)/shard_map/reduce_scatter | solution.py:322
  296.9 77.6 %copy-start.35 = (f32[1024]{0:T(1024)}, f32[1024]{0:T(1024)S(1)}, u32[]{:S(2)}) copy-start(f32[1024]{0:T(1024)S(1)} %broadcast_multiply_fusion.4) | copy-start | bytes 12292
  298.9 75.6 %copy-start.41 = (f32[1024]{0:T(1024)}, f32[1024]{0:T(1024)S(1)}, u32[]{:S(2)}) copy-start(f32[1024]{0:T(1024)S(1)} %add_rsqrt_fusion.1) | copy-start | bytes 12292
  380.5 391.5 %reduce-scatter.7.cloned.1.call-start = ((), (), s32[]{:S(2)}) async-start(), calls=%async_computation.20 | async-start | bytes 1327104 | tf_op jit(solution)/shard_map/reduce_scatter | solution.py:313
  609.2 162.7 %reduce-scatter.9.cloned.1.call-start = ((), (), s32[]{:S(2)}) async-start(), calls=%async_computation.21 | async-start | bytes 1327104 | tf_op jit(solution)/shard_map/reduce_scatter | solution.py:316
  615.2 156.8 %reduce-scatter.11.cloned.1.call-start = ((), (), s32[]{:S(2)}) async-start(), calls=%async_computation.22 | async-start | bytes 1327104 | tf_op jit(solution)/shard_map/reduce_scatter | solution.py:319
  621.1 179.3 %reduce-scatter.17.cloned.1.call-start = ((), (), s32[]{:S(2)}) async-start(), calls=%async_computation.25 | async-start | bytes 5308416 | tf_op jit(solution)/shard_map/reduce_scatter | solution.py:328
  631.0 227.5 %reduce-scatter.15.cloned.1.call-start = ((), (), s32[]{:S(2)}) async-start(), calls=%async_computation.24 | async-start | bytes 5308416 | tf_op jit(solution)/shard_map/reduce_scatter | solution.py:325
  695.4 35.3 %all-to-all-start.2 = ((bf16[8,2,49152]{2,1,0:T(2,128)(2,1)}), bf16[8,2,49152]{2,1,0:T(2,128)(2,1)}, u32[]{:S(2)}, u32[]{:S(2)}) async-start(bf16[8,2,49152]{2,1,0:T(2,128)(2,1)} %reshape.369), calls=%async_computation.2 | async-start | bytes 3145728 | tf_op jit(solution)/shard_map/all_to_all | solution.py:378
  730.7 25.3 %all-to-all-start.6 = ((bf16[8,2,49152]{2,1,0:T(2,128)(2,1)}), bf16[8,2,49152]{2,1,0:T(2,128)(2,1)}, u32[]{:S(2)}, u32[]{:S(2)}) async-start(bf16[8,2,49152]{2,1,0:T(2,128)(2,1)} %reshape.373), calls=%async_computation.6 | async-start | bytes 3145728 | tf_op jit(solution)/shard_map/all_to_all | solution.py:379
  768.3 90.3 %all-to-all-start.7 = ((bf16[8,128,768]{2,1,0:T(8,128)(2,1)}), bf16[8,128,768]{2,1,0:T(8,128)(2,1)S(1)}, u32[]{:S(2)}, u32[]{:S(2)}) async-start(bf16[8,128,768]{2,1,0:T(8,128)(2,1)} %get-tuple-element.399), calls=%async_computation.7 | async-start | bytes 3145728 | tf_op jit(solution)/shard_map/all_to_all | solution.py:391
  771.9 165.8 %all-reduce.23.cloned.1.call-start = ((), (), s32[]{:S(2)}) async-start(), calls=%async_computation.26 | async-start | bytes 3538944 | tf_op jit(solution)/shard_map/psum | solution.py:360
  858.6 24.5 %all-to-all-start.3 = ((bf16[8,128,768]{2,1,0:T(8,128)(2,1)}), bf16[8,128,768]{2,1,0:T(8,128)(2,1)S(1)}, u32[]{:S(2)}, u32[]{:S(2)}) async-start(bf16[8,128,768]{2,1,0:T(8,128)(2,1)} %get-tuple-element.400), calls=%async_computation.3 | async-start | bytes 3145728 | tf_op jit(solution)/shard_map/all_to_all | solution.py:390
  (77 other events, 545.5 us)
Sparse Core Ops, SparseCore 0:
  10.5 26.6 all-gather.7
  39.6 28.1 all-gather.9
  70.3 28.6 all-gather.11
  101.3 28.6 all-gather.13
  132.3 49.3 all-gather.15
  184.0 38.7 all-gather.17
  380.6 38.5 reduce-scatter.12
  609.4 38.4 reduce-scatter.6
  651.6 36.6 reduce-scatter.8
  691.4 43.6 reduce-scatter.10
  738.6 61.7 reduce-scatter.16
  803.7 54.7 reduce-scatter.14
  861.4 76.1 all-reduce.22
where the time goes:
time: 968 us; the launch traced here: 957 us
  matrix products  374 us (39%)
  waiting for transfers between devices  177 us (18%)
  other arithmetic  125 us (13%)
  local copies, waits for them, and re-layouts  122 us (13%)
  blocking collectives  109 us (11%)
  starting transfers between devices  29.7 us (3%)
  between operations  19.3 us (2%)
    unnamed x202, local copies, waits for them, and re-layouts  72.9 us
    dot_general x2, matrix products, per_block(): jnp.einsum('hqk,qhd->khd', dscores, query_blk, preferred_element_type=jnp...  69.5 us
    dot_general x2, matrix products, per_block(): jnp.einsum('hqk,khd->qhd', dscores, keys_seq, preferred_element_type=jnp....  66.1 us
    unnamed x2, blocking collectives  60.6 us
    reduce_scatter x1, waiting for transfers between devices, body(): lax.psum_scatter(local_grads[4].astype(jnp.bfloat16), 'shard', scatter_di...  58.1 us
    psum x1, waiting for transfers between devices, body(): lax.psum(shares[0].astype(jnp.bfloat16), 'rep').astype(jnp.float32)  54.5 us
    dot_general x4, matrix products, score_block(): jnp.einsum('qhd,khd->hqk', query_blk, keys_seq, preferred_element_type=jn...  50.4 us
    unnamed x8, other arithmetic  46 us
  transfers between devices with their start and end apart: 20, of which 7 were waited for; matrix products, arithmetic and copies ran while one was open for 58% of the time, Pallas kernels for 0%

commit v1 on v0

--- a/solution.py
+++ b/solution.py
@@ -138,19 +138,13 @@
     row_count = per_device * LEN
     block_rows = min(512, LEN)
     group_order = dealing[0]
-    pieces = (
-        lax.all_to_all(tokens, "shard", split_axis=1, concat_axis=0, tiled=True),
-        lax.all_to_all(cotangent, "shard", split_axis=1, concat_axis=0, tiled=True),
-    )
-    placed = (jnp.take(pieces[0], group_order, axis=0), jnp.take(pieces[1], group_order, axis=0))
-    local_tokens, local_cotan = (
-        lax.all_to_all(placed[0], "shard", split_axis=0, concat_axis=1, tiled=True),
-        lax.all_to_all(placed[1], "shard", split_axis=0, concat_axis=1, tiled=True),
-    )
+    local_tokens, local_cotan = tokens, cotangent
     first_slot = lax.axis_index("shard") * per_device
-    my_order = lax.dynamic_slice_in_dim(group_order, first_slot, per_device)
-    my_lengths = jnp.take(lengths[0], my_order)
-    my_flags = lax.dynamic_slice_in_dim(drop_flags[0], first_slot, per_device)
+    mine = first_slot + jnp.arange(per_device)
+    my_lengths = lax.dynamic_slice_in_dim(lengths[0], first_slot, per_device)
+    my_flags = jnp.sum(
+        jnp.where(group_order[None, :] == mine[:, None], drop_flags[0][None, :], 0), axis=1
+    )
     positions = jnp.arange(LEN)
     row_live = ((positions[None, :] < my_lengths[:, None]) & (my_flags[:, None] == 0)).reshape(
         row_count, 1
@@ -219,28 +213,6 @@
     normed_two, inverse_two = layer_stats(first + branch)
     final = normed_two * final_scale.astype(jnp.float32) + final_add.astype(jnp.float32)
     output = jnp.where(row_live, final, token_float).astype(jnp.bfloat16)
-    weights_back = jax.tree.map(
-        lambda part, own: part.astype(own.dtype),
-        lax.all_gather(for_sending(lowered), "shard", axis=0, tiled=True),
-        lowered,
-    )
-    (
-        query_full,
-        key_full,
-        value_full,
-        out_full,
-        up_full,
-        down_full,
-        query_add,
-        value_add,
-        out_add,
-        attn_scale,
-        attn_add,
-        up_add,
-        down_add,
-        final_scale,
-        final_add,
-    ) = weights_back
     cotan_float = local_cotan.reshape(row_count, D).astype(jnp.float32)
     upstream = jnp.where(row_live, cotan_float, 0.0)
     grad_final_scale = jnp.sum(upstream * normed_two, axis=0)
@@ -373,23 +345,8 @@
         lax.psum(shares[13].astype(jnp.bfloat16), "rep").astype(jnp.float32),
         lax.psum(shares[14].astype(jnp.bfloat16), "rep").astype(jnp.float32),
     )
-    returning = (output.reshape(per_device, LEN, D), input_grad.reshape(per_device, LEN, D))
-    back_pieces = (
-        lax.all_to_all(returning[0], "shard", split_axis=1, concat_axis=0, tiled=True),
-        lax.all_to_all(returning[1], "shard", split_axis=1, concat_axis=0, tiled=True),
-    )
-    slot_ids = jnp.arange(group_order.shape[0], dtype=jnp.int32)
-    inverse_order = jnp.sum(
-        jnp.where(group_order[None, :] == slot_ids[:, None], slot_ids[None, :], 0), axis=1
-    )
-    restored = (
-        jnp.take(back_pieces[0], inverse_order, axis=0),
-        jnp.take(back_pieces[1], inverse_order, axis=0),
-    )
-    final_out, final_grad = (
-        lax.all_to_all(restored[0], "shard", split_axis=0, concat_axis=1, tiled=True),
-        lax.all_to_all(restored[1], "shard", split_axis=0, concat_axis=1, tiled=True),
-    )
+    final_out = output.reshape(per_device, LEN, D)
+    final_grad = input_grad.reshape(per_device, LEN, D)
     return (
         final_out,
         final_grad,

time: 968 us -> 876 us (0.905)
  waiting for transfers between devices: 177 us -> 265 us
  other arithmetic: 125 us -> 63.1 us
  local copies, waits for them, and re-layouts: 122 us -> 66.6 us
  blocking collectives: 109 us -> 70.1 us
  starting transfers between devices: 29.7 us -> 0.54 us
    unnamed x13 -> x16, waiting for transfers between devices: 0.21 us -> 73.1 us
    unnamed x8 -> x4, other arithmetic: 46 us -> 0.01 us
    reduce_scatter x1, waiting for transfers between devices: 0.02 us -> 38 us  [body(): lax.psum_scatter(local_grads[3].astype(jnp.bfloat16), 'shard', scatter_di...]
    all_to_all x7 -> x0, waiting for transfers between devices: 35.2 us -> none  [the longest x1 15.3 us: body(): lax.all_to_all(cotangent, 'shard', split_axis=1, concat_axis=0, tiled=True)]
    psum x1, waiting for transfers between devices: 54.5 us -> 25.3 us  [body(): lax.psum(shares[0].astype(jnp.bfloat16), 'rep').astype(jnp.float32)]
    all_to_all x7 -> x0, starting transfers between devices: 29.2 us -> none  [the longest x1 5.21 us: body(): lax.all_to_all(tokens, 'shard', split_axis=1, concat_axis=0, tiled=True)]
    reduce_scatter x1, waiting for transfers between devices: 28.4 us -> 57.3 us  [body(): lax.psum_scatter(local_grads[5].astype(jnp.bfloat16), 'shard', scatter_di...]
    all_to_all x1 -> x0, blocking collectives: 26.8 us -> none  [body(): lax.all_to_all(placed[1], 'shard', split_axis=0, concat_axis=1, tiled=True)]
  transfers between devices with their start and end apart: 20 -> 13, of which waited for: 7 -> 7; matrix products, arithmetic and copies ran while one was open for 58% -> 25% of each run, Pallas kernels for 0% -> 0%
where the time goes in v1:
time: 876 us; the launch traced here: 864 us
  matrix products  380 us (43%)
  waiting for transfers between devices  265 us (30%)
  blocking collectives  70.1 us (8%)
  local copies, waits for them, and re-layouts  66.6 us (8%)
  other arithmetic  63.1 us (7%)
  between operations  18 us (2%)
    unnamed x16, waiting for transfers between devices  73.1 us
    dot_general x2, matrix products, per_block(): jnp.einsum('hqk,qhd->khd', dscores, query_blk, preferred_element_type=jnp...  69.5 us
    dot_general x2, matrix products, per_block(): jnp.einsum('hqk,khd->qhd', dscores, keys_seq, preferred_element_type=jnp....  66.2 us
    reduce_scatter x1, waiting for transfers between devices, body(): lax.psum_scatter(local_grads[5].astype(jnp.bfloat16), 'shard', scatter_di...  57.3 us
    reduce_scatter x1, waiting for transfers between devices, body(): lax.psum_scatter(local_grads[4].astype(jnp.bfloat16), 'shard', scatter_di...  57.1 us
    dot_general x4, matrix products, score_block(): jnp.einsum('qhd,khd->hqk', query_blk, keys_seq, preferred_element_type=jn...  50.5 us
    unnamed x2, blocking collectives  50.3 us
    unnamed x194, local copies, waits for them, and re-layouts  47.3 us
  transfers between devices with their start and end apart: 13, of which 7 were waited for; matrix products, arithmetic and copies ran while one was open for 25% of the time, Pallas kernels for 0%

profile of v1, /device:TPU:0, one launch (start us, length us, event | category | flops | bytes accessed | tf_op | source)
XLA Modules:
  0.0 864.2 jit_solution(17336670399727990471)
XLA Ops:
  22.0 25.8 %all-reduce.18 = (bf16[768]{0:T(1024)(128)(2,1)S(1)}, bf16[768]{0:T(1024)(128)(2,1)S(1)}, bf16[768]{0:T(1024)(128)(2,1)S(1)}, bf16[768]{0:T(1024)(128)(2,1)S(1)}...) all-reduce(bf16[768]{0:T(1024)(128)(2,1)S(1)} %dynamic-update-slice, ...), channel_id=1, replica_groups=mesh['rep'=4,'shard'=8] {'shard'}, use_global_device_ids=true, to_apply=%add | all-reduce | flops 5376 | bytes 21504
  75.7 14.4 %all-gather.12.cloned.1.call-done = bf16[768,768]{1,0:T(8,128)(2,1)} async-done(((bf16[96,768]{1,0:T(8,128)(2,1)}), bf16[768,768]{1,0:T(8,128)(2,1)}) %all-gather.12.cloned.1.call-update) | async-done | bytes 1179664 | tf_op jit(solution)/shard_map/all_gather | solution.py:155
  94.6 73.8 %while.48 = (s32[]{:T(128)}, bf16[2,512,12,64]{1,3,2,0:T(8,128)(2,1)}, f32[2,12,512,1]{2,1,3,0:T(8,128)S(1)}, bf16[2,512,12,64]{1,3,2,0:T(8,128)(2,1)}, bf16[102...) while((s32[]{:T(128)}, ...), condition=%wide.region_4.5_spmd.clone, body=%wide.region_1.4_spmd.clone.sunk | while | flops 1686498304 | bytes 93040808 | solution.py:65
  118.5 11.8 %fusion.186 = bf16[2,512,12,64]{1,3,2,0:T(8,128)(2,1)S(1)} fusion(bf16[2,512,12,64]{1,3,2,0:T(8,128)(2,1)S(1)} %copy-done.16, s32[]{:T(128)S(6)} %copy.116, bf16[1024,12,64]{0,2,1:T(8,128)(2,1)S(1)} %get-tuple-element.544, f32[12,512,1024]{2,1,0:T(8,128)} %get-tuple-element.511, f32[12,512]{1,0:T(8,128)S(1)} %fusion.185, ...), kind=kOutput, calls=%fused_computation.10.clone.1 | convolution fusion | flops 837156864 | bytes 27591684 | tf_op jit(solution)/shard_map/while/body/eval_jaxpr/while/body/eval_jaxpr/hqk,khd->qhd/dot_general | solution.py:62
  132.1 12.1 %fusion.184 = (f32[12,512]{1,0:T(8,128)S(1)}, f32[12,512,1024]{2,1,0:T(8,128)}) fusion(pred[1024]{0:T(1024)(128)(4,1)S(1)} %iota_compare_fusion.5, bf16[1024,12,64]{0,2,1:T(8,128)(2,1)S(1)} %get-tuple-element.543, bf16[2,512,12,64]{1,3,2,0:T(8,128)(2,1)} %get-tuple-element.542, s32[]{:T(128)S(6)} %copy.116), kind=kOutput, calls=%fused_computation.5.clone.1 | convolution fusion | flops 824174592 | bytes 27550724 | tf_op jit(solution)/shard_map/while/body/eval_jaxpr/while/body/eval_jaxpr/qhd,khd->hqk/dot_general | solution.py:47
  179.7 38.5 %fusion.60 = (bf16[1024,3072]{1,0:T(8,128)(2,1)}, f32[1024,3072]{1,0:T(8,128)}) fusion(f32[3072]{0:T(1024)S(1)} %bitcast.193, bf16[768,3072]{1,0:T(8,128)(2,1)} %all-gather.16.cloned.1.call-done, f32[1024,768]{0,1:T(8,128)} %copy-done.8, f32[768]{0:T(1024)S(1)} %copy-done.53, f32[768]{0:T(1024)S(1)} %copy-done.43, f32[1024]{0:T(1024)S(1)} %add_rsqrt_fusion.1, ...), kind=kOutput, calls=%fused_computation.56 | convolution fusion | flops 5043388416 | bytes 26765312 | tf_op jit(solution)/shard_map/dot_general | solution.py:206
  234.3 14.7 %fusion.131 = (bf16[3072]{0:T(1024)(128)(2,1)}, bf16[1024,3072]{1,0:T(8,128)(2,1)}) fusion(f32[1024,3072]{1,0:T(8,128)} %get-tuple-element.407, f32[3072]{0:T(1024)S(1)} %bitcast.194, bf16[1024,768]{0,1:T(8,128)(2,1)S(1)} %get-tuple-element.395, bf16[3072,768]{1,0:T(8,128)(2,1)S(1)} %bitcast.198), kind=kOutput, calls=%fused_computation.154 | convolution fusion | flops 4869583872 | bytes 25184256 | tf_op jit(solution)/shard_map/dot_general | solution.py:41
  271.9 209.6 %while.49 = (s32[]{:T(128)}, f32[1024,12,64]{0,2,1:T(8,128)}, f32[1024,12,64]{0,2,1:T(8,128)}, bf16[2,512,12,64]{1,3,2,0:T(8,128)(2,1)}, bf16[2,512,12,64]{1,3,2...) while((s32[]{:T(128)}, f32[1024,12,64]{0,2,1:T(8,128)}, ...), condition=%wide.region_15.16_spmd.clone, body=%wide.region_13.15_spmd.clone.sunk | while | flops 4124457984 | bytes 298133664 | solution.py:92
  272.6 13.4 %exponential_select_fusion.2 = f32[12,512,1024]{2,1,0:T(8,128)} fusion(f32[12,512]{1,0:T(8,128)S(1)} %dynamic-slice_bitcast_fusion.2, pred[1024]{0:T(1024)(128)(4,1)S(1)} %iota_compare_fusion.6, bf16[1024,12,64]{0,2,1:T(8,128)(2,1)} %get-tuple-element.576, bf16[2,512,12,64]{1,3,2,0:T(8,128)(2,1)} %get-tuple-element.575, s32[]{:T(128)S(6)} %copy.127), kind=kOutput, calls=%fused_computation.23.clone.1 | convolution fusion | flops 830472192 | bytes 27550724 | tf_op jit(solution)/shard_map/while/body/eval_jaxpr/while/body/eval_jaxpr/qhd,khd->hqk/dot_general | solution.py:47
  286.0 12.2 %bitcast_add_fusion.5 = f32[1024,12,64]{0,2,1:T(8,128)} fusion(f32[1024,12,64]{0,2,1:T(8,128)} %get-tuple-element.561, f32[12,512,1024]{2,1,0:T(8,128)} %exponential_select_fusion.2, pred[]{:T(512)S(6)} %compare.3, bf16[2,512,12,64]{1,3,2,0:T(8,128)(2,1)S(1)} %get-tuple-element.578, s32[]{:T(128)S(6)} %copy.127), kind=kOutput, calls=%fused_computation.28.clone.1 | convolution fusion | flops 813170688 | bytes 32243716 | tf_op jit(solution)/shard_map/while/body/eval_jaxpr/while/body/eval_jaxpr/hqk,qhd->khd/dot_general | solution.py:86
  308.3 33.1 %fusion.198 = bf16[2,512,12,64]{1,3,2,0:T(8,128)(2,1)} fusion(bf16[2,512,12,64]{1,3,2,0:T(8,128)(2,1)} %get-tuple-element.562, s32[]{:T(128)S(6)} %copy.127, bf16[1024,12,64]{0,2,1:T(8,128)(2,1)} %get-tuple-element.576, f32[12,512,1024]{2,1,0:T(8,128)} %exponential_select_fusion.2, f32[12,512,1024]{2,1,0:T(8,128)} %fusion.197), kind=kOutput, calls=%fused_computation.32.clone.1 | convolution fusion | flops 837164032 | bytes 103022592 | tf_op jit(solution)/shard_map/while/body/eval_jaxpr/while/body/eval_jaxpr/hqk,khd->qhd/dot_general | solution.py:80
  341.3 34.3 %bitcast_add_fusion.4 = f32[1024,12,64]{0,2,1:T(8,128)} fusion(f32[1024,12,64]{0,2,1:T(8,128)} %get-tuple-element.560, f32[12,512,1024]{2,1,0:T(8,128)} %exponential_select_fusion.2, f32[12,512,1024]{2,1,0:T(8,128)} %fusion.197, pred[]{:T(512)S(6)} %compare.3, bf16[2,512,12,64]{1,3,2,0:T(8,128)(2,1)} %get-tuple-element.575, s32[]{:T(128)S(6)} %copy.127), kind=kOutput, calls=%fused_computation.29.clone.1 | convolution fusion | flops 838343680 | bytes 107741192 | tf_op jit(solution)/shard_map/while/body/eval_jaxpr/while/body/eval_jaxpr/hqk,qhd->khd/dot_general | solution.py:83
  376.3 13.4 %exponential_select_fusion.2 = f32[12,512,1024]{2,1,0:T(8,128)} fusion(f32[12,512]{1,0:T(8,128)S(1)} %dynamic-slice_bitcast_fusion.2, pred[1024]{0:T(1024)(128)(4,1)S(1)} %iota_compare_fusion.6, bf16[1024,12,64]{0,2,1:T(8,128)(2,1)} %get-tuple-element.576, bf16[2,512,12,64]{1,3,2,0:T(8,128)(2,1)} %get-tuple-element.575, s32[]{:T(128)S(6)} %copy.127), kind=kOutput, calls=%fused_computation.23.clone.1 | convolution fusion | flops 830472192 | bytes 27550724 | tf_op jit(solution)/shard_map/while/body/eval_jaxpr/while/body/eval_jaxpr/qhd,khd->hqk/dot_general | solution.py:47
  389.6 13.1 %bitcast_add_fusion.5 = f32[1024,12,64]{0,2,1:T(8,128)} fusion(f32[1024,12,64]{0,2,1:T(8,128)} %get-tuple-element.561, f32[12,512,1024]{2,1,0:T(8,128)} %exponential_select_fusion.2, pred[]{:T(512)S(6)} %compare.3, bf16[2,512,12,64]{1,3,2,0:T(8,128)(2,1)S(1)} %get-tuple-element.578, s32[]{:T(128)S(6)} %copy.127), kind=kOutput, calls=%fused_computation.28.clone.1 | convolution fusion | flops 813170688 | bytes 32243716 | tf_op jit(solution)/shard_map/while/body/eval_jaxpr/while/body/eval_jaxpr/hqk,qhd->khd/dot_general | solution.py:86
  412.8 33.1 %fusion.198 = bf16[2,512,12,64]{1,3,2,0:T(8,128)(2,1)} fusion(bf16[2,512,12,64]{1,3,2,0:T(8,128)(2,1)} %get-tuple-element.562, s32[]{:T(128)S(6)} %copy.127, bf16[1024,12,64]{0,2,1:T(8,128)(2,1)} %get-tuple-element.576, f32[12,512,1024]{2,1,0:T(8,128)} %exponential_select_fusion.2, f32[12,512,1024]{2,1,0:T(8,128)} %fusion.197), kind=kOutput, calls=%fused_computation.32.clone.1 | convolution fusion | flops 837164032 | bytes 103022592 | tf_op jit(solution)/shard_map/while/body/eval_jaxpr/while/body/eval_jaxpr/hqk,khd->qhd/dot_general | solution.py:80
  445.9 35.3 %bitcast_add_fusion.4 = f32[1024,12,64]{0,2,1:T(8,128)} fusion(f32[1024,12,64]{0,2,1:T(8,128)} %get-tuple-element.560, f32[12,512,1024]{2,1,0:T(8,128)} %exponential_select_fusion.2, f32[12,512,1024]{2,1,0:T(8,128)} %fusion.197, pred[]{:T(512)S(6)} %compare.3, bf16[2,512,12,64]{1,3,2,0:T(8,128)(2,1)} %get-tuple-element.575, s32[]{:T(128)S(6)} %copy.127), kind=kOutput, calls=%fused_computation.29.clone.1 | convolution fusion | flops 838343680 | bytes 107741192 | tf_op jit(solution)/shard_map/while/body/eval_jaxpr/while/body/eval_jaxpr/hqk,qhd->khd/dot_general | solution.py:83
  533.8 34.7 %reduce-scatter.21.cloned.1.call-done = bf16[96,768]{1,0:T(8,128)(2,1)} async-done(((bf16[768,768]{1,0:T(8,128)(2,1)}), bf16[96,768]{1,0:T(8,128)(2,1)}) %reduce-scatter.21.cloned.1.call-update) | async-done | bytes 147472
  570.2 38.2 %reduce-scatter.23.cloned.1.call-done = bf16[96,768]{1,0:T(8,128)(2,1)} async-done(((bf16[768,768]{1,0:T(8,128)(2,1)}), bf16[96,768]{1,0:T(8,128)(2,1)}) %reduce-scatter.23.cloned.1.call-update) | async-done | bytes 147472
  610.2 38.0 %reduce-scatter.13.cloned.1.call-done = bf16[96,768]{1,0:T(8,128)(2,1)} async-done(((bf16[768,768]{1,0:T(8,128)(2,1)}), bf16[96,768]{1,0:T(8,128)(2,1)}) %reduce-scatter.13.cloned.1.call-update) | async-done | bytes 147472 | tf_op jit(solution)/shard_map/reduce_scatter | solution.py:294
  648.2 57.3 %reduce-scatter.17.cloned.1.call-done = bf16[384,768]{1,0:T(8,128)(2,1)} async-done(((bf16[3072,768]{1,0:T(8,128)(2,1)}), bf16[384,768]{1,0:T(8,128)(2,1)}) %reduce-scatter.17.cloned.1.call-update) | async-done | bytes 589840 | tf_op jit(solution)/shard_map/reduce_scatter | solution.py:300
  705.5 57.1 %reduce-scatter.15.cloned.1.call-done = bf16[96,3072]{1,0:T(8,128)(2,1)} async-done(((bf16[768,3072]{1,0:T(8,128)(2,1)}), bf16[96,3072]{1,0:T(8,128)(2,1)}) %reduce-scatter.15.cloned.1.call-update) | async-done | bytes 589840 | tf_op jit(solution)/shard_map/reduce_scatter | solution.py:297
  774.1 24.5 %all-reduce.17 = (bf16[768]{0:T(1024)(128)(2,1)S(1)}, bf16[768]{0:T(1024)(128)(2,1)S(1)}, bf16[768]{0:T(1024)(128)(2,1)S(1)}, bf16[768]{0:T(1024)(128)(2,1)S(1)}...) all-reduce(bf16[768]{0:T(1024)(128)(2,1)S(1)} %dynamic-update-slice, ...), channel_id=1, replica_groups=mesh['rep'=4,'shard'=8] {'shard'}, use_global_device_ids=true, to_apply=%add.7 | all-reduce | flops 9984 | bytes 39936
  799.3 11.8 %all-reduce.19 = (bf16[96]{0:T(256)(128)(2,1)S(1)}, bf16[96]{0:T(256)(128)(2,1)S(1)}, bf16[96]{0:T(256)(128)(2,1)S(1)}, bf16[96]{0:T(256)(128)(2,1)S(1)}, bf16[9...) all-reduce(bf16[96]{0:T(256)(128)(2,1)S(1)} %dynamic-slice.11, ...), channel_id=1, replica_groups=mesh['rep'=4,'shard'=8] {'rep'}, use_global_device_ids=true, to_apply=%region_30.31 | all-reduce | flops 1152 | bytes 4608 | tf_op jit(solution)/shard_map/psum | solution.py:338
  821.9 25.3 %all-reduce.23.cloned.1.call-done = (bf16[96,768]{0,1:T(8,128)(2,1)}, bf16[96,768]{0,1:T(8,128)(2,1)}, bf16[96,768]{0,1:T(8,128)(2,1)}, bf16[96,768]{1,0:T(8,128...) async-done(((bf16[96,768]{0,1:T(8,128)(2,1)}, bf16[96,768]{0,1:T(8,128)(2,1)}, bf16[96,768]{0,1:T(8,128)(2,1)}, bf16[96,768]{1,0:T(8,128)(2,1)}, ...) | async-done | bytes 1769488 | tf_op jit(solution)/shard_map/psum | solution.py:332
  (335 shorter events, 253.4 us)
Async XLA Ops:
  7.2 55.5 %copy-start = (s32[1,8]{1,0:T(1,128)S(1)}, s32[1,8]{1,0:T(1,128)}, u32[]{:S(2)}) copy-start(s32[1,8]{1,0:T(1,128)} %param.26) | copy-start | bytes 100
  7.2 57.3 %all-gather.8.cloned.1.call-start = ((), (), s32[]{:S(2)}) async-start(), calls=%async_computation.6 | async-start | bytes 1327104 | tf_op jit(solution)/shard_map/all_gather | solution.py:155
  9.0 63.7 %all-gather.10.cloned.1.call-start = ((), (), s32[]{:S(2)}) async-start(), calls=%async_computation.7 | async-start | bytes 1327104 | tf_op jit(solution)/shard_map/all_gather | solution.py:155
  10.8 48.6 %copy-start.19 = (bf16[1,1024,768]{2,1,0:T(8,128)(2,1)S(1)}, bf16[1,1024,768]{2,1,0:T(8,128)(2,1)}, u32[]{:S(2)}) copy-start(bf16[1,1024,768]{2,1,0:T(8,128)(2,1)} %param.25) | copy-start | bytes 4718596
  10.8 79.3 %all-gather.12.cloned.1.call-start = ((), (), s32[]{:S(2)}) async-start(), calls=%async_computation.8 | async-start | bytes 1327104 | tf_op jit(solution)/shard_map/all_gather | solution.py:155
  12.7 160.9 %all-gather.14.cloned.1.call-start = ((), (), s32[]{:S(2)}) async-start(), calls=%async_computation.9 | async-start | bytes 1327104 | tf_op jit(solution)/shard_map/all_gather | solution.py:155
  14.4 165.3 %all-gather.16.cloned.1.call-start = ((), (), s32[]{:S(2)}) async-start(), calls=%async_computation.10 | async-start | bytes 5308416 | tf_op jit(solution)/shard_map/all_gather | solution.py:155
  15.3 45.7 %copy-start.20 = (bf16[1,1024,768]{2,1,0:T(8,128)(2,1)S(1)}, bf16[1,1024,768]{2,1,0:T(8,128)(2,1)}, u32[]{:S(2)}) copy-start(bf16[1,1024,768]{2,1,0:T(8,128)(2,1)} %param.24) | copy-start | bytes 4718596
  15.4 202.9 %all-gather.18.cloned.1.call-start = ((), (), s32[]{:S(2)}) async-start(), calls=%async_computation.11 | async-start | bytes 5308416 | tf_op jit(solution)/shard_map/all_gather | solution.py:155
  17.7 514.4 %reduce-scatter.19.cloned.1.call-start = ((), (), s32[]{:S(2)}) async-start(), calls=%async_computation.15 | async-start | bytes 1327104
  177.6 81.2 %copy-start.39 = (f32[1024]{0:T(1024)}, f32[1024]{0:T(1024)S(1)}, u32[]{:S(2)}) copy-start(f32[1024]{0:T(1024)S(1)} %broadcast_multiply_fusion.5) | copy-start | bytes 12292
  179.6 79.1 %copy-start.45 = (f32[1024]{0:T(1024)}, f32[1024]{0:T(1024)S(1)}, u32[]{:S(2)}) copy-start(f32[1024]{0:T(1024)S(1)} %add_rsqrt_fusion.1) | copy-start | bytes 12292
  179.7 38.6 %copy-start.55 = (f32[768]{0:T(1024)S(1)}, f32[768]{0:T(1024)}, u32[]{:S(2)}) copy-start(f32[768]{0:T(1024)} %convert_element_type.294) | copy-start | bytes 9220
  491.2 77.3 %reduce-scatter.21.cloned.1.call-start = ((), (), s32[]{:S(2)}) async-start(), calls=%async_computation.16 | async-start | bytes 1327104
  496.0 112.4 %reduce-scatter.23.cloned.1.call-start = ((), (), s32[]{:S(2)}) async-start(), calls=%async_computation.17 | async-start | bytes 1327104
  504.5 143.7 %reduce-scatter.13.cloned.1.call-start = ((), (), s32[]{:S(2)}) async-start(), calls=%async_computation.12 | async-start | bytes 1327104 | tf_op jit(solution)/shard_map/reduce_scatter | solution.py:294
  508.6 196.9 %reduce-scatter.17.cloned.1.call-start = ((), (), s32[]{:S(2)}) async-start(), calls=%async_computation.14 | async-start | bytes 5308416 | tf_op jit(solution)/shard_map/reduce_scatter | solution.py:300
  517.8 244.7 %reduce-scatter.15.cloned.1.call-start = ((), (), s32[]{:S(2)}) async-start(), calls=%async_computation.13 | async-start | bytes 5308416 | tf_op jit(solution)/shard_map/reduce_scatter | solution.py:297
  529.7 232.8 %copy-start.26 = (bf16[96,8,2,512]{3,1,2,0:T(8,128)(2,1)S(1)}, bf16[96,8,2,512]{3,1,2,0:T(8,128)(2,1)}, u32[]{:S(2)}) copy-start(bf16[96,8,2,512]{3,1,2,0:T(8,128)(2,1)} %copy-done.25) | copy-start | bytes 4718596
  529.8 317.5 %all-reduce.23.cloned.1.call-start = ((), (), s32[]{:S(2)}) async-start(), calls=%async_computation.18 | async-start | bytes 3833856 | tf_op jit(solution)/shard_map/psum | solution.py:332
  771.3 44.5 %copy-start.3 = (f32[1024,768]{0,1:T(8,128)S(1)}, f32[1024,768]{0,1:T(8,128)}, u32[]{:S(2)}) copy-start(f32[1024,768]{0,1:T(8,128)} %copy-done.2) | copy-start | bytes 9437188
  771.3 44.5 %copy-start.34 = (f32[1024]{0:T(1024)S(1)}, f32[1024]{0:T(1024)}, u32[]{:S(2)}) copy-start(f32[1024]{0:T(1024)} %copy-done.33) | copy-start | bytes 12292
  771.3 44.5 %copy-start.36 = (f32[768]{0:T(1024)S(1)}, f32[768]{0:T(1024)}, u32[]{:S(2)}) copy-start(f32[768]{0:T(1024)} %convert_element_type.296) | copy-start | bytes 9220
  771.3 44.5 %copy-start.38 = (f32[1024]{0:T(1024)S(1)}, f32[1024]{0:T(1024)}, u32[]{:S(2)}) copy-start(f32[1024]{0:T(1024)} %copy-done.37) | copy-start | bytes 12292
  (68 other events, 423.5 us)
Sparse Core Ops, SparseCore 0:
  10.5 26.6 all-gather.7
  39.7 23.9 all-gather.9
  66.1 23.9 all-gather.11
  92.4 23.9 all-gather.13
  118.7 38.8 all-gather.15
  159.9 38.8 all-gather.17
  491.3 36.5 reduce-scatter.18
  531.8 36.6 reduce-scatter.20
  571.7 36.6 reduce-scatter.22
  611.5 36.6 reduce-scatter.12
  651.6 53.7 reduce-scatter.16
  708.8 53.7 reduce-scatter.14
  766.0 81.1 all-reduce.22

commit v2 on v1

v2 whole, which is shorter than its diff:
```python
import functools
import math

import jax
import jax.numpy as jnp
from jax import lax
from jax.experimental import pallas as pl
from jax.experimental.pallas import tpu as pltpu
from jax.sharding import PartitionSpec as P

D = 768
HEADS = 12
HD = 64
LEN = 1024
FF = 3072
SLABS = 8
SROWS = D // SLABS
BF = jnp.bfloat16
F32 = jnp.float32
NN = (((1,), (0,)), ((), ()))
NT = (((1,), (1,)), ((), ()))
TN = (((0,), (0,)), ((), ()))
SMEM = pl.BlockSpec(memory_space=pltpu.SMEM)
ANY = pl.BlockSpec(memory_space=pl.ANY)


def dot(left, right, dims=NN):
    return lax.dot_general(left, right, dims, preferred_element_type=F32)


def sds(*shape, dtype=BF):
    return jax.ShapeDtypeStruct(shape, dtype)


def full(shape):
    return pl.BlockSpec(shape, lambda i: (0,) * len(shape), pipeline_mode=pl.Buffered(1))


def rows(count, width):
    return pl.BlockSpec((count, width), lambda i: (i, 0))


def cost(flops, moved):
    return pl.CostEstimate(flops=int(flops), bytes_accessed=int(moved), transcendentals=0)


def split3(value):
    high = value.astype(BF)
    rest = value - high.astype(F32)
    mid = rest.astype(BF)
    return high, mid, (rest - mid.astype(F32)).astype(BF)


def load_pieces(pieces, parts, me, scratch, sem):
    if len(pieces) == 1:
        copy = pltpu.make_async_copy(pieces[0], scratch, sem)
        copy.start()
        copy.wait()
        return
    for index, piece in enumerate(pieces):
        owner, half = me ^ (index // 2), index % 2
        for source, count, base, stride in parts:
            target = pl.multiple_of(base + owner * stride + half * count, 16)
            pltpu.make_async_copy(
                piece.at[pl.ds(source, count), :], scratch.at[pl.ds(target, count), :], sem
            ).start()
    pltpu.make_async_copy(scratch, scratch, sem).wait()


QKV_PARTS = tuple((48 * j, 48, D * j, 96) for j in range(3))
MID_PARTS = tuple((48 * j, 48, D * j, 96) for j in range(5)) + ((240, 192, 5 * D, 384),)
QKV_ROWS = 3 * D
MID_ROWS = 5 * D + FF
UP0 = D
DOWN0 = 5 * D


def qkv_kernel(meta_ref, x_ref, vec_ref, *refs, count):
    pieces, (q_ref, k_ref, v_ref, w_s, sem) = refs[:count], refs[count:]

    @pl.when(pl.program_id(0) == 0)
    def _():
        load_pieces(pieces, QKV_PARTS, meta_ref[2], w_s, sem)

    x = x_ref[...]
    q_ref[...] = ((dot(x, w_s[0:D, :]) + vec_ref[0:1, :]) * 0.125).astype(BF)
    k_ref[...] = dot(x, w_s[D : 2 * D, :]).astype(BF)
    v_ref[...] = (dot(x, w_s[2 * D : 3 * D, :]) + vec_ref[1:2, :]).astype(BF)


def qkv(meta, x, vec, pieces, R=256):
    return pl.pallas_call(
        functools.partial(qkv_kernel, count=len(pieces)),
        grid=(LEN // R,),
        in_specs=[SMEM, rows(R, D), full(vec.shape)] + [ANY] * len(pieces),
        out_specs=[rows(R, D)] * 3,
        out_shape=[sds(LEN, D)] * 3,
        scratch_shapes=[pltpu.VMEM((QKV_ROWS, D), BF), pltpu.SemaphoreType.DMA],
        cost_estimate=cost(2 * LEN * D * 3 * D, 10e6),
        name="qkv",
    )(meta, x, vec, *pieces)


def input_grad_kernel(meta_ref, da_ref, dq_ref, dk_ref, dv_ref, cot_ref, *refs, count, R):
    pieces, (out_ref, w_s, sem) = refs[:count], refs[count:]
    i = pl.program_id(0)

    @pl.when(i == 0)
    def _():
        load_pieces(pieces, QKV_PARTS, meta_ref[2], w_s, sem)

    total = da_ref[...].astype(F32) + dot(dq_ref[...], w_s[0:D, :], NT)
    total += dot(dk_ref[...], w_s[D : 2 * D, :], NT)
    total += dot(dv_ref[...], w_s[2 * D : 3 * D, :], NT)
    row = lax.broadcasted_iota(jnp.int32, (R, 1), 0) + i * R
    live = (row < meta_ref[0]) & (meta_ref[1] == 0)
    out_ref[...] = jnp.where(live, total, cot_ref[...].astype(F32)).astype(BF)


def input_grad(meta, da, dq, dk, dv, cot, pieces, R=256):
    return pl.pallas_call(
        functools.partial(input_grad_kernel, count=len(pieces), R=R),
        grid=(LEN // R,),
        in_specs=[SMEM] + [rows(R, D)] * 5 + [ANY] * len(pieces),
        out_specs=rows(R, D),
        out_shape=sds(LEN, D),
        scratch_shapes=[pltpu.VMEM((QKV_ROWS, D), BF), pltpu.SemaphoreType.DMA],
        cost_estimate=cost(2 * LEN * D * 3 * D, 13e6),
        name="input_grad",
    )(meta, da, dq, dk, dv, cot, *pieces)


def own_lanes(lane, head):
    return (lane < 64) if head == 0 else (lane >= 64)


def attend_kernel(meta_ref, q_ref, k_ref, v_ref, ctx_ref, aug_ref, *, qb):
    length = meta_ref[0]
    lane = lax.broadcasted_iota(jnp.int32, (LEN, 128), 1)
    row = lax.broadcasted_iota(jnp.int32, (LEN, 128), 0)
    bias = jnp.where(row < length, 0.0, -1e30).astype(BF)
    k = k_ref[...]
    v = v_ref[...]
    one = jnp.ones((), BF)
    zero = jnp.zeros((), BF)
    heads = []
    for h in range(2):
        mine = own_lanes(lane, h)
        spare = 64 if h == 0 else 0
        heads.append(
            (
                jnp.where(mine, k, jnp.where(lane == spare + 3, bias, one)),
                jnp.where(mine, v, one),
                spare,
            )
        )
    lane_q = lax.broadcasted_iota(jnp.int32, (qb, 128), 1)

    @pl.loop(0, LEN // qb)
    def _(i):
        r0 = pl.multiple_of(i * qb, qb)
        q = q_ref[pl.ds(r0, qb), :]
        outs = []
        for h in range(2):
            kh, vh, spare = heads[h]
            qh = jnp.where(own_lanes(lane_q, h), q, jnp.where(lane_q == spare + 3, one, zero))
            s = dot(qh, kh, NT)
            peak = jnp.max(s, axis=1, keepdims=True)
            p = jnp.exp(s - peak).astype(BF)
            o = dot(p, vh)
            total = o[:, 64:65] if h == 0 else o[:, 0:1]
            high, mid, low = split3(-(peak + jnp.log(total)))
            aug_ref[h, pl.ds(r0, qb), :] = jnp.where(
                lane_q == spare,
                high,
                jnp.where(lane_q == spare + 1, mid, jnp.where(lane_q == spare + 2, low, qh)),
            )
            outs.append(o / total)
        ctx_ref[pl.ds(r0, qb), :] = jnp.where(lane_q < 64, outs[0], outs[1]).astype(BF)


def attend(meta, q, k, v, first, count, qb=512):
    wide = pl.BlockSpec((LEN, 128), lambda i: (0, i + first))
    return pl.pallas_call(
        functools.partial(attend_kernel, qb=qb),
        grid=(count,),
        in_specs=[SMEM, wide, wide, wide],
        out_specs=[
            pl.BlockSpec((LEN, 128), lambda i: (0, i)),
            pl.BlockSpec((2, LEN, 128), lambda i: (i, 0, 0)),
        ],
        out_shape=[sds(LEN, 128 * count), sds(2 * count, LEN, 128)],
        cost_estimate=cost(count * 2.4e9, count * 1.5e6),
        name="attend",
    )(meta, q, k, v)


def attend_back_kernel(
    meta_ref, aug_ref, k_ref, v_ref, o_ref, do_ref, dq_ref, dk_ref, dv_ref, sums_ref,
    qa_s, doa_s, dom_s, kt_s, dqt_s, *, kb
):
    length = meta_ref[0]
    one = jnp.ones((), BF)
    zero = jnp.zeros((), BF)
    lane = lax.broadcasted_iota(jnp.int32, (LEN, 128), 1)
    do = do_ref[...]
    product = do.astype(F32) * o_ref[...].astype(F32)
    for h in range(2):
        mine = own_lanes(lane, h)
        spare = 64 if h == 0 else 0
        high, mid, low = split3(
            -jnp.sum(jnp.where(mine, product, 0.0), axis=1, keepdims=True)
        )
        own = jnp.where(mine, do, zero)
        dom_s[h] = own
        doa_s[h] = jnp.where(
            lane == spare,
            high,
            jnp.where(lane == spare + 1, mid, jnp.where(lane == spare + 2, low, own)),
        )
        qa_s[h] = jnp.where(mine, aug_ref[h], zero)
    kt_s[...] = k_ref[...].astype(F32).T.astype(BF)
    dqt_s[...] = jnp.zeros_like(dqt_s)
    sums_ref[...] = jnp.zeros_like(sums_ref)
    lane_k = lax.broadcasted_iota(jnp.int32, (kb, 128), 1)

    @pl.loop(0, LEN // kb)
    def _(i):
        r0 = pl.multiple_of(i * kb, kb)
        row = lax.broadcasted_iota(jnp.int32, (kb, 128), 0) + r0
        bias = jnp.where(row < length, 0.0, -1e30).astype(BF)
        k = k_ref[pl.ds(r0, kb), :]
        v = v_ref[pl.ds(r0, kb), :]
        kt = kt_s[:, pl.ds(r0, kb)]
        dk = dv = None
        for h in range(2):
            mine = own_lanes(lane_k, h)
            spare = 64 if h == 0 else 0
            unit = jnp.where((lane_k >= spare) & (lane_k < spare + 3), one, zero)
            kh = jnp.where(mine, k, jnp.where(lane_k == spare + 3, bias, unit))
            vh = jnp.where(mine, v, unit)
            p = jnp.exp(dot(kh, aug_ref[h], NT))
            dp = dot(vh, doa_s[h], NT)
            ds = (p * dp).astype(BF)
            dvh = dot(p.astype(BF), dom_s[h])
            dkh = dot(ds, qa_s[h])
            dqt_s[64 * h : 64 * h + 64, :] += dot(kt[64 * h : 64 * h + 64, :], ds)
            dk, dv = (dkh, dvh) if h == 0 else (dk + dkh, dv + dvh)
        dv_ref[pl.ds(r0, kb), :] = dv.astype(BF)
        dk_ref[pl.ds(r0, kb), :] = dk.astype(BF)
        sums_ref[1:2, :] += jnp.sum(dv, axis=0, keepdims=True)

    dq = (dqt_s[...] * 0.125).T
    sums_ref[0:1, :] = jnp.sum(dq, axis=0, keepdims=True)
    dq_ref[...] = dq.astype(BF)


def attend_back(meta, aug, k, v, o, do, first, local, count, kb=512):
    wide = pl.BlockSpec((LEN, 128), lambda i: (0, i + first))
    near = pl.BlockSpec((LEN, 128), lambda i: (0, i + local))
    out = pl.BlockSpec((LEN, 128), lambda i: (0, i))
    return pl.pallas_call(
        functools.partial(attend_back_kernel, kb=kb),
        grid=(count,),
        in_specs=[
            SMEM, pl.BlockSpec((2, LEN, 128), lambda i: (i + local, 0, 0)), wide, wide, near, wide
        ],
        out_specs=[out, out, out, pl.BlockSpec((8, 128), lambda i: (0, i))],
        out_shape=[sds(LEN, 128 * count)] * 3 + [sds(8, 128 * count, dtype=F32)],
        scratch_shapes=[pltpu.VMEM((2, LEN, 128), BF)] * 3
        + [pltpu.VMEM((128, LEN), BF), pltpu.VMEM((128, LEN), F32)],
        cost_estimate=cost(count * 3.4e9, count * 2.5e6),
        name="attend_back",
    )(meta, aug, k, v, o, do)


def gelu_parts(u):
    t = 1.0 / (1.0 + (0.3275911 * math.sqrt(0.5)) * jnp.abs(u))
    poly = t * (
        0.127414796
        + t * (-0.142248368 + t * (0.7107068705 + t * (-0.7265760135 + t * 0.5307027145)))
    )
    bell = jnp.exp(-0.5 * (u * u))
    tail = poly * bell
    phi = jnp.where(u >= 0, 1.0 - tail, tail)
    return u * phi, phi + u * bell * (1.0 / math.sqrt(2.0 * math.pi))


def norm(h):
    offset = h - jnp.mean(h, axis=1, keepdims=True)
    inverse = lax.rsqrt(jnp.mean(offset * offset, axis=1, keepdims=True) + 1e-05)
    return offset * inverse, inverse


def norm_back(s, normed, inverse):
    return inverse * (
        s
        - jnp.mean(s, axis=1, keepdims=True)
        - normed * jnp.mean(s * normed, axis=1, keepdims=True)
    )


def mid1_kernel(meta_ref, x_ref, ctxa_ref, ctxb_ref, cot_ref, vec_ref, ub_ref, *refs, count, R):
    pieces = refs[:count]
    (out_ref, fl_ref, act_ref, slope_ref, n1_ref, inv_ref, db_ref, sums_ref,
     acc_s, w_s, sem) = refs[count:]
    i = pl.program_id(0)

    @pl.when(i == 0)
    def _():
        load_pieces(pieces, MID_PARTS, meta_ref[2], w_s, sem)
        sums_ref[...] = jnp.zeros_like(sums_ref)

    x = x_ref[...].astype(F32)
    wide = ctxa_ref.shape[1]
    attended = dot(ctxa_ref[...], w_s[0:wide, :]) + dot(ctxb_ref[...], w_s[wide:D, :])
    n1, inv1 = norm(x + attended + vec_ref[2:3, :])
    first = n1 * vec_ref[3:4, :] + vec_ref[4:5, :]
    fl_ref[...] = first.astype(BF)
    n1_ref[...] = n1.astype(BF)
    inv_ref[...] = jnp.broadcast_to(inv1, (R, 128))
    acc_s[...] = first + vec_ref[5:6, :]

    @pl.loop(0, FF // D)
    def _(c):
        c0 = pl.multiple_of(c * D, D)
        u = dot(fl_ref[...], w_s[pl.ds(UP0 + c0, D), :]) + ub_ref[0:1, pl.ds(c0, D)]
        act, slope = gelu_parts(u)
        act = act.astype(BF)
        act_ref[:, pl.ds(c0, D)] = act
        slope_ref[:, pl.ds(c0, D)] = slope.astype(BF)
        acc_s[...] += dot(act, w_s[pl.ds(DOWN0 + c0, D), :])

    n2, inv2 = norm(acc_s[...])
    gain = vec_ref[6:7, :]
    final = n2 * gain + vec_ref[7:8, :]
    row = lax.broadcasted_iota(jnp.int32, (R, 1), 0) + i * R
    live = (row < meta_ref[0]) & (meta_ref[1] == 0)
    out_ref[...] = jnp.where(live, final, x).astype(BF)
    up = jnp.where(live, cot_ref[...].astype(F32), 0.0)
    db = norm_back(up * gain, n2, inv2).astype(BF)
    db_ref[...] = db
    sums_ref[0:1, :] += jnp.sum(up * n2, axis=0, keepdims=True)
    sums_ref[1:2, :] += jnp.sum(up, axis=0, keepdims=True)
    sums_ref[2:3, :] += jnp.sum(db.astype(F32), axis=0, keepdims=True)


def mid1(meta, x, ctxa, ctxb, cot, vec, ub, pieces, R=256):
    return pl.pallas_call(
        functools.partial(mid1_kernel, count=len(pieces), R=R),
        grid=(LEN // R,),
        in_specs=[
            SMEM, rows(R, D), rows(R, ctxa.shape[1]), rows(R, ctxb.shape[1]), rows(R, D),
            full(vec.shape), full(ub.shape),
        ]
        + [ANY] * len(pieces),
        out_specs=[
            rows(R, D), rows(R, D), rows(R, FF), rows(R, FF), rows(R, D), rows(R, 128),
            rows(R, D), pl.BlockSpec((8, D), lambda i: (0, 0)),
        ],
        out_shape=[
            sds(LEN, D), sds(LEN, D), sds(LEN, FF), sds(LEN, FF), sds(LEN, D),
            sds(LEN, 128, dtype=F32), sds(LEN, D), sds(8, D, dtype=F32),
        ],
        scratch_shapes=[
            pltpu.VMEM((R, D), F32), pltpu.VMEM((MID_ROWS, D), BF), pltpu.SemaphoreType.DMA
        ],
        cost_estimate=cost(16e9, 34e6),
        name="mid1",
    )(meta, x, ctxa, ctxb, cot, vec, ub, *pieces)


def mid2_kernel(meta_ref, db_ref, slope_ref, n1_ref, inv_ref, vec_ref, *refs, count, R):
    pieces = refs[:count]
    dh_ref, da_ref, dctx_ref, sums_ref, ups_ref, acc_s, w_s, sem = refs[count:]

    @pl.when(pl.program_id(0) == 0)
    def _():
        load_pieces(pieces, MID_PARTS, meta_ref[2], w_s, sem)
        sums_ref[...] = jnp.zeros_like(sums_ref)
        ups_ref[...] = jnp.zeros_like(ups_ref)

    acc_s[...] = db_ref[...].astype(F32)

    @pl.loop(0, FF // D)
    def _(c):
        c0 = pl.multiple_of(c * D, D)
        dact = dot(db_ref[...], w_s[pl.ds(DOWN0 + c0, D), :], NT)
        dh = (dact * slope_ref[:, pl.ds(c0, D)].astype(F32)).astype(BF)
        dh_ref[:, pl.ds(c0, D)] = dh
        ups_ref[0:1, pl.ds(c0, D)] += jnp.sum(dh.astype(F32), axis=0, keepdims=True)
        acc_s[...] += dot(dh, w_s[pl.ds(UP0 + c0, D), :], NT)

    df = acc_s[...]
    n1 = n1_ref[...].astype(F32)
    da = norm_back(df * vec_ref[3:4, :], n1, inv_ref[:, 0:1]).astype(BF)
    da_ref[...] = da
    dctx_ref[...] = dot(da, w_s[0:D, :], NT).astype(BF)
    sums_ref[0:1, :] += jnp.sum(df * n1, axis=0, keepdims=True)
    sums_ref[1:2, :] += jnp.sum(df, axis=0, keepdims=True)
    sums_ref[2:3, :] += jnp.sum(da.astype(F32), axis=0, keepdims=True)


def mid2(meta, db, slope, n1, inv, vec, pieces, R=256):
    return pl.pallas_call(
        functools.partial(mid2_kernel, count=len(pieces), R=R),
        grid=(LEN // R,),
        in_specs=[SMEM, rows(R, D), rows(R, FF), rows(R, D), rows(R, 128), full(vec.shape)]
        + [ANY] * len(pieces),
        out_specs=[
            rows(R, FF), rows(R, D), rows(R, D),
            pl.BlockSpec((8, D), lambda i: (0, 0)), pl.BlockSpec((8, FF), lambda i: (0, 0)),
        ],
        out_shape=[
            sds(LEN, FF), sds(LEN, D), sds(LEN, D), sds(8, D, dtype=F32), sds(8, FF, dtype=F32)
        ],
        scratch_shapes=[
            pltpu.VMEM((R, D), F32), pltpu.VMEM((MID_ROWS, D), BF), pltpu.SemaphoreType.DMA
        ],
        cost_estimate=cost(12e9, 30e6),
        name="mid2",
    )(meta, db, slope, n1, inv, vec, *pieces)


def slabs_out(scr, me, send_ref, keep_ref, row0, sem):
    copies = []
    for k in range(SLABS):
        source = scr.at[pl.ds(pl.multiple_of((me ^ k) * SROWS, 16), SROWS), :]
        target = (send_ref if k % 2 else keep_ref).at[k // 2, pl.ds(row0, SROWS), :]
        copies.append(pltpu.make_async_copy(source, target, sem.at[k]))
    return copies


def pairs_kernel(meta_ref, *refs, groups, total):
    count = len(groups)
    send_ref, keep_ref, scr, sem = refs[2 * count :]
    me = meta_ref[2]
    step = 0
    waiting = {}
    for g, blocks in enumerate(groups):
        left_ref, right_ref = refs[2 * g], refs[2 * g + 1]
        width = scr.shape[2]
        for b in range(blocks):
            slot = step % 2
            if step >= 2:
                for copy in waiting[step - 2]:
                    copy.wait()
            scr[slot] = dot(left_ref[...], right_ref[:, width * b : width * (b + 1)], TN).astype(BF)
            waiting[step] = slabs_out(
                scr.at[slot], me, send_ref, keep_ref, step * SROWS, sem.at[slot]
            )
            for copy in waiting[step]:
                copy.start()
            step += 1
    for late in (total - 2, total - 1):
        if late >= 0:
            for copy in waiting[late]:
                copy.wait()


def pair_grads(meta, pairs, width):
    groups = tuple(right.shape[1] // width for _, right in pairs)
    total = sum(groups)
    flat = [a for pair in pairs for a in pair]
    vm = pl.BlockSpec(memory_space=pltpu.VMEM)
    return pl.pallas_call(
        functools.partial(pairs_kernel, groups=groups, total=total),
        in_specs=[SMEM] + [vm] * len(flat),
        out_specs=[ANY, ANY],
        out_shape=[sds(4, total * SROWS, width)] * 2,
        scratch_shapes=[pltpu.VMEM((2, D, width), BF), pltpu.SemaphoreType.DMA((2, SLABS))],
        cost_estimate=cost(2 * LEN * D * width * total * 1.2, 15e6),
        name="pair_grads",
    )(meta, *flat)


def down_kernel(meta_ref, act_ref, db_ref, send_ref, keep_ref):
    i = pl.program_id(0)
    value = dot(act_ref[...], db_ref[...], TN).astype(BF)

    @pl.when(i < 4)
    def _():
        send_ref[0] = value

    @pl.when(i >= 4)
    def _():
        keep_ref[0] = value


def down_grads(meta, act, db):
    def owner(i, m):
        k = jnp.where(i < 4, 2 * i + 1, 2 * (i - 4))
        return m[2] ^ k

    return pl.pallas_call(
        down_kernel,
        grid_spec=pltpu.PrefetchScalarGridSpec(
            num_scalar_prefetch=1,
            grid=(SLABS,),
            in_specs=[
                pl.BlockSpec((LEN, FF // SLABS), lambda i, m: (0, owner(i, m))),
                pl.BlockSpec((LEN, D), lambda i, m: (0, 0), pipeline_mode=pl.Buffered(1)),
            ],
            out_specs=[
                pl.BlockSpec((1, FF // SLABS, D), lambda i, m: (jnp.minimum(i, 3), 0, 0)),
                pl.BlockSpec((1, FF // SLABS, D), lambda i, m: (jnp.maximum(i - 4, 0), 0, 0)),
            ],
        ),
        out_shape=[sds(4, FF // SLABS, D)] * 2,
        cost_estimate=cost(2 * LEN * FF * D * 1.2, 13e6),
        name="down_grads",
    )(meta, act, db)


def swap(value, axis, bit, size):
    return lax.ppermute(value, axis, [(i, i ^ bit) for i in range(size)])


def gather_halves(halves):
    pieces = [None] * 16
    held = [{0: halves[0]}, {0: halves[1]}]
    for stage in range(3):
        for h, order in enumerate(((2, 4, 1), (4, 2, 1))):
            bit = order[stage]
            held[h].update({k ^ bit: swap(v, "shard", bit, 8) for k, v in list(held[h].items())})
    for h in range(2):
        for k, v in held[h].items():
            pieces[2 * k + h] = v
    return pieces


def add(*terms):
    return sum(t.astype(F32) for t in terms).astype(BF)


def reduce_slabs(send, keep):
    got = swap(send, "shard", 1, 8)
    half = send.shape[1] // 2
    ends = []
    for cut, first, second, out, stay in (
        (slice(0, half), 2, 4, (1, 3), (0, 2)),
        (slice(half, None), 4, 2, (2, 3), (0, 1)),
    ):
        away = [add(keep[p, cut], got[p, cut]) for p in out]
        back = swap(jnp.stack(away), "shard", first, 8)
        far = add(keep[stay[1], cut], got[stay[1], cut], back[1])
        last = swap(far, "shard", second, 8)
        ends.append(add(keep[0, cut], got[0, cut], back[0], last))
    return jnp.concatenate(ends)


def reduce_rep(value, place):
    quarter = value.shape[0] // 4
    parts = value.reshape(4, quarter, value.shape[1])
    mine = lax.dynamic_index_in_dim(parts, place, 0, False)
    terms = [mine]
    for k in (1, 2, 3):
        part = lax.dynamic_index_in_dim(parts, place ^ k, 0, False)
        terms.append(swap(part, "rep", k, 4))
    total = add(*terms)
    out = jnp.zeros(parts.shape, F32)
    out = lax.dynamic_update_index_in_dim(out, total.astype(F32), place, 0)
    for k in (1, 2, 3):
        out = lax.dynamic_update_index_in_dim(
            out, swap(total, "rep", k, 4).astype(F32), place ^ k, 0
        )
    return out.reshape(value.shape)


def whole_slabs(send, keep):
    return jnp.stack([keep, send], axis=1).reshape((SLABS,) + send.shape[1:])


def reduce_any(matrix):
    share = lax.psum_scatter(matrix, "shard", scatter_dimension=0, tiled=True)
    return lax.psum(share, "rep").astype(F32)


def body(n_shard, n_rep, tokens, cotangent, lengths, dealing, drop_flags, *masters):
    matrices = [m.astype(BF) for m in masters[:6]]
    vectors = [m.astype(BF) for m in masters[6:]]
    permuted = n_shard == 8 and n_rep == 4
    position = lax.axis_index("shard")
    me = position if permuted else jnp.zeros((), jnp.int32)
    place = lax.axis_index("rep")
    length = lax.dynamic_index_in_dim(lengths[0], position, 0, False)
    flag = jnp.sum(jnp.where(dealing[0] == position, drop_flags[0], 0))
    meta = jnp.stack([length, flag, me]).astype(jnp.int32)
    x = tokens.reshape(LEN, D)
    cot = cotangent.reshape(LEN, D)

    names = vectors[:5] + vectors[6:9]
    width = D // n_shard
    small = jnp.concatenate([v[None] for v in names] + [vectors[5].reshape(4, width)])
    wq, wk, wv, wo, wu, wd = matrices
    if permuted:
        held = small[None]
        for bit in (1, 2, 4):
            held = jnp.concatenate([held, swap(held, "shard", bit, 8)])
        every = jnp.take(held, jnp.arange(8, dtype=jnp.int32) ^ position, axis=0)
        ups = [wu[:, D * j : D * (j + 1)] for j in range(4)]
        cuts = (slice(0, 48), slice(48, 96))
        near = gather_halves(
            [jnp.concatenate([m[c] for m in (wq, wk, wv)]) for c in cuts]
        )
        down_cuts = (slice(0, 192), slice(192, 384))
        far_halves = [
            jnp.concatenate([m[c] for m in [wo] + ups] + [wd[c2]])
            for c, c2 in zip(cuts, down_cuts)
        ]
        far_halves[0], far_halves[1], near = lax.optimization_barrier(
            (far_halves[0], far_halves[1], near)
        )
        far = gather_halves(far_halves)
    else:
        every = lax.all_gather(small, "shard", axis=0)
        whole = [lax.all_gather(m, "shard", axis=0, tiled=True) for m in matrices]
        near = [jnp.concatenate(whole[:3])]
        far = [
            jnp.concatenate(
                [whole[3]] + [whole[4][:, D * j : D * (j + 1)] for j in range(4)] + [whole[5]]
            )
        ]
    every = every.astype(F32)
    vec = every[:, :8].transpose(1, 0, 2).reshape(8, D)
    ub = every[:, 8:].reshape(1, FF)
    ub = jnp.broadcast_to(ub, (8, FF))

    q, k, v = qkv(meta, x, vec, near)
    ctxa, auga = attend(meta, q, k, v, 0, 4)
    ctxb, augb = attend(meta, q, k, v, 4, 2)
    output, first, act, slope, n1, inv, db, sums1 = mid1(meta, x, ctxa, ctxb, cot, vec, ub, far)
    down = down_grads(meta, act, db)
    dh, da, dctx, sums2, sums_up = mid2(meta, db, slope, n1, inv, vec, far)
    ctx = jnp.concatenate([ctxa, ctxb], axis=1)
    upout = pair_grads(meta, ((first, dh), (ctx, da)), D)
    dqa, dka, dva, sums_a = attend_back(meta, auga, k, v, ctxa, dctx, 0, 0, 4)
    qkva = pair_grads(meta, ((x, dqa), (x, dka), (x, dva)), 512)
    dqb, dkb, dvb, sums_b = attend_back(meta, augb, k, v, ctxb, dctx, 4, 0, 2)
    qkvb = pair_grads(meta, ((x, dqb), (x, dkb), (x, dvb)), 256)
    dq, dk, dv = (
        jnp.concatenate(p, axis=1) for p in ((dqa, dqb), (dka, dkb), (dva, dvb))
    )
    grad_x = input_grad(meta, da, dq, dk, dv, cot, near)

    sums_ab = jnp.concatenate([sums_a[:2], sums_b[:2]], axis=1)
    sums = jnp.concatenate(
        [
            sums_ab, sums2[2:3], sums2[0:2], sums1[2:3], sums1[0:2],
            sums_up[0].reshape(4, D),
        ]
    )
    if permuted:
        for bit in (1, 2, 4):
            sums = sums + swap(sums, "shard", bit, 8)
        for bit in (1, 2):
            sums = sums + swap(sums, "rep", bit, 4)
    else:
        sums = lax.psum(sums, ("rep", "shard"))
    grads_v = [
        lax.dynamic_slice_in_dim(sums[r], position * width, width) for r in range(8)
    ]
    grad_ub = lax.dynamic_slice_in_dim(
        sums[8:].reshape(FF), position * (FF // n_shard), FF // n_shard
    )

    if permuted:
        grad_down = reduce_rep(reduce_slabs(*down), place)
        g_uo = reduce_rep(reduce_slabs(*upout), place)
        g_a = reduce_rep(reduce_slabs(*qkva), place)
        g_b = reduce_rep(reduce_slabs(*qkvb), place)
        grad_up = jnp.concatenate([g_uo[96 * j : 96 * (j + 1)] for j in range(4)], axis=1)
        grad_out = g_uo[384:]
        grad_qkv = [
            jnp.concatenate([g[96 * j : 96 * (j + 1)] for g in (g_a, g_b)], axis=1)
            for j in range(3)
        ]
    else:
        def rebuild(slabs, j):
            return slabs[:, SROWS * j : SROWS * (j + 1)].reshape(D, slabs.shape[2])

        grad_down = reduce_any(whole_slabs(*down).reshape(FF, D))
        g_uo, g_a, g_b = (whole_slabs(*p) for p in (upout, qkva, qkvb))
        grad_up = reduce_any(jnp.concatenate([rebuild(g_uo, j) for j in range(4)], axis=1))
        grad_out = reduce_any(rebuild(g_uo, 4))
        grad_qkv = [
            reduce_any(jnp.concatenate([rebuild(g, j) for g in (g_a, g_b)], axis=1))
            for j in range(3)
        ]
    return (
        output.reshape(tokens.shape),
        grad_x.reshape(tokens.shape),
        grad_qkv[0],
        grad_qkv[1],
        grad_qkv[2],
        grad_out,
        grad_up,
        grad_down,
        grads_v[0],
        grads_v[1],
        grads_v[2],
        grads_v[3],
        grads_v[4],
        grad_ub,
        grads_v[5],
        grads_v[6],
        grads_v[7],
    )


def solution(mesh):
    tokens = P(("rep", "shard"), None, None)
    table = P("rep", None)
    matrix = P("shard", None)
    vector = P("shard")
    return jax.shard_map(
        functools.partial(body, mesh.shape["shard"], mesh.shape["rep"]),
        mesh=mesh,
        in_specs=(tokens, tokens) + (table,) * 3 + (matrix,) * 6 + (vector,) * 9,
        out_specs=(tokens, tokens) + (matrix,) * 6 + (vector,) * 9,
        check_vma=False,
    )
```

time: 876 us -> 455 us (0.52)
  matrix products: 380 us -> 0 us
  Pallas kernels: 0 us -> 193 us
  waiting for transfers between devices: 265 us -> 123 us
  starting transfers between devices: 0.54 us -> 82.8 us
  blocking collectives: 70.1 us -> 0 us
  local copies, waits for them, and re-layouts: 66.6 us -> 19.9 us
  other arithmetic: 63.1 us -> 29.4 us
  between operations: 18 us -> 2.11 us
    dot_general x32 -> x0, matrix products: 380 us -> none  [the longest x2 69.5 us: per_block(): jnp.einsum('hqk,qhd->khd', dscores, query_blk, preferred_element_type=jnp...]
    pallas_call x0 -> x12, Pallas kernels: none -> 193 us  [the longest x2 43 us: attend_back(): pl.pallas_call(functools.partial(attend_back_kernel, kb=kb), grid=(count,...]
    reduce_scatter x3 -> x0, waiting for transfers between devices: 152 us -> none  [the longest x1 57.3 us: body(): lax.psum_scatter(local_grads[5].astype(jnp.bfloat16), 'shard', scatter_di...]
    ppermute x0 -> x80, waiting for transfers between devices: none -> 123 us  [swap(): return lax.ppermute(value, axis, [(i, i ^ bit) for i in range(size)])]
    ppermute x0 -> x80, starting transfers between devices: none -> 82.8 us  [swap(): return lax.ppermute(value, axis, [(i, i ^ bit) for i in range(size)])]
    unnamed x16 -> x0, waiting for transfers between devices: 73.1 us -> none
    unnamed x2 -> x0, blocking collectives: 50.3 us -> none
    unnamed x194 -> x101, local copies, waits for them, and re-layouts: 47.3 us -> 3.11 us
  transfers between devices with their start and end apart: 13 -> 80, of which waited for: 7 -> 38; matrix products, arithmetic and copies ran while one was open for 25% -> 8% of each run, Pallas kernels for 0% -> 20%
where the time goes in v2:
time: 455 us; the launch traced here: 451 us
  Pallas kernels  193 us (42%)
  waiting for transfers between devices  123 us (27%)
  starting transfers between devices  82.8 us (18%)
  other arithmetic  29.4 us (6%)
  local copies, waits for them, and re-layouts  19.9 us (4%)
    ppermute x80, waiting for transfers between devices, swap(): return lax.ppermute(value, axis, [(i, i ^ bit) for i in range(size)])  123 us
    ppermute x80, starting transfers between devices, swap(): return lax.ppermute(value, axis, [(i, i ^ bit) for i in range(size)])  82.8 us
    pallas_call x2, Pallas kernels, attend_back(): pl.pallas_call(functools.partial(attend_back_kernel, kb=kb), grid=(count,...  43 us
    pallas_call x1, Pallas kernels, mid1(): pl.pallas_call(functools.partial(mid1_kernel, count=len(pieces), R=R), gr...  35.1 us
    pallas_call x2, Pallas kernels, attend(): pl.pallas_call(functools.partial(attend_kernel, qb=qb), grid=(count,), in...  31 us
    pallas_call x3, Pallas kernels, pair_grads(): pl.pallas_call(functools.partial(pairs_kernel, groups=groups, total=total...  28.1 us
    pallas_call x1, Pallas kernels, mid2(): pl.pallas_call(functools.partial(mid2_kernel, count=len(pieces), R=R), gr...  25.6 us
    pallas_call x1, Pallas kernels, down_grads(): pl.pallas_call(down_kernel, grid_spec=pltpu.PrefetchScalarGridSpec(num_sc...  12.2 us
  transfers between devices with their start and end apart: 80, of which 38 were waited for; matrix products, arithmetic and copies ran while one was open for 8% of the time, Pallas kernels for 20%

profile of v2, /device:TPU:0, one launch (start us, length us, event | category | flops | bytes accessed | tf_op | source)
XLA Modules:
  0.0 450.8 jit_solution(7624864354342789354)
XLA Ops:
  13.2 5.4 %collective-permute-done.10.refs_9_ = bf16[144,768]{1,0:T(8,128)(2,1)} collective-permute-done((bf16[144,768]{1,0:T(8,128)(2,1)S(1)}, bf16[144,768]{1,0:T(8,128)(2,1)}, u32[]{:S(2)}, u32[]{:S(2)}) %collective-permute-start.10) | collective-permute-done | bytes 221216 | tf_op jit(solution)/shard_map/ppermute | solution.py:516
  21.4 5.5 %collective-permute-done.13.refs_12_ = bf16[144,768]{1,0:T(8,128)(2,1)S(1)} collective-permute-done((bf16[144,768]{1,0:T(8,128)(2,1)S(1)}, bf16[144,768]{1,0:T(8,128)(2,1)S(1)}, u32[]{:S(2)}, u32[]{:S(2)}) %collective-permute-start.13) | collective-permute-done | bytes 221216 | tf_op jit(solution)/shard_map/ppermute | solution.py:516
  35.6 26.3 %collective-permute-done.1 = bf16[2,12,96]{2,1,0:T(8,128)(2,1)S(1)} collective-permute-done((bf16[2,12,96]{2,1,0:T(8,128)(2,1)S(1)}, bf16[2,12,96]{2,1,0:T(8,128)(2,1)S(1)}, u32[]{:S(2)}, u32[]{:S(2)}) %collective-permute-start.1) | collective-permute-done | bytes 4640 | tf_op jit(solution)/shard_map/ppermute | solution.py:516
  69.9 8.8 %qkv.1 = (bf16[1024,768]{1,0:T(8,128)(2,1)}, bf16[1024,768]{1,0:T(8,128)(2,1)}, bf16[1024,768]{1,0:T(8,128)(2,1)}) custom-call(s32[3]{0:T(128)} %pad_add_fusion.meta_ref, bf16[1024,768]{1,0:T(8,128)(2,1)} %bitcast.188, f32[8,768]{1,0:T(8,128)} %reshape.213.vec_ref, bf16[144,768]{1,0:T(8,128)(2,1)} %copy-done.18, bf16[144,768]{1,0:T(8,128)(2,1)} %copy-done.19, ...), custom_call_target="tpu_custom_call" | custom-call | flops 3623878656 | bytes 10000000 | tf_op jit(solution)/shard_map/qkv/pallas_call | solution.py:92
  79.3 4.6 %collective-permute-done.27.refs_12_ = bf16[432,768]{1,0:T(8,128)(2,1)} collective-permute-done((bf16[432,768]{1,0:T(8,128)(2,1)S(1)}, bf16[432,768]{1,0:T(8,128)(2,1)}, u32[]{:S(2)}, u32[]{:S(2)}) %collective-permute-start.27) | collective-permute-done | bytes 663584 | tf_op jit(solution)/shard_map/ppermute | solution.py:516
  85.4 20.0 %attend.2 = (bf16[1024,512]{1,0:T(8,128)(2,1)}, bf16[8,1024,128]{2,1,0:T(8,128)(2,1)}) custom-call(s32[3]{0:T(128)} %pad_add_fusion.meta_ref, bf16[1024,768]{1,0:T(8,128)(2,1)} %get-tuple-element.87.q_ref, bf16[1024,768]{1,0:T(8,128)(2,1)} %get-tuple-element.88.k_ref, bf16[1024,768]{1,0:T(8,128)(2,1)} %get-tuple-element.89.v_ref), custom_call_target="tpu_custom_call" | custom-call | flops 9600000000 | bytes 6000000 | tf_op jit(solution)/shard_map/attend/pallas_call | solution.py:184
  105.3 11.1 %attend.3 = (bf16[1024,256]{1,0:T(8,128)(2,1)}, bf16[4,1024,128]{2,1,0:T(8,128)(2,1)}) custom-call(s32[3]{0:T(128)} %pad_add_fusion.meta_ref, bf16[1024,768]{1,0:T(8,128)(2,1)} %get-tuple-element.87.q_ref, bf16[1024,768]{1,0:T(8,128)(2,1)} %get-tuple-element.88.k_ref, bf16[1024,768]{1,0:T(8,128)(2,1)} %get-tuple-element.89.v_ref), custom_call_target="tpu_custom_call" | custom-call | flops 4800000000 | bytes 3000000 | tf_op jit(solution)/shard_map/attend/pallas_call | solution.py:184
  119.8 35.1 %mid1.1 = (bf16[1024,768]{1,0:T(8,128)(2,1)}, bf16[1024,768]{1,0:T(8,128)(2,1)}, bf16[1024,3072]{1,0:T(8,128)(2,1)}, bf16[1024,3072]{1,0:T(8,128)(2,1)}, bf16[10...) custom-call(s32[3]{0:T(128)} %pad_add_fusion.meta_ref, ...), custom_call_target="tpu_custom_call" | custom-call | flops 16000000000 | bytes 34000000 | tf_op jit(solution)/shard_map/mid1/pallas_call | solution.py:349
  154.9 25.6 %mid2.1 = (bf16[1024,3072]{1,0:T(8,128)(2,1)}, bf16[1024,768]{1,0:T(8,128)(2,1)}, bf16[1024,768]{1,0:T(8,128)(2,1)}, f32[8,768]{1,0:T(8,128)}, f32[8,3072]{1,0:T(8,128)}) custom-call(s32[3]{0:T(128)} %pad_add_fusion.meta_ref, bf16[1024,768]{1,0:T(8,128)(2,1)} %get-tuple-element.95.db_ref, bf16[1024,3072]{1,0:T(8,128)(2,1)} %get-tuple-element.96.slope_ref, ...), custom_call_target="tpu_custom_call" | custom-call | flops 12000000000 | bytes 30000000 | tf_op jit(solution)/shard_map/mid2/pallas_call | solution.py:405
  183.5 28.0 %attend_back.2 = (bf16[1024,512]{1,0:T(8,128)(2,1)}, bf16[1024,512]{1,0:T(8,128)(2,1)}, bf16[1024,512]{1,0:T(8,128)(2,1)}, f32[8,512]{1,0:T(8,128)}) custom-call(s32[3]{0:T(128)} %pad_add_fusion.meta_ref, bf16[8,1024,128]{2,1,0:T(8,128)(2,1)} %get-tuple-element.100.aug_ref, bf16[1024,768]{1,0:T(8,128)(2,1)} %get-tuple-element.88.k_ref, ...), custom_call_target="tpu_custom_call" | custom-call | flops 13600000000 | bytes 10000000 | tf_op jit(solution)/shard_map/attend_back/pallas_call | solution.py:262
  212.2 15.0 %attend_back.3 = (bf16[1024,256]{1,0:T(8,128)(2,1)}, bf16[1024,256]{1,0:T(8,128)(2,1)}, bf16[1024,256]{1,0:T(8,128)(2,1)}, f32[8,256]{1,0:T(8,128)}) custom-call(s32[3]{0:T(128)} %pad_add_fusion.meta_ref, bf16[4,1024,128]{2,1,0:T(8,128)(2,1)} %get-tuple-element.103.aug_ref, bf16[1024,768]{1,0:T(8,128)(2,1)} %get-tuple-element.88.k_ref, ...), custom_call_target="tpu_custom_call" | custom-call | flops 6800000000 | bytes 5000000 | tf_op jit(solution)/shard_map/attend_back/pallas_call | solution.py:262
  228.9 12.2 %down_grads.1 = (bf16[4,384,768]{2,1,0:T(8,128)(2,1)}, bf16[4,384,768]{2,1,0:T(8,128)(2,1)}) custom-call(s32[3]{0:T(128)} %pad_add_fusion.meta_ref, bf16[1024,3072]{1,0:T(8,128)(2,1)} %get-tuple-element.117.act_ref, bf16[1024,768]{1,0:T(8,128)(2,1)} %get-tuple-element.95.db_ref), custom_call_target="tpu_custom_call" | custom-call | flops 5798205952 | bytes 13000000 | tf_op jit(solution)/shard_map/down_grads/pallas_call | solution.py:495
  241.7 7.4 %pair_grads.3 = (bf16[4,288,512]{2,1,0:T(8,128)(2,1)}, bf16[4,288,512]{2,1,0:T(8,128)(2,1)}) custom-call(s32[3]{0:T(128)} %pad_add_fusion.meta_ref, bf16[1024,768]{1,0:T(8,128)(2,1)} %bitcast.190, bf16[1024,512]{1,0:T(8,128)(2,1)} %get-tuple-element.102.refs_1_, bf16[1024,768]{1,0:T(8,128)(2,1)} %bitcast.191, bf16[1024,512]{1,0:T(8,128)(2,1)} %get-tuple-element.105.refs_3_, ...), custom_call_target="tpu_custom_call" | custom-call | flops 2899102976 | bytes 15000000 | tf_op jit(solution)/shard_map/pair_grads/pallas_call | solution.py:466
  251.7 6.7 %pair_grads.4 = (bf16[4,288,256]{2,1,0:T(8,128)(2,1)}, bf16[4,288,256]{2,1,0:T(8,128)(2,1)}) custom-call(s32[3]{0:T(128)} %pad_add_fusion.meta_ref, bf16[1024,768]{1,0:T(8,128)(2,1)} %bitcast.193, bf16[1024,256]{1,0:T(8,128)(2,1)} %get-tuple-element.104.refs_1_, bf16[1024,768]{1,0:T(8,128)(2,1)} %bitcast.194, bf16[1024,256]{1,0:T(8,128)(2,1)} %get-tuple-element.106.refs_3_, ...), custom_call_target="tpu_custom_call" | custom-call | flops 1449551488 | bytes 15000000 | tf_op jit(solution)/shard_map/pair_grads/pallas_call | solution.py:466
  260.7 14.0 %pair_grads.5 = (bf16[4,480,768]{2,1,0:T(8,128)(2,1)}, bf16[4,480,768]{2,1,0:T(8,128)(2,1)}) custom-call(s32[3]{0:T(128)} %pad_add_fusion.meta_ref, bf16[1024,768]{1,0:T(8,128)(2,1)} %get-tuple-element.113.refs_0_, bf16[1024,3072]{1,0:T(8,128)(2,1)} %get-tuple-element.114.refs_1_, bf16[1024,768]{1,0:T(8,128)(2,1)} %pad_maximum_fusion.3.refs_2_, ...), custom_call_target="tpu_custom_call" | custom-call | flops 7247757312 | bytes 15000000 | tf_op jit(solution)/shard_map/pair_grads/pallas_call | solution.py:466
  287.1 9.7 %input_grad.1 = bf16[1024,768]{1,0:T(8,128)(2,1)} custom-call(s32[3]{0:T(128)} %pad_add_fusion.meta_ref, bf16[1024,768]{1,0:T(8,128)(2,1)} %get-tuple-element.99.da_ref.refs_3_, bf16[1024,768]{1,0:T(8,128)(2,1)} %pad_maximum_fusion.dq_ref, bf16[1024,768]{1,0:T(8,128)(2,1)} %pad_maximum_fusion.1.dk_ref, bf16[1024,768]{1,0:T(8,128)(2,1)} %pad_maximum_fusion.2.dv_ref, ...), custom_call_target="tpu_custom_call" | custom-call | flops 3623878656 | bytes 13000000 | tf_op jit(solution)/shard_map/input_grad/pallas_call | solution.py:121
  340.0 4.1 collective-permute-done.33
  351.3 4.4 collective-permute-done.38
  363.9 10.3 %collective-permute-done.67 = bf16[2,192,768]{2,1,0:T(8,128)(2,1)S(1)} collective-permute-done((bf16[2,192,768]{2,1,0:T(8,128)(2,1)S(1)}, bf16[2,192,768]{2,1,0:T(8,128)(2,1)S(1)}, u32[]{:S(2)}, u32[]{:S(2)}) %collective-permute-start.67) | collective-permute-done | bytes 589856 | tf_op jit(solution)/shard_map/ppermute | solution.py:516
  392.1 8.7 %collective-permute-done.70 = bf16[96,768]{1,0:T(8,128)(2,1)S(1)} collective-permute-done((bf16[96,768]{1,0:T(8,128)(2,1)S(1)}, bf16[96,768]{1,0:T(8,128)(2,1)S(1)}, u32[]{:S(2)}, u32[]{:S(2)}) %collective-permute-start.70) | collective-permute-done | bytes 147488 | tf_op jit(solution)/shard_map/ppermute | solution.py:516
  400.9 7.7 %collective-permute-start.72 = (bf16[96,768]{1,0:T(8,128)(2,1)S(1)}, bf16[96,768]{1,0:T(8,128)(2,1)S(1)}, u32[]{:S(2)}, u32[]{:S(2)}) collective-permute-start(bf16[96,768]{1,0:T(8,128)(2,1)S(1)} %get-tuple-element.126), channel_id=1, source_target_pairs={{0,8},{8,0},{16,24},{24,16},{1,9},{9,1},{17,25},{25,17},{2,10},{10... | collective-permute-start | bytes 442376 | tf_op jit(solution)/shard_map/ppermute | solution.py:516
  418.8 3.2 collective-permute-start.60
  426.7 8.7 %collective-permute-done.59 = bf16[120,768]{1,0:T(8,128)(2,1)S(1)} collective-permute-done((bf16[120,768]{1,0:T(8,128)(2,1)S(1)}, bf16[120,768]{1,0:T(8,128)(2,1)S(1)}, u32[]{:S(2)}, u32[]{:S(2)}) %collective-permute-start.59) | collective-permute-done | bytes 184352 | tf_op jit(solution)/shard_map/ppermute | solution.py:516
  441.7 6.8 %collective-permute-done.62 = bf16[120,768]{1,0:T(8,128)(2,1)S(1)} collective-permute-done((bf16[120,768]{1,0:T(8,128)(2,1)S(1)}, bf16[120,768]{1,0:T(8,128)(2,1)S(1)}, u32[]{:S(2)}, u32[]{:S(2)}) %collective-permute-start.62) | collective-permute-done | bytes 184352 | tf_op jit(solution)/shard_map/ppermute | solution.py:516
  (370 shorter events, 159.8 us)
Async XLA Ops:
  29.1 37.7 %collective-permute-start.24 = (bf16[432,768]{1,0:T(8,128)(2,1)S(1)}, bf16[432,768]{1,0:T(8,128)(2,1)}, u32[]{:S(2)}, u32[]{:S(2)}) collective-permute-start(bf16[432,768]{1,0:T(8,128)(2,1)S(1)} %get-tuple-element.93.refs_1_), channel_id=1, source_target_pairs={{0,4},{1,5},{2,6},{3,7},{4,0},{5,1},{6,2},{7,3},{8,12},{9,13},{10,... | collective-permute-start | bytes 1990664 | tf_op jit(solution)/shard_map/ppermute | solution.py:516
  30.8 36.4 %collective-permute-start.20 = (bf16[432,768]{1,0:T(8,128)(2,1)S(1)}, bf16[432,768]{1,0:T(8,128)(2,1)}, u32[]{:S(2)}, u32[]{:S(2)}) collective-permute-start(bf16[432,768]{1,0:T(8,128)(2,1)S(1)} %get-tuple-element.93.refs_1_), channel_id=1, source_target_pairs={{0,2},{1,3},{2,0},{3,1},{4,6},{5,7},{6,4},{7,5},{8,10},{9,11},{10,... | collective-permute-start | bytes 1990664 | tf_op jit(solution)/shard_map/ppermute | solution.py:516
  32.3 34.0 %collective-permute-start.19 = (bf16[432,768]{1,0:T(8,128)(2,1)S(1)}, bf16[432,768]{1,0:T(8,128)(2,1)S(1)}, u32[]{:S(2)}, u32[]{:S(2)}) collective-permute-start(bf16[432,768]{1,0:T(8,128)(2,1)S(1)} %get-tuple-element.92.refs_0_), channel_id=1, source_target_pairs={{0,2},{1,3},{2,0},{3,1},{4,6},{5,7},{6,4},{7,5},{8,10},{9,11},{10,... | collective-permute-start | bytes 1990664 | tf_op jit(solution)/shard_map/ppermute | solution.py:516
  32.9 34.3 %collective-permute-start.23 = (bf16[432,768]{1,0:T(8,128)(2,1)S(1)}, bf16[432,768]{1,0:T(8,128)(2,1)S(1)}, u32[]{:S(2)}, u32[]{:S(2)}) collective-permute-start(bf16[432,768]{1,0:T(8,128)(2,1)S(1)} %get-tuple-element.92.refs_0_), channel_id=1, source_target_pairs={{0,4},{1,5},{2,6},{3,7},{4,0},{5,1},{6,2},{7,3},{8,12},{9,13},{10,... | collective-permute-start | bytes 1990664 | tf_op jit(solution)/shard_map/ppermute | solution.py:516
  33.3 28.6 %collective-permute-start.1 = (bf16[2,12,96]{2,1,0:T(8,128)(2,1)S(1)}, bf16[2,12,96]{2,1,0:T(8,128)(2,1)S(1)}, u32[]{:S(2)}, u32[]{:S(2)}) collective-permute-start(bf16[2,12,96]{2,1,0:T(8,128)(2,1)S(1)} %pad_maximum_fusion.24), channel_id=1, source_target_pairs={{0,2},{1,3},{2,0},{3,1},{4,6},{5,7},{6,4},{7,5},{8,10},{9,11},{10,... | collective-permute-start | bytes 13832 | tf_op jit(solution)/shard_map/ppermute | solution.py:516
  66.9 17.0 %collective-permute-start.27 = (bf16[432,768]{1,0:T(8,128)(2,1)S(1)}, bf16[432,768]{1,0:T(8,128)(2,1)}, u32[]{:S(2)}, u32[]{:S(2)}) collective-permute-start(bf16[432,768]{1,0:T(8,128)(2,1)S(1)} %collective-permute-done.19.refs_4_), channel_id=1, source_target_pairs={{0,4},{1,5},{2,6},{3,7},{4,0},{5,1},{6,2},{7,3},{8,12},{9,13},{10,... | collective-permute-start | bytes 1990664 | tf_op jit(solution)/shard_map/ppermute | solution.py:516
  67.2 17.7 %collective-permute-start.21 = (bf16[432,768]{1,0:T(8,128)(2,1)S(1)}, bf16[432,768]{1,0:T(8,128)(2,1)}, u32[]{:S(2)}, u32[]{:S(2)}) collective-permute-start(bf16[432,768]{1,0:T(8,128)(2,1)S(1)} %collective-permute-done.19.refs_4_), channel_id=1, source_target_pairs={{0,1},{1,0},{2,3},{3,2},{4,5},{5,4},{6,7},{7,6},{8,9},{9,8},{10,11... | collective-permute-start | bytes 1990664 | tf_op jit(solution)/shard_map/ppermute | solution.py:516
  67.2 17.6 %collective-permute-start.28 = (bf16[432,768]{1,0:T(8,128)(2,1)}, bf16[432,768]{1,0:T(8,128)(2,1)}, u32[]{:S(2)}, u32[]{:S(2)}) collective-permute-start(bf16[432,768]{1,0:T(8,128)(2,1)} %collective-permute-done.24.refs_9_), channel_id=1, source_target_pairs={{0,2},{1,3},{2,0},{3,1},{4,6},{5,7},{6,4},{7,5},{8,10},{9,11},{10,... | collective-permute-start | bytes 1990664 | tf_op jit(solution)/shard_map/ppermute | solution.py:516
  78.7 40.0 %collective-permute-start.26 = (bf16[432,768]{1,0:T(8,128)(2,1)}, bf16[432,768]{1,0:T(8,128)(2,1)S(1)}, u32[]{:S(2)}, u32[]{:S(2)}) collective-permute-start(bf16[432,768]{1,0:T(8,128)(2,1)} %collective-permute-done.24.refs_9_), channel_id=1, source_target_pairs={{0,1},{1,0},{2,3},{3,2},{4,5},{5,4},{6,7},{7,6},{8,9},{9,8},{10,11... | collective-permute-start | bytes 1990664 | tf_op jit(solution)/shard_map/ppermute | solution.py:516
  79.0 39.8 %collective-permute-start.22 = (bf16[432,768]{1,0:T(8,128)(2,1)}, bf16[432,768]{1,0:T(8,128)(2,1)S(1)}, u32[]{:S(2)}, u32[]{:S(2)}) collective-permute-start(bf16[432,768]{1,0:T(8,128)(2,1)} %collective-permute-done.20.refs_5_), channel_id=1, source_target_pairs={{0,1},{1,0},{2,3},{3,2},{4,5},{5,4},{6,7},{7,6},{8,9},{9,8},{10,11... | collective-permute-start | bytes 1990664 | tf_op jit(solution)/shard_map/ppermute | solution.py:516
  83.9 34.9 %collective-permute-start.25 = (bf16[432,768]{1,0:T(8,128)(2,1)}, bf16[432,768]{1,0:T(8,128)(2,1)}, u32[]{:S(2)}, u32[]{:S(2)}) collective-permute-start(bf16[432,768]{1,0:T(8,128)(2,1)} %copy-done.34), channel_id=1, source_target_pairs={{0,1},{1,0},{2,3},{3,2},{4,5},{5,4},{6,7},{7,6},{8,9},{9,8},{10,11... | collective-permute-start | bytes 1990664 | tf_op jit(solution)/shard_map/ppermute | solution.py:516
  84.9 33.9 %collective-permute-start.29 = (bf16[432,768]{1,0:T(8,128)(2,1)}, bf16[432,768]{1,0:T(8,128)(2,1)}, u32[]{:S(2)}, u32[]{:S(2)}) collective-permute-start(bf16[432,768]{1,0:T(8,128)(2,1)} %collective-permute-done.27.refs_12_), channel_id=1, source_target_pairs={{0,1},{1,0},{2,3},{3,2},{4,5},{5,4},{6,7},{7,6},{8,9},{9,8},{10,11... | collective-permute-start | bytes 1990664 | tf_op jit(solution)/shard_map/ppermute | solution.py:516
  84.9 33.9 %collective-permute-start.30 = (bf16[432,768]{1,0:T(8,128)(2,1)}, bf16[432,768]{1,0:T(8,128)(2,1)}, u32[]{:S(2)}, u32[]{:S(2)}) collective-permute-start(bf16[432,768]{1,0:T(8,128)(2,1)} %collective-permute-done.28.refs_13_), channel_id=1, source_target_pairs={{0,1},{1,0},{2,3},{3,2},{4,5},{5,4},{6,7},{7,6},{8,9},{9,8},{10,11... | collective-permute-start | bytes 1990664 | tf_op jit(solution)/shard_map/ppermute | solution.py:516
  228.9 30.1 %collective-permute-start.75 = (f32[12,768]{1,0:T(8,128)S(1)}, f32[12,768]{1,0:T(8,128)S(1)}, u32[]{:S(2)}, u32[]{:S(2)}) collective-permute-start(f32[12,768]{1,0:T(8,128)S(1)} %concatenate.89), channel_id=1, source_target_pairs={{0,1},{1,0},{2,3},{3,2},{4,5},{5,4},{6,7},{7,6},{8,9},{9,8},{10,11... | collective-permute-start | bytes 110600 | tf_op jit(solution)/shard_map/ppermute | solution.py:516
  241.1 119.1 %collective-permute-start.64 = (bf16[4,384,768]{2,1,0:T(8,128)(2,1)}, bf16[4,384,768]{2,1,0:T(8,128)(2,1)S(1)}, u32[]{:S(2)}, u32[]{:S(2)}) collective-permute-start(bf16[4,384,768]{2,1,0:T(8,128)(2,1)} %get-tuple-element.119), channel_id=1, source_target_pairs={{0,1},{1,0},{2,3},{3,2},{4,5},{5,4},{6,7},{7,6},{8,9},{9,8},{10,11... | collective-permute-start | bytes 7077896 | tf_op jit(solution)/shard_map/ppermute | solution.py:516
  249.1 78.8 %collective-permute-start.31 = (bf16[4,288,512]{2,1,0:T(8,128)(2,1)}, bf16[4,288,512]{2,1,0:T(8,128)(2,1)}, u32[]{:S(2)}, u32[]{:S(2)}) collective-permute-start(bf16[4,288,512]{2,1,0:T(8,128)(2,1)} %get-tuple-element.110), channel_id=1, source_target_pairs={{0,1},{1,0},{2,3},{3,2},{4,5},{5,4},{6,7},{7,6},{8,9},{9,8},{10,11... | collective-permute-start | bytes 3538952 | tf_op jit(solution)/shard_map/ppermute | solution.py:516
  258.4 41.6 %collective-permute-start.42 = (bf16[4,288,256]{2,1,0:T(8,128)(2,1)}, bf16[4,288,256]{2,1,0:T(8,128)(2,1)S(1)}, u32[]{:S(2)}, u32[]{:S(2)}) collective-permute-start(bf16[4,288,256]{2,1,0:T(8,128)(2,1)} %get-tuple-element.112), channel_id=1, source_target_pairs={{0,1},{1,0},{2,3},{3,2},{4,5},{5,4},{6,7},{7,6},{8,9},{9,8},{10,11... | collective-permute-start | bytes 1769480 | tf_op jit(solution)/shard_map/ppermute | solution.py:516
  258.9 15.8 %collective-permute-start.76 = (f32[12,768]{1,0:T(8,128)S(1)}, f32[12,768]{1,0:T(8,128)}, u32[]{:S(2)}, u32[]{:S(2)}) collective-permute-start(f32[12,768]{1,0:T(8,128)S(1)} %add.446), channel_id=1, source_target_pairs={{0,2},{1,3},{2,0},{3,1},{4,6},{5,7},{6,4},{7,5},{8,10},{9,11},{10,... | collective-permute-start | bytes 110600 | tf_op jit(solution)/shard_map/ppermute | solution.py:516
  322.9 55.2 %collective-permute-start.53 = (bf16[4,480,768]{2,1,0:T(8,128)(2,1)}, bf16[4,480,768]{2,1,0:T(8,128)(2,1)S(1)}, u32[]{:S(2)}, u32[]{:S(2)}) collective-permute-start(bf16[4,480,768]{2,1,0:T(8,128)(2,1)} %get-tuple-element.116), channel_id=1, source_target_pairs={{0,1},{1,0},{2,3},{3,2},{4,5},{5,4},{6,7},{7,6},{8,9},{9,8},{10,11... | collective-permute-start | bytes 8847368 | tf_op jit(solution)/shard_map/ppermute | solution.py:516
  378.6 30.0 %collective-permute-start.56 = (bf16[2,240,768]{2,1,0:T(8,128)(2,1)S(1)}, bf16[2,240,768]{2,1,0:T(8,128)(2,1)S(1)}, u32[]{:S(2)}, u32[]{:S(2)}) collective-permute-start(bf16[2,240,768]{2,1,0:T(8,128)(2,1)S(1)} %pad_maximum_fusion.6), channel_id=1, source_target_pairs={{0,4},{1,5},{2,6},{3,7},{4,0},{5,1},{6,2},{7,3},{8,12},{9,13},{10,... | collective-permute-start | bytes 2211848 | tf_op jit(solution)/shard_map/ppermute | solution.py:516
  380.7 27.9 %collective-permute-start.54 = (bf16[2,240,768]{2,1,0:T(8,128)(2,1)S(1)}, bf16[2,240,768]{2,1,0:T(8,128)(2,1)S(1)}, u32[]{:S(2)}, u32[]{:S(2)}) collective-permute-start(bf16[2,240,768]{2,1,0:T(8,128)(2,1)S(1)} %pad_maximum_fusion.5), channel_id=1, source_target_pairs={{0,2},{1,3},{2,0},{3,1},{4,6},{5,7},{6,4},{7,5},{8,10},{9,11},{10,... | collective-permute-start | bytes 2211848 | tf_op jit(solution)/shard_map/ppermute | solution.py:516
  411.0 27.2 %collective-permute-start.74 = (bf16[96,768]{1,0:T(8,128)(2,1)S(1)}, bf16[96,768]{1,0:T(8,128)(2,1)S(1)}, u32[]{:S(2)}, u32[]{:S(2)}) collective-permute-start(bf16[96,768]{1,0:T(8,128)(2,1)S(1)} %get-tuple-element.126), channel_id=1, source_target_pairs={{0,24},{8,16},{16,8},{24,0},{1,25},{9,17},{17,9},{25,1},{2,26},{10... | collective-permute-start | bytes 442376 | tf_op jit(solution)/shard_map/ppermute | solution.py:516
  417.6 17.7 %collective-permute-start.59 = (bf16[120,768]{1,0:T(8,128)(2,1)S(1)}, bf16[120,768]{1,0:T(8,128)(2,1)S(1)}, u32[]{:S(2)}, u32[]{:S(2)}) collective-permute-start(bf16[120,768]{1,0:T(8,128)(2,1)S(1)} %get-tuple-element.172), channel_id=1, source_target_pairs={{0,16},{8,24},{16,0},{24,8},{1,17},{9,25},{17,1},{25,9},{2,18},{10... | collective-permute-start | bytes 552968 | tf_op jit(solution)/shard_map/ppermute | solution.py:516
  418.8 16.5 %collective-permute-start.60 = (bf16[120,768]{1,0:T(8,128)(2,1)S(1)}, bf16[120,768]{1,0:T(8,128)(2,1)S(1)}, u32[]{:S(2)}, u32[]{:S(2)}) collective-permute-start(bf16[120,768]{1,0:T(8,128)(2,1)S(1)} %get-tuple-element.171), channel_id=1, source_target_pairs={{0,24},{8,16},{16,8},{24,0},{1,25},{9,17},{17,9},{25,1},{2,26},{10... | collective-permute-start | bytes 552968 | tf_op jit(solution)/shard_map/ppermute | solution.py:516
  (104 other events, 919.4 us)

commit v3 on v2

--- a/solution.py
+++ b/solution.py
@@ -134,7 +134,8 @@
     return (lane < 64) if head == 0 else (lane >= 64)
 
 
-def attend_kernel(meta_ref, q_ref, k_ref, v_ref, ctx_ref, aug_ref, *, qb):
+def attend_kernel(meta_ref, q_ref, k_ref, v_ref, *refs, qb):
+    ctx_ref, aug_ref = refs[-2:]
     length = meta_ref[0]
     lane = lax.broadcasted_iota(jnp.int32, (LEN, 128), 1)
     row = lax.broadcasted_iota(jnp.int32, (LEN, 128), 0)
@@ -179,26 +180,22 @@
         ctx_ref[pl.ds(r0, qb), :] = jnp.where(lane_q < 64, outs[0], outs[1]).astype(BF)
 
 
-def attend(meta, q, k, v, first, count, qb=512):
+def attend(meta, q, k, v, held, first, count, qb=512):
     wide = pl.BlockSpec((LEN, 128), lambda i: (0, i + first))
     return pl.pallas_call(
         functools.partial(attend_kernel, qb=qb),
         grid=(count,),
-        in_specs=[SMEM, wide, wide, wide],
-        out_specs=[
-            pl.BlockSpec((LEN, 128), lambda i: (0, i)),
-            pl.BlockSpec((2, LEN, 128), lambda i: (i, 0, 0)),
-        ],
-        out_shape=[sds(LEN, 128 * count), sds(2 * count, LEN, 128)],
+        in_specs=[SMEM, wide, wide, wide] + [ANY] * len(held),
+        out_specs=[wide, pl.BlockSpec((2, LEN, 128), lambda i: (i + first, 0, 0))],
+        out_shape=[sds(LEN, D), sds(HEADS, LEN, 128)],
+        input_output_aliases={4 + j: j for j in range(len(held))},
         cost_estimate=cost(count * 2.4e9, count * 1.5e6),
         name="attend",
-    )(meta, q, k, v)
-
-
-def attend_back_kernel(
-    meta_ref, aug_ref, k_ref, v_ref, o_ref, do_ref, dq_ref, dk_ref, dv_ref, sums_ref,
-    qa_s, doa_s, dom_s, kt_s, dqt_s, *, kb
-):
+    )(meta, q, k, v, *held)
+
+
+def attend_back_kernel(meta_ref, aug_ref, k_ref, v_ref, o_ref, do_ref, old_ref, *refs, kb):
+    dq_ref, dk_ref, dv_ref, sums_ref, qa_s, doa_s, dom_s, kt_s, dqt_s = refs[-9:]
     length = meta_ref[0]
     one = jnp.ones((), BF)
     zero = jnp.zeros((), BF)
@@ -221,7 +218,7 @@
         qa_s[h] = jnp.where(mine, aug_ref[h], zero)
     kt_s[...] = k_ref[...].astype(F32).T.astype(BF)
     dqt_s[...] = jnp.zeros_like(dqt_s)
-    sums_ref[...] = jnp.zeros_like(sums_ref)
+    sums_ref[...] = old_ref[...]
     lane_k = lax.broadcasted_iota(jnp.int32, (kb, 128), 1)
 
     @pl.loop(0, LEN // kb)
@@ -255,23 +252,26 @@
     dq_ref[...] = dq.astype(BF)
 
 
-def attend_back(meta, aug, k, v, o, do, first, local, count, kb=512):
+def attend_back(meta, aug, k, v, o, do, sums, held, first, count, kb=512):
     wide = pl.BlockSpec((LEN, 128), lambda i: (0, i + first))
-    near = pl.BlockSpec((LEN, 128), lambda i: (0, i + local))
-    out = pl.BlockSpec((LEN, 128), lambda i: (0, i))
+    tall = pl.BlockSpec((16, 128), lambda i: (0, i + first))
+    aliases = {6: 3}
+    aliases.update({7 + j: j for j in range(len(held))})
     return pl.pallas_call(
         functools.partial(attend_back_kernel, kb=kb),
         grid=(count,),
-        in_specs=[
-            SMEM, pl.BlockSpec((2, LEN, 128), lambda i: (i + local, 0, 0)), wide, wide, near, wide
-        ],
-        out_specs=[out, out, out, pl.BlockSpec((8, 128), lambda i: (0, i))],
-        out_shape=[sds(LEN, 128 * count)] * 3 + [sds(8, 128 * count, dtype=F32)],
+        in_specs=[SMEM, pl.BlockSpec((2, LEN, 128), lambda i: (i + first, 0, 0))]
+        + [wide] * 4
+        + [tall]
+        + [ANY] * len(held),
+        out_specs=[wide, wide, wide, tall],
+        out_shape=[sds(LEN, D)] * 3 + [sds(16, D, dtype=F32)],
         scratch_shapes=[pltpu.VMEM((2, LEN, 128), BF)] * 3
         + [pltpu.VMEM((128, LEN), BF), pltpu.VMEM((128, LEN), F32)],
+        input_output_aliases=aliases,
         cost_estimate=cost(count * 3.4e9, count * 2.5e6),
         name="attend_back",
-    )(meta, aug, k, v, o, do)
+    )(meta, aug, k, v, o, do, sums, *held)
 
 
 def gelu_parts(u):
@@ -300,7 +300,7 @@
     )
 
 
-def mid1_kernel(meta_ref, x_ref, ctxa_ref, ctxb_ref, cot_ref, vec_ref, ub_ref, *refs, count, R):
+def mid1_kernel(meta_ref, x_ref, ctx_ref, cot_ref, vec_ref, ub_ref, *refs, count, R):
     pieces = refs[:count]
     (out_ref, fl_ref, act_ref, slope_ref, n1_ref, inv_ref, db_ref, sums_ref,
      acc_s, w_s, sem) = refs[count:]
@@ -312,8 +312,7 @@
         sums_ref[...] = jnp.zeros_like(sums_ref)
 
     x = x_ref[...].astype(F32)
-    wide = ctxa_ref.shape[1]
-    attended = dot(ctxa_ref[...], w_s[0:wide, :]) + dot(ctxb_ref[...], w_s[wide:D, :])
+    attended = dot(ctx_ref[...], w_s[0:D, :])
     n1, inv1 = norm(x + attended + vec_ref[2:3, :])
     first = n1 * vec_ref[3:4, :] + vec_ref[4:5, :]
     fl_ref[...] = first.astype(BF)
@@ -340,17 +339,17 @@
     up = jnp.where(live, cot_ref[...].astype(F32), 0.0)
     db = norm_back(up * gain, n2, inv2).astype(BF)
     db_ref[...] = db
-    sums_ref[0:1, :] += jnp.sum(up * n2, axis=0, keepdims=True)
-    sums_ref[1:2, :] += jnp.sum(up, axis=0, keepdims=True)
-    sums_ref[2:3, :] += jnp.sum(db.astype(F32), axis=0, keepdims=True)
-
-
-def mid1(meta, x, ctxa, ctxb, cot, vec, ub, pieces, R=256):
+    sums_ref[5:6, :] += jnp.sum(db.astype(F32), axis=0, keepdims=True)
+    sums_ref[6:7, :] += jnp.sum(up * n2, axis=0, keepdims=True)
+    sums_ref[7:8, :] += jnp.sum(up, axis=0, keepdims=True)
+
+
+def mid1(meta, x, ctx, cot, vec, ub, pieces, R=256):
     return pl.pallas_call(
         functools.partial(mid1_kernel, count=len(pieces), R=R),
         grid=(LEN // R,),
         in_specs=[
-            SMEM, rows(R, D), rows(R, ctxa.shape[1]), rows(R, ctxb.shape[1]), rows(R, D),
+            SMEM, rows(R, D), rows(R, D), rows(R, D),
             full(vec.shape), full(ub.shape),
         ]
         + [ANY] * len(pieces),
@@ -367,18 +366,18 @@
         ],
         cost_estimate=cost(16e9, 34e6),
         name="mid1",
-    )(meta, x, ctxa, ctxb, cot, vec, ub, *pieces)
-
-
-def mid2_kernel(meta_ref, db_ref, slope_ref, n1_ref, inv_ref, vec_ref, *refs, count, R):
+    )(meta, x, ctx, cot, vec, ub, *pieces)
+
+
+def mid2_kernel(meta_ref, db_ref, slope_ref, n1_ref, inv_ref, vec_ref, old_ref, *refs, count, R):
     pieces = refs[:count]
-    dh_ref, da_ref, dctx_ref, sums_ref, ups_ref, acc_s, w_s, sem = refs[count:]
+    dh_ref, da_ref, dctx_ref, sums_ref, acc_s, w_s, sem = refs[count:]
 
     @pl.when(pl.program_id(0) == 0)
     def _():
         load_pieces(pieces, MID_PARTS, meta_ref[2], w_s, sem)
-        sums_ref[...] = jnp.zeros_like(sums_ref)
-        ups_ref[...] = jnp.zeros_like(ups_ref)
+        sums_ref[0:8, :] = old_ref[...]
+        sums_ref[8:16, :] = jnp.zeros_like(old_ref)
 
     acc_s[...] = db_ref[...].astype(F32)
 
@@ -388,7 +387,7 @@
         dact = dot(db_ref[...], w_s[pl.ds(DOWN0 + c0, D), :], NT)
         dh = (dact * slope_ref[:, pl.ds(c0, D)].astype(F32)).astype(BF)
         dh_ref[:, pl.ds(c0, D)] = dh
-        ups_ref[0:1, pl.ds(c0, D)] += jnp.sum(dh.astype(F32), axis=0, keepdims=True)
+        sums_ref[pl.ds(8 + c, 1), :] += jnp.sum(dh.astype(F32), axis=0, keepdims=True)
         acc_s[...] += dot(dh, w_s[pl.ds(UP0 + c0, D), :], NT)
 
     df = acc_s[...]
@@ -396,30 +395,29 @@
     da = norm_back(df * vec_ref[3:4, :], n1, inv_ref[:, 0:1]).astype(BF)
     da_ref[...] = da
     dctx_ref[...] = dot(da, w_s[0:D, :], NT).astype(BF)
-    sums_ref[0:1, :] += jnp.sum(df * n1, axis=0, keepdims=True)
-    sums_ref[1:2, :] += jnp.sum(df, axis=0, keepdims=True)
     sums_ref[2:3, :] += jnp.sum(da.astype(F32), axis=0, keepdims=True)
-
-
-def mid2(meta, db, slope, n1, inv, vec, pieces, R=256):
+    sums_ref[3:4, :] += jnp.sum(df * n1, axis=0, keepdims=True)
+    sums_ref[4:5, :] += jnp.sum(df, axis=0, keepdims=True)
+
+
+def mid2(meta, db, slope, n1, inv, vec, sums, pieces, R=256):
     return pl.pallas_call(
         functools.partial(mid2_kernel, count=len(pieces), R=R),
         grid=(LEN // R,),
-        in_specs=[SMEM, rows(R, D), rows(R, FF), rows(R, D), rows(R, 128), full(vec.shape)]
+        in_specs=[SMEM, rows(R, D), rows(R, FF), rows(R, D), rows(R, 128), full(vec.shape), full((8, D))]
         + [ANY] * len(pieces),
         out_specs=[
-            rows(R, FF), rows(R, D), rows(R, D),
-            pl.BlockSpec((8, D), lambda i: (0, 0)), pl.BlockSpec((8, FF), lambda i: (0, 0)),
+            rows(R, FF), rows(R, D), rows(R, D), pl.BlockSpec((16, D), lambda i: (0, 0)),
         ],
         out_shape=[
-            sds(LEN, FF), sds(LEN, D), sds(LEN, D), sds(8, D, dtype=F32), sds(8, FF, dtype=F32)
+            sds(LEN, FF), sds(LEN, D), sds(LEN, D), sds(16, D, dtype=F32)
         ],
         scratch_shapes=[
             pltpu.VMEM((R, D), F32), pltpu.VMEM((MID_ROWS, D), BF), pltpu.SemaphoreType.DMA
         ],
         cost_estimate=cost(12e9, 30e6),
         name="mid2",
-    )(meta, db, slope, n1, inv, vec, *pieces)
+    )(meta, db, slope, n1, inv, vec, sums, *pieces)
 
 
 def slabs_out(scr, me, send_ref, keep_ref, row0, sem):
@@ -458,14 +456,24 @@
                 copy.wait()
 
 
-def pair_grads(meta, pairs, width):
-    groups = tuple(right.shape[1] // width for _, right in pairs)
+def pair_grads(meta, pairs, width, column=None):
+    groups = tuple(1 if column is not None else r.shape[1] // width for _, r in pairs)
     total = sum(groups)
     flat = [a for pair in pairs for a in pair]
-    vm = pl.BlockSpec(memory_space=pltpu.VMEM)
+    left_spec = full((LEN, D))
+    specs = []
+    for _, right in pairs:
+        specs.append(left_spec)
+        if column is None:
+            specs.append(full(right.shape))
+        else:
+            specs.append(
+                pl.BlockSpec((LEN, width), lambda i: (0, column), pipeline_mode=pl.Buffered(1))
+            )
     return pl.pallas_call(
         functools.partial(pairs_kernel, groups=groups, total=total),
-        in_specs=[SMEM] + [vm] * len(flat),
+        grid=(1,),
+        in_specs=[SMEM] + specs,
         out_specs=[ANY, ANY],
         out_shape=[sds(4, total * SROWS, width)] * 2,
         scratch_shapes=[pltpu.VMEM((2, D, width), BF), pltpu.SemaphoreType.DMA((2, SLABS))],
@@ -474,40 +482,25 @@
     )(meta, *flat)
 
 
-def down_kernel(meta_ref, act_ref, db_ref, send_ref, keep_ref):
-    i = pl.program_id(0)
-    value = dot(act_ref[...], db_ref[...], TN).astype(BF)
-
-    @pl.when(i < 4)
-    def _():
-        send_ref[0] = value
-
-    @pl.when(i >= 4)
-    def _():
-        keep_ref[0] = value
-
-
-def down_grads(meta, act, db):
-    def owner(i, m):
-        k = jnp.where(i < 4, 2 * i + 1, 2 * (i - 4))
-        return m[2] ^ k
-
+def down_kernel(meta_ref, act_ref, db_ref, out_ref):
+    out_ref[0] = dot(act_ref[...], db_ref[...], TN).astype(BF)
+
+
+def down_grads(meta, act, db, parity):
+    wide = FF // SLABS
     return pl.pallas_call(
         down_kernel,
         grid_spec=pltpu.PrefetchScalarGridSpec(
             num_scalar_prefetch=1,
-            grid=(SLABS,),
+            grid=(4,),
             in_specs=[
-                pl.BlockSpec((LEN, FF // SLABS), lambda i, m: (0, owner(i, m))),
+                pl.BlockSpec((LEN, wide), lambda i, m: (0, m[2] ^ (2 * i + parity))),
                 pl.BlockSpec((LEN, D), lambda i, m: (0, 0), pipeline_mode=pl.Buffered(1)),
             ],
-            out_specs=[
-                pl.BlockSpec((1, FF // SLABS, D), lambda i, m: (jnp.minimum(i, 3), 0, 0)),
-                pl.BlockSpec((1, FF // SLABS, D), lambda i, m: (jnp.maximum(i - 4, 0), 0, 0)),
-            ],
+            out_specs=pl.BlockSpec((1, wide, D), lambda i, m: (i, 0, 0)),
         ),
-        out_shape=[sds(4, FF // SLABS, D)] * 2,
-        cost_estimate=cost(2 * LEN * FF * D * 1.2, 13e6),
+        out_shape=sds(4, wide, D),
+        cost_estimate=cost(LEN * FF * D * 1.2, 7e6),
         name="down_grads",
     )(meta, act, db)
 
@@ -516,55 +509,91 @@
     return lax.ppermute(value, axis, [(i, i ^ bit) for i in range(size)])
 
 
-def gather_halves(halves):
-    pieces = [None] * 16
-    held = [{0: halves[0]}, {0: halves[1]}]
-    for stage in range(3):
-        for h, order in enumerate(((2, 4, 1), (4, 2, 1))):
-            bit = order[stage]
-            held[h].update({k ^ bit: swap(v, "shard", bit, 8) for k, v in list(held[h].items())})
-    for h in range(2):
-        for k, v in held[h].items():
-            pieces[2 * k + h] = v
-    return pieces
+def gather_begin(halves):
+    return [{0: halves[0]}, {0: halves[1]}]
+
+
+def gather_stage(held, stage):
+    for h, (near, far) in enumerate(((2, 4), (4, 2))):
+        mine = held[h]
+        if stage < 2:
+            bit = (near, far)[stage]
+            mine.update({k ^ bit: swap(mine[k], "shard", bit, 8) for k in list(mine) if k % 2 == 0})
+        fresh = [k for k in mine if k % 2 == 0 and k ^ 1 not in mine]
+        fresh = [k for k in fresh if stage == 2 or not k & (near, far)[stage]]
+        mine.update({k ^ 1: swap(mine[k], "shard", 1, 8) for k in fresh})
+    return held
+
+
+def gathered(held):
+    return [held[h][k] for k in range(8) for h in range(2)]
 
 
 def add(*terms):
     return sum(t.astype(F32) for t in terms).astype(BF)
 
 
-def reduce_slabs(send, keep):
-    got = swap(send, "shard", 1, 8)
-    half = send.shape[1] // 2
-    ends = []
-    for cut, first, second, out, stay in (
-        (slice(0, half), 2, 4, (1, 3), (0, 2)),
-        (slice(half, None), 4, 2, (2, 3), (0, 1)),
-    ):
-        away = [add(keep[p, cut], got[p, cut]) for p in out]
-        back = swap(jnp.stack(away), "shard", first, 8)
-        far = add(keep[stay[1], cut], got[stay[1], cut], back[1])
-        last = swap(far, "shard", second, 8)
-        ends.append(add(keep[0, cut], got[0, cut], back[0], last))
-    return jnp.concatenate(ends)
-
-
-def reduce_rep(value, place):
-    quarter = value.shape[0] // 4
-    parts = value.reshape(4, quarter, value.shape[1])
-    mine = lax.dynamic_index_in_dim(parts, place, 0, False)
-    terms = [mine]
-    for k in (1, 2, 3):
-        part = lax.dynamic_index_in_dim(parts, place ^ k, 0, False)
-        terms.append(swap(part, "rep", k, 4))
-    total = add(*terms)
-    out = jnp.zeros(parts.shape, F32)
-    out = lax.dynamic_update_index_in_dim(out, total.astype(F32), place, 0)
-    for k in (1, 2, 3):
-        out = lax.dynamic_update_index_in_dim(
-            out, swap(total, "rep", k, 4).astype(F32), place ^ k, 0
+class Reduction:
+    def __init__(self, send, keep, place):
+        self.keep, self.place, self.stage = keep, place, 0
+        self.got = swap(send, "shard", 1, 8)
+        self.half = send.shape[1] // 2
+        self.cuts = (
+            (slice(0, self.half), 2, 4, (1, 3), (0, 2)),
+            (slice(self.half, None), 4, 2, (2, 3), (0, 1)),
         )
-    return out.reshape(value.shape)
+
+    def step(self):
+        self.stage += 1
+        return (self.near, self.far, self.across, self.share)[self.stage - 1]()
+
+    def near(self):
+        sent = []
+        self.back = []
+        for cut, first, _, out, _ in self.cuts:
+            away = jnp.stack([add(self.keep[p, cut], self.got[p, cut]) for p in out])
+            sent.append(away)
+            self.back.append(swap(away, "shard", first, 8))
+        return sent
+
+    def far(self):
+        sent = []
+        self.last = []
+        for (cut, _, second, _, stay), back in zip(self.cuts, self.back):
+            away = add(self.keep[stay[1], cut], self.got[stay[1], cut], back[1])
+            sent.append(away)
+            self.last.append(swap(away, "shard", second, 8))
+        return sent
+
+    def across(self):
+        ends = [
+            add(self.keep[0, cut[0]], self.got[0, cut[0]], back[0], last)
+            for cut, back, last in zip(self.cuts, self.back, self.last)
+        ]
+        value = jnp.concatenate(ends)
+        self.shape = value.shape
+        parts = value.reshape(4, value.shape[0] // 4, value.shape[1])
+        own, *sent = [
+            lax.dynamic_index_in_dim(parts, self.place ^ k, 0, False) for k in range(4)
+        ]
+        self.terms = [own] + [swap(p, "rep", k, 4) for k, p in zip((1, 2, 3), sent)]
+        return [own] + sent
+
+    def share(self):
+        self.total = add(*self.terms)
+        self.others = [swap(self.total, "rep", k, 4) for k in (1, 2, 3)]
+        return [self.total]
+
+    def result(self):
+        quarter = self.shape[0] // 4
+        out = jnp.zeros((4, quarter, self.shape[1]), F32)
+        for k, part in enumerate([self.total] + self.others):
+            out = lax.dynamic_update_index_in_dim(out, part.astype(F32), self.place ^ k, 0)
+        return out.reshape(self.shape)
+
+
+def after(meta, *values):
+    return lax.optimization_barrier((meta,) + values)[0]
 
 
 def whole_slabs(send, keep):
@@ -600,18 +629,19 @@
         every = jnp.take(held, jnp.arange(8, dtype=jnp.int32) ^ position, axis=0)
         ups = [wu[:, D * j : D * (j + 1)] for j in range(4)]
         cuts = (slice(0, 48), slice(48, 96))
-        near = gather_halves(
-            [jnp.concatenate([m[c] for m in (wq, wk, wv)]) for c in cuts]
-        )
-        down_cuts = (slice(0, 192), slice(192, 384))
+        near = gather_begin([jnp.concatenate([m[c] for m in (wq, wk, wv)]) for c in cuts])
+        gather_stage(near, 0)
+        gather_stage(near, 1)
         far_halves = [
             jnp.concatenate([m[c] for m in [wo] + ups] + [wd[c2]])
-            for c, c2 in zip(cuts, down_cuts)
+            for c, c2 in zip(cuts, (slice(0, 192), slice(192, 384)))
         ]
-        far_halves[0], far_halves[1], near = lax.optimization_barrier(
-            (far_halves[0], far_halves[1], near)
+        far = gather_begin(
+            lax.optimization_barrier(tuple(far_halves) + (near[0][6], near[1][6], held))[:2]
         )
-        far = gather_halves(far_halves)
+        gather_stage(near, 2)
+        near = gathered(near)
+        gather_stage(far, 0)
     else:
         every = lax.all_gather(small, "shard", axis=0)
         whole = [lax.all_gather(m, "shard", axis=0, tiled=True) for m in matrices]
@@ -627,29 +657,50 @@
     ub = jnp.broadcast_to(ub, (8, FF))
 
     q, k, v = qkv(meta, x, vec, near)
-    ctxa, auga = attend(meta, q, k, v, 0, 4)
-    ctxb, augb = attend(meta, q, k, v, 4, 2)
-    output, first, act, slope, n1, inv, db, sums1 = mid1(meta, x, ctxa, ctxb, cot, vec, ub, far)
-    down = down_grads(meta, act, db)
-    dh, da, dctx, sums2, sums_up = mid2(meta, db, slope, n1, inv, vec, far)
-    ctx = jnp.concatenate([ctxa, ctxb], axis=1)
-    upout = pair_grads(meta, ((first, dh), (ctx, da)), D)
-    dqa, dka, dva, sums_a = attend_back(meta, auga, k, v, ctxa, dctx, 0, 0, 4)
-    qkva = pair_grads(meta, ((x, dqa), (x, dka), (x, dva)), 512)
-    dqb, dkb, dvb, sums_b = attend_back(meta, augb, k, v, ctxb, dctx, 4, 0, 2)
-    qkvb = pair_grads(meta, ((x, dqb), (x, dkb), (x, dvb)), 256)
-    dq, dk, dv = (
-        jnp.concatenate(p, axis=1) for p in ((dqa, dqb), (dka, dkb), (dva, dvb))
-    )
-    grad_x = input_grad(meta, da, dq, dk, dv, cot, near)
-
-    sums_ab = jnp.concatenate([sums_a[:2], sums_b[:2]], axis=1)
-    sums = jnp.concatenate(
-        [
-            sums_ab, sums2[2:3], sums2[0:2], sums1[2:3], sums1[0:2],
-            sums_up[0].reshape(4, D),
-        ]
-    )
+    heads = attend(meta, q, k, v, (), 0, 2)
+    if permuted:
+        gather_stage(far, 1)
+        m = after(meta, heads[0], far[0][2], far[1][4])
+    else:
+        m = after(meta, heads[0])
+    heads = attend(m, q, k, v, heads, 2, 4)
+    ctx, aug = heads
+    if permuted:
+        gather_stage(far, 2)
+        far = gathered(far)
+    output, first, act, slope, n1, inv, db, sums = mid1(meta, x, ctx, cot, vec, ub, far)
+    jobs = []
+
+    def begin(send, keep):
+        if permuted:
+            jobs.append(Reduction(send, keep, place))
+
+    def step(index):
+        return tuple(jobs[index].step()) if permuted else ()
+
+    d_send = down_grads(meta, act, db, 1)
+    d_keep = down_grads(after(meta, d_send), act, db, 0)
+    begin(d_send, d_keep)
+    m = after(meta, d_keep, *step(0))
+    dh, da, dctx, sums = mid2(m, db, slope, n1, inv, vec, sums, far)
+    m = after(meta, dctx, *step(0))
+    u_send, u_keep = pair_grads(m, ((first, dh), (ctx, da)), D)
+    begin(u_send, u_keep)
+    m = after(meta, u_keep, *step(0))
+    *grads, sums = attend_back(m, aug, k, v, ctx, dctx, sums, (), 0, 2)
+    m = after(meta, sums, *step(1), *step(0))
+    *grads, sums = attend_back(m, aug, k, v, ctx, dctx, sums, grads, 2, 2)
+    m = after(meta, sums, *step(1))
+    a_send, a_keep = pair_grads(m, [(x, g) for g in grads], 512, 0)
+    begin(a_send, a_keep)
+    m = after(meta, a_keep)
+    *grads, sums = attend_back(m, aug, k, v, ctx, dctx, sums, grads, 4, 2)
+    m = after(meta, sums, *step(1), *step(2))
+    b_send, b_keep = pair_grads(m, [(x, g) for g in grads], 256, 2)
+    begin(b_send, b_keep)
+    m = after(meta, b_keep, *step(2))
+    grad_x = input_grad(m, da, *grads, cot, near)
+
     if permuted:
         for bit in (1, 2, 4):
             sums = sums + swap(sums, "shard", bit, 8)
@@ -657,18 +708,18 @@
             sums = sums + swap(sums, "rep", bit, 4)
     else:
         sums = lax.psum(sums, ("rep", "shard"))
-    grads_v = [
-        lax.dynamic_slice_in_dim(sums[r], position * width, width) for r in range(8)
-    ]
-    grad_ub = lax.dynamic_slice_in_dim(
-        sums[8:].reshape(FF), position * (FF // n_shard), FF // n_shard
-    )
+    grads_v = lax.dynamic_index_in_dim(sums[:8].reshape(8, n_shard, width), position, 1, False)
+    grad_ub = lax.dynamic_index_in_dim(sums[8:12].reshape(n_shard, FF // n_shard), position, 0, False)
 
     if permuted:
-        grad_down = reduce_rep(reduce_slabs(*down), place)
-        g_uo = reduce_rep(reduce_slabs(*upout), place)
-        g_a = reduce_rep(reduce_slabs(*qkva), place)
-        g_b = reduce_rep(reduce_slabs(*qkvb), place)
+        step(3)
+        step(3)
+        step(2)
+        step(3)
+        step(1)
+        step(2)
+        step(3)
+        grad_down, g_uo, g_a, g_b = (job.result() for job in jobs)
         grad_up = jnp.concatenate([g_uo[96 * j : 96 * (j + 1)] for j in range(4)], axis=1)
         grad_out = g_uo[384:]
         grad_qkv = [
@@ -679,8 +730,10 @@
         def rebuild(slabs, j):
             return slabs[:, SROWS * j : SROWS * (j + 1)].reshape(D, slabs.shape[2])
 
-        grad_down = reduce_any(whole_slabs(*down).reshape(FF, D))
-        g_uo, g_a, g_b = (whole_slabs(*p) for p in (upout, qkva, qkvb))
+        grad_down = reduce_any(whole_slabs(d_send, d_keep).reshape(FF, D))
+        g_uo = whole_slabs(u_send, u_keep)
+        g_a = whole_slabs(a_send, a_keep)
+        g_b = whole_slabs(b_send, b_keep)
         grad_up = reduce_any(jnp.concatenate([rebuild(g_uo, j) for j in range(4)], axis=1))
         grad_out = reduce_any(rebuild(g_uo, 4))
         grad_qkv = [

time: 455 us -> 420 us (0.923)
  waiting for transfers between devices: 123 us -> 83.4 us
  local copies, waits for them, and re-layouts: 19.9 us -> 9.96 us
  starting transfers between devices: 82.8 us -> 88.3 us
  Pallas kernels: 193 us -> 198 us
  other arithmetic: 29.4 us -> 34.1 us
    ppermute x80, waiting for transfers between devices: 123 us -> 83.4 us  [swap(): return lax.ppermute(value, axis, [(i, i ^ bit) for i in range(size)])]
    concatenate x9 -> x4, other arithmetic: 8.7 us -> 0.13 us  [across(): value = jnp.concatenate(ends)]
    convert_element_type x12, other arithmetic: 7.5 us -> 14.9 us  [add(): return sum((t.astype(F32) for t in terms)).astype(BF)]
    ppermute x80, starting transfers between devices: 82.8 us -> 88.3 us  [swap(): return lax.ppermute(value, axis, [(i, i ^ bit) for i in range(size)])]
    dynamic_slice x9 -> x1, local copies, waits for them, and re-layouts: 6 us -> 0.6 us  [body(): lax.dynamic_index_in_dim(sums[8:12].reshape(n_shard, FF // n_shard), posi...]
    slice x9 -> x2, local copies, waits for them, and re-layouts: 5.32 us -> 0.01 us  [the longest x1 0.01 us: body(): sums[:8].reshape(8, n_shard, width)]
    pallas_call x2 -> x3, Pallas kernels: 43 us -> 45.5 us  [attend_back(): pl.pallas_call(functools.partial(attend_back_kernel, kb=kb), grid=(count,...]
    pallas_call x1 -> x2, Pallas kernels: 12.2 us -> 14.2 us  [down_grads(): pl.pallas_call(down_kernel, grid_spec=pltpu.PrefetchScalarGridSpec(num_sc...]
  transfers between devices with their start and end apart: 80 -> 80, of which waited for: 38 -> 27; matrix products, arithmetic and copies ran while one was open for 8% -> 7% of each run, Pallas kernels for 20% -> 34%
where the time goes in v3:
time: 420 us; the launch traced here: 416 us
  Pallas kernels  198 us (47%)
  starting transfers between devices  88.3 us (21%)
  waiting for transfers between devices  83.4 us (20%)
  other arithmetic  34.1 us (8%)
  local copies, waits for them, and re-layouts  9.96 us (2%)
    ppermute x80, starting transfers between devices, swap(): return lax.ppermute(value, axis, [(i, i ^ bit) for i in range(size)])  88.3 us
    ppermute x80, waiting for transfers between devices, swap(): return lax.ppermute(value, axis, [(i, i ^ bit) for i in range(size)])  83.4 us
    pallas_call x3, Pallas kernels, attend_back(): pl.pallas_call(functools.partial(attend_back_kernel, kb=kb), grid=(count,...  45.5 us
    pallas_call x1, Pallas kernels, mid1(): pl.pallas_call(functools.partial(mid1_kernel, count=len(pieces), R=R), gr...  35 us
    pallas_call x2, Pallas kernels, attend(): pl.pallas_call(functools.partial(attend_kernel, qb=qb), grid=(count,), in...  31 us
    pallas_call x3, Pallas kernels, pair_grads(): pl.pallas_call(functools.partial(pairs_kernel, groups=groups, total=total...  28 us
    pallas_call x1, Pallas kernels, mid2(): pl.pallas_call(functools.partial(mid2_kernel, count=len(pieces), R=R), gr...  25.8 us
    convert_element_type x12, other arithmetic, add(): return sum((t.astype(F32) for t in terms)).astype(BF)  14.9 us
  transfers between devices with their start and end apart: 80, of which 27 were waited for; matrix products, arithmetic and copies ran while one was open for 7% of the time, Pallas kernels for 34%

profile of v3, /device:TPU:0, one launch (start us, length us, event | category | flops | bytes accessed | tf_op | source)
XLA Modules:
  0.0 415.5 jit_solution(4468724828701248257)
XLA Ops:
  15.8 4.4 %collective-permute-done.10.refs_9_ = bf16[144,768]{1,0:T(8,128)(2,1)} collective-permute-done((bf16[144,768]{1,0:T(8,128)(2,1)S(1)}, bf16[144,768]{1,0:T(8,128)(2,1)}, u32[]{:S(2)}, u32[]{:S(2)}) %collective-permute-start.10) | collective-permute-done | bytes 221216 | tf_op jit(solution)/shard_map/ppermute | solution.py:509
  37.0 8.1 %collective-permute-done.17.refs_4_ = bf16[432,768]{1,0:T(8,128)(2,1)S(1)} collective-permute-done((bf16[432,768]{1,0:T(8,128)(2,1)}, bf16[432,768]{1,0:T(8,128)(2,1)S(1)}, u32[]{:S(2)}, u32[]{:S(2)}) %collective-permute-start.17) | collective-permute-done | bytes 663584 | tf_op jit(solution)/shard_map/ppermute | solution.py:509
  48.6 8.8 %qkv.1 = (bf16[1024,768]{1,0:T(8,128)(2,1)}, bf16[1024,768]{1,0:T(8,128)(2,1)}, bf16[1024,768]{1,0:T(8,128)(2,1)}) custom-call(s32[3]{0:T(128)} %pad_add_fusion.meta_ref, bf16[1024,768]{1,0:T(8,128)(2,1)} %bitcast.186, f32[8,768]{1,0:T(8,128)} %reshape.220.vec_ref, bf16[144,768]{1,0:T(8,128)(2,1)} %copy-done.8, bf16[144,768]{1,0:T(8,128)(2,1)} %copy-done.9, ...), custom_call_target="tpu_custom_call" | custom-call | flops 3623878656 | bytes 10000000 | tf_op jit(solution)/shard_map/qkv/pallas_call | solution.py:92
  57.4 11.0 %attend.2 = (bf16[1024,768]{1,0:T(8,128)(2,1)}, bf16[12,1024,128]{2,1,0:T(8,128)(2,1)}) custom-call(s32[3]{0:T(128)} %pad_add_fusion.meta_ref, bf16[1024,768]{1,0:T(8,128)(2,1)} %get-tuple-element.66.q_ref, bf16[1024,768]{1,0:T(8,128)(2,1)} %get-tuple-element.67.k_ref, bf16[1024,768]{1,0:T(8,128)(2,1)} %get-tuple-element.68.v_ref), custom_call_target="tpu_custom_call" | custom-call | flops 4800000000 | bytes 3000000 | tf_op jit(solution)/shard_map/attend/pallas_call | solution.py:185
  69.1 6.5 %collective-permute-done.27.refs_12_ = bf16[432,768]{1,0:T(8,128)(2,1)} collective-permute-done((bf16[432,768]{1,0:T(8,128)(2,1)S(1)}, bf16[432,768]{1,0:T(8,128)(2,1)}, u32[]{:S(2)}, u32[]{:S(2)}) %collective-permute-start.27) | collective-permute-done | bytes 663584 | tf_op jit(solution)/shard_map/ppermute | solution.py:509
  76.0 20.0 %attend.3 = (bf16[1024,768]{1,0:T(8,128)(2,1)}, bf16[12,1024,128]{2,1,0:T(8,128)(2,1)}) custom-call(s32[3]{0:T(128)} %pad_add_fusion.meta_ref, bf16[1024,768]{1,0:T(8,128)(2,1)} %get-tuple-element.66.q_ref, bf16[1024,768]{1,0:T(8,128)(2,1)} %get-tuple-element.67.k_ref, ...), custom_call_target="tpu_custom_call", output_to_operand_aliasing={{0}: (4, {}), {1}: (5, {})} | custom-call | flops 9600000000 | bytes 6000000 | tf_op jit(solution)/shard_map/attend/pallas_call | solution.py:185
  97.4 35.0 %mid1.1 = (bf16[1024,768]{1,0:T(8,128)(2,1)}, bf16[1024,768]{1,0:T(8,128)(2,1)}, bf16[1024,3072]{1,0:T(8,128)(2,1)}, bf16[1024,3072]{1,0:T(8,128)(2,1)}, bf16[10...) custom-call(s32[3]{0:T(128)} %pad_add_fusion.meta_ref, ...), custom_call_target="tpu_custom_call" | custom-call | flops 16000000000 | bytes 34000000 | tf_op jit(solution)/shard_map/mid1/pallas_call | solution.py:348
  132.4 7.1 %down_grads.2 = bf16[4,384,768]{2,1,0:T(8,128)(2,1)} custom-call(s32[3]{0:T(128)} %pad_add_fusion.meta_ref, bf16[1024,3072]{1,0:T(8,128)(2,1)} %get-tuple-element.76.act_ref, bf16[1024,768]{1,0:T(8,128)(2,1)} %get-tuple-element.77.db_ref), custom_call_target="tpu_custom_call" | custom-call | flops 2899102976 | bytes 7000000 | tf_op jit(solution)/shard_map/down_grads/pallas_call | solution.py:491
  139.5 7.1 %down_grads.3 = bf16[4,384,768]{2,1,0:T(8,128)(2,1)} custom-call(s32[3]{0:T(128)} %pad_add_fusion.meta_ref, bf16[1024,3072]{1,0:T(8,128)(2,1)} %get-tuple-element.76.act_ref, bf16[1024,768]{1,0:T(8,128)(2,1)} %get-tuple-element.77.db_ref), custom_call_target="tpu_custom_call" | custom-call | flops 2899102976 | bytes 7000000 | tf_op jit(solution)/shard_map/down_grads/pallas_call | solution.py:491
  152.0 25.8 %mid2.1 = (bf16[1024,3072]{1,0:T(8,128)(2,1)}, bf16[1024,768]{1,0:T(8,128)(2,1)}, bf16[1024,768]{1,0:T(8,128)(2,1)}, f32[16,768]{1,0:T(8,128)}) custom-call(s32[3]{0:T(128)} %pad_add_fusion.meta_ref, bf16[1024,768]{1,0:T(8,128)(2,1)} %get-tuple-element.77.db_ref, bf16[1024,3072]{1,0:T(8,128)(2,1)} %get-tuple-element.80.slope_ref, ...), custom_call_target="tpu_custom_call" | custom-call | flops 12000000000 | bytes 30000000 | tf_op jit(solution)/shard_map/mid2/pallas_call | solution.py:404
  179.9 13.9 %pair_grads.3 = (bf16[4,480,768]{2,1,0:T(8,128)(2,1)}, bf16[4,480,768]{2,1,0:T(8,128)(2,1)}) custom-call(s32[3]{0:T(128)} %pad_add_fusion.meta_ref, bf16[1024,768]{1,0:T(8,128)(2,1)} %get-tuple-element.86.refs_0_, bf16[1024,3072]{1,0:T(8,128)(2,1)} %get-tuple-element.87.refs_1_, bf16[1024,768]{1,0:T(8,128)(2,1)} %get-tuple-element.74.ctx_ref.refs_2_.o_ref, ...), custom_call_target="tpu_custom_call" | custom-call | flops 7247757312 | bytes 15000000 | tf_op jit(solution)/shard_map/pair_grads/pallas_call | solution.py:473
  195.9 7.7 %collective-permute-done.34 = bf16[192,768]{1,0:T(8,128)(2,1)} collective-permute-done((bf16[192,768]{1,0:T(8,128)(2,1)}, bf16[192,768]{1,0:T(8,128)(2,1)}, u32[]{:S(2)}, u32[]{:S(2)}) %collective-permute-start.34) | collective-permute-done | bytes 294944 | tf_op jit(solution)/shard_map/ppermute | solution.py:509
  206.2 3.6 collective-permute-start.39
  210.6 4.5 %collective-permute-done.39 = bf16[96,768]{1,0:T(8,128)(2,1)} collective-permute-done((bf16[96,768]{1,0:T(8,128)(2,1)}, bf16[96,768]{1,0:T(8,128)(2,1)}, u32[]{:S(2)}, u32[]{:S(2)}) %collective-permute-start.39) | collective-permute-done | bytes 147488 | tf_op jit(solution)/shard_map/ppermute | solution.py:509
  215.1 7.0 %collective-permute-done.38 = bf16[96,768]{1,0:T(8,128)(2,1)} collective-permute-done((bf16[96,768]{1,0:T(8,128)(2,1)}, bf16[96,768]{1,0:T(8,128)(2,1)}, u32[]{:S(2)}, u32[]{:S(2)}) %collective-permute-start.38) | collective-permute-done | bytes 147488 | tf_op jit(solution)/shard_map/ppermute | solution.py:509
  231.5 15.2 %attend_back.3 = (bf16[1024,768]{1,0:T(8,128)(2,1)}, bf16[1024,768]{1,0:T(8,128)(2,1)}, bf16[1024,768]{1,0:T(8,128)(2,1)}, f32[16,768]{1,0:T(8,128)}) custom-call(s32[3]{0:T(128)} %pad_add_fusion.meta_ref, bf16[12,1024,128]{2,1,0:T(8,128)(2,1)} %get-tuple-element.91.aug_ref, ...), custom_call_target="tpu_custom_call", output_to_operand_aliasing={{3}: (6, {})} | custom-call | flops 6800000000 | bytes 5000000 | tf_op jit(solution)/shard_map/attend_back/pallas_call | solution.py:260
  246.8 15.1 %attend_back.4 = (bf16[1024,768]{1,0:T(8,128)(2,1)}, bf16[1024,768]{1,0:T(8,128)(2,1)}, bf16[1024,768]{1,0:T(8,128)(2,1)}, f32[16,768]{1,0:T(8,128)}) custom-call(s32[3]{0:T(128)} %pad_add_fusion.meta_ref, bf16[12,1024,128]{2,1,0:T(8,128)(2,1)} %get-tuple-element.91.aug_ref, ...), custom_call_target="tpu_custom_call", output_to_operand_aliasing={{3}: (6, {}), {0}: (7, {}), {1}: (8, {}), {2}: (9, {})} | custom-call | flops 6800000000 | bytes 5000000 | tf_op jit(solution)/shard_map/attend_back/pallas_call | solution.py:260
  265.5 7.5 %pair_grads.4 = (bf16[4,288,512]{2,1,0:T(8,128)(2,1)}, bf16[4,288,512]{2,1,0:T(8,128)(2,1)}) custom-call(s32[3]{0:T(128)} %pad_add_fusion.meta_ref, bf16[1024,768]{1,0:T(8,128)(2,1)} %bitcast.188, bf16[1024,768]{1,0:T(8,128)(2,1)} %get-tuple-element.101.refs_1_.refs_0_, bf16[1024,768]{1,0:T(8,128)(2,1)} %bitcast.189, ...), custom_call_target="tpu_custom_call" | custom-call | flops 2899102976 | bytes 15000000 | tf_op jit(solution)/shard_map/pair_grads/pallas_call | solution.py:473
  273.0 15.3 %attend_back.5 = (bf16[1024,768]{1,0:T(8,128)(2,1)}, bf16[1024,768]{1,0:T(8,128)(2,1)}, bf16[1024,768]{1,0:T(8,128)(2,1)}, f32[16,768]{1,0:T(8,128)}) custom-call(s32[3]{0:T(128)} %pad_add_fusion.meta_ref, bf16[12,1024,128]{2,1,0:T(8,128)(2,1)} %get-tuple-element.91.aug_ref, ...), custom_call_target="tpu_custom_call", output_to_operand_aliasing={{3}: (6, {}), {0}: (7, {}), {1}: (8, {}), {2}: (9, {})} | custom-call | flops 6800000000 | bytes 5000000 | tf_op jit(solution)/shard_map/attend_back/pallas_call | solution.py:260
  313.0 9.0 %collective-permute-start.79 = (f32[16,768]{1,0:T(8,128)S(1)}, f32[16,768]{1,0:T(8,128)S(1)}, u32[]{:S(2)}, u32[]{:S(2)}) collective-permute-start(f32[16,768]{1,0:T(8,128)S(1)} %add.440), channel_id=1, source_target_pairs={{0,16},{8,24},{16,0},{24,8},{1,17},{9,25},{17,1},{25,9},{2,18},{10... | collective-permute-start | bytes 147464 | tf_op jit(solution)/shard_map/ppermute | solution.py:509
  322.0 4.4 %collective-permute-done.67 = bf16[120,768]{1,0:T(8,128)(2,1)S(1)} collective-permute-done((bf16[120,768]{1,0:T(8,128)(2,1)S(1)}, bf16[120,768]{1,0:T(8,128)(2,1)S(1)}, u32[]{:S(2)}, u32[]{:S(2)}) %collective-permute-start.67) | collective-permute-done | bytes 184352 | tf_op jit(solution)/shard_map/ppermute | solution.py:509
  333.2 11.5 %collective-permute-done.70 = bf16[120,768]{1,0:T(8,128)(2,1)S(1)} collective-permute-done((bf16[120,768]{1,0:T(8,128)(2,1)S(1)}, bf16[120,768]{1,0:T(8,128)(2,1)S(1)}, u32[]{:S(2)}, u32[]{:S(2)}) %collective-permute-start.70) | collective-permute-done | bytes 184352 | tf_op jit(solution)/shard_map/ppermute | solution.py:509
  358.8 6.7 %pair_grads.5 = (bf16[4,288,256]{2,1,0:T(8,128)(2,1)}, bf16[4,288,256]{2,1,0:T(8,128)(2,1)}) custom-call(s32[3]{0:T(128)} %pad_add_fusion.meta_ref, bf16[1024,768]{1,0:T(8,128)(2,1)} %bitcast.191, bf16[1024,768]{1,0:T(8,128)(2,1)} %get-tuple-element.109.refs_1_.dq_ref, bf16[1024,768]{1,0:T(8,128)(2,1)} %bitcast.192, ...), custom_call_target="tpu_custom_call" | custom-call | flops 1449551488 | bytes 15000000 | tf_op jit(solution)/shard_map/pair_grads/pallas_call | solution.py:473
  371.2 9.5 %input_grad.1 = bf16[1024,768]{1,0:T(8,128)(2,1)} custom-call(s32[3]{0:T(128)} %pad_add_fusion.meta_ref, bf16[1024,768]{1,0:T(8,128)(2,1)} %get-tuple-element.88.refs_3_.da_ref, bf16[1024,768]{1,0:T(8,128)(2,1)} %get-tuple-element.109.refs_1_.dq_ref, bf16[1024,768]{1,0:T(8,128)(2,1)} %get-tuple-element.110.refs_3_.dk_ref, ...), custom_call_target="tpu_custom_call" | custom-call | flops 3623878656 | bytes 13000000 | tf_op jit(solution)/shard_map/input_grad/pallas_call | solution.py:121
  (328 shorter events, 149.1 us)
Async XLA Ops:
  28.5 18.1 %collective-permute-start.19 = (bf16[432,768]{1,0:T(8,128)(2,1)}, bf16[432,768]{1,0:T(8,128)(2,1)S(1)}, u32[]{:S(2)}, u32[]{:S(2)}) collective-permute-start(bf16[432,768]{1,0:T(8,128)(2,1)} %copy-done.11), channel_id=1, source_target_pairs={{0,1},{1,0},{2,3},{3,2},{4,5},{5,4},{6,7},{7,6},{8,9},{9,8},{10,11... | collective-permute-start | bytes 1990664 | tf_op jit(solution)/shard_map/ppermute | solution.py:509
  28.5 18.1 %collective-permute-start.18 = (bf16[432,768]{1,0:T(8,128)(2,1)}, bf16[432,768]{1,0:T(8,128)(2,1)S(1)}, u32[]{:S(2)}, u32[]{:S(2)}) collective-permute-start(bf16[432,768]{1,0:T(8,128)(2,1)} %copy-done.10), channel_id=1, source_target_pairs={{0,4},{1,5},{2,6},{3,7},{4,0},{5,1},{6,2},{7,3},{8,12},{9,13},{10,... | collective-permute-start | bytes 1990664 | tf_op jit(solution)/shard_map/ppermute | solution.py:509
  36.3 32.1 %collective-permute-start.21 = (bf16[432,768]{1,0:T(8,128)(2,1)}, bf16[432,768]{1,0:T(8,128)(2,1)S(1)}, u32[]{:S(2)}, u32[]{:S(2)}) collective-permute-start(bf16[432,768]{1,0:T(8,128)(2,1)} %copy-done.10), channel_id=1, source_target_pairs={{0,2},{1,3},{2,0},{3,1},{4,6},{5,7},{6,4},{7,5},{8,10},{9,11},{10,... | collective-permute-start | bytes 1990664 | tf_op jit(solution)/shard_map/ppermute | solution.py:509
  45.1 23.4 %collective-permute-start.24 = (bf16[432,768]{1,0:T(8,128)(2,1)}, bf16[432,768]{1,0:T(8,128)(2,1)}, u32[]{:S(2)}, u32[]{:S(2)}) collective-permute-start(bf16[432,768]{1,0:T(8,128)(2,1)} %copy-done.11), channel_id=1, source_target_pairs={{0,4},{1,5},{2,6},{3,7},{4,0},{5,1},{6,2},{7,3},{8,12},{9,13},{10,... | collective-permute-start | bytes 1990664 | tf_op jit(solution)/shard_map/ppermute | solution.py:509
  46.6 22.4 %collective-permute-start.22 = (bf16[432,768]{1,0:T(8,128)(2,1)S(1)}, bf16[432,768]{1,0:T(8,128)(2,1)}, u32[]{:S(2)}, u32[]{:S(2)}) collective-permute-start(bf16[432,768]{1,0:T(8,128)(2,1)S(1)} %collective-permute-done.17.refs_4_), channel_id=1, source_target_pairs={{0,1},{1,0},{2,3},{3,2},{4,5},{5,4},{6,7},{7,6},{8,9},{9,8},{10,11... | collective-permute-start | bytes 1990664 | tf_op jit(solution)/shard_map/ppermute | solution.py:509
  46.6 28.9 %collective-permute-start.27 = (bf16[432,768]{1,0:T(8,128)(2,1)S(1)}, bf16[432,768]{1,0:T(8,128)(2,1)}, u32[]{:S(2)}, u32[]{:S(2)}) collective-permute-start(bf16[432,768]{1,0:T(8,128)(2,1)S(1)} %collective-permute-done.17.refs_4_), channel_id=1, source_target_pairs={{0,4},{1,5},{2,6},{3,7},{4,0},{5,1},{6,2},{7,3},{8,12},{9,13},{10,... | collective-permute-start | bytes 1990664 | tf_op jit(solution)/shard_map/ppermute | solution.py:509
  47.6 27.9 %collective-permute-start.28 = (bf16[432,768]{1,0:T(8,128)(2,1)S(1)}, bf16[432,768]{1,0:T(8,128)(2,1)}, u32[]{:S(2)}, u32[]{:S(2)}) collective-permute-start(bf16[432,768]{1,0:T(8,128)(2,1)S(1)} %collective-permute-done.18.refs_9_), channel_id=1, source_target_pairs={{0,2},{1,3},{2,0},{3,1},{4,6},{5,7},{6,4},{7,5},{8,10},{9,11},{10,... | collective-permute-start | bytes 1990664 | tf_op jit(solution)/shard_map/ppermute | solution.py:509
  68.4 27.7 %collective-permute-start.26 = (bf16[432,768]{1,0:T(8,128)(2,1)S(1)}, bf16[432,768]{1,0:T(8,128)(2,1)S(1)}, u32[]{:S(2)}, u32[]{:S(2)}) collective-permute-start(bf16[432,768]{1,0:T(8,128)(2,1)S(1)} %collective-permute-done.18.refs_9_), channel_id=1, source_target_pairs={{0,1},{1,0},{2,3},{3,2},{4,5},{5,4},{6,7},{7,6},{8,9},{9,8},{10,11... | collective-permute-start | bytes 1990664 | tf_op jit(solution)/shard_map/ppermute | solution.py:509
  68.5 27.5 %collective-permute-start.23 = (bf16[432,768]{1,0:T(8,128)(2,1)S(1)}, bf16[432,768]{1,0:T(8,128)(2,1)S(1)}, u32[]{:S(2)}, u32[]{:S(2)}) collective-permute-start(bf16[432,768]{1,0:T(8,128)(2,1)S(1)} %collective-permute-done.21.refs_5_), channel_id=1, source_target_pairs={{0,1},{1,0},{2,3},{3,2},{4,5},{5,4},{6,7},{7,6},{8,9},{9,8},{10,11... | collective-permute-start | bytes 1990664 | tf_op jit(solution)/shard_map/ppermute | solution.py:509
  69.0 27.1 %collective-permute-start.25 = (bf16[432,768]{1,0:T(8,128)(2,1)}, bf16[432,768]{1,0:T(8,128)(2,1)}, u32[]{:S(2)}, u32[]{:S(2)}) collective-permute-start(bf16[432,768]{1,0:T(8,128)(2,1)} %collective-permute-done.24.refs_8_), channel_id=1, source_target_pairs={{0,1},{1,0},{2,3},{3,2},{4,5},{5,4},{6,7},{7,6},{8,9},{9,8},{10,11... | collective-permute-start | bytes 1990664 | tf_op jit(solution)/shard_map/ppermute | solution.py:509
  75.5 20.6 %collective-permute-start.29 = (bf16[432,768]{1,0:T(8,128)(2,1)}, bf16[432,768]{1,0:T(8,128)(2,1)S(1)}, u32[]{:S(2)}, u32[]{:S(2)}) collective-permute-start(bf16[432,768]{1,0:T(8,128)(2,1)} %collective-permute-done.27.refs_12_), channel_id=1, source_target_pairs={{0,1},{1,0},{2,3},{3,2},{4,5},{5,4},{6,7},{7,6},{8,9},{9,8},{10,11... | collective-permute-start | bytes 1990664 | tf_op jit(solution)/shard_map/ppermute | solution.py:509
  75.5 20.6 %collective-permute-start.30 = (bf16[432,768]{1,0:T(8,128)(2,1)}, bf16[432,768]{1,0:T(8,128)(2,1)}, u32[]{:S(2)}, u32[]{:S(2)}) collective-permute-start(bf16[432,768]{1,0:T(8,128)(2,1)} %collective-permute-done.28.refs_13_), channel_id=1, source_target_pairs={{0,1},{1,0},{2,3},{3,2},{4,5},{5,4},{6,7},{7,6},{8,9},{9,8},{10,11... | collective-permute-start | bytes 1990664 | tf_op jit(solution)/shard_map/ppermute | solution.py:509
  149.0 28.8 %collective-permute-start.33 = (bf16[2,192,768]{2,1,0:T(8,128)(2,1)}, bf16[2,192,768]{2,1,0:T(8,128)(2,1)S(1)}, u32[]{:S(2)}, u32[]{:S(2)}) collective-permute-start(bf16[2,192,768]{2,1,0:T(8,128)(2,1)} %pad_maximum_fusion.5), channel_id=1, source_target_pairs={{0,4},{1,5},{2,6},{3,7},{4,0},{5,1},{6,2},{7,3},{8,12},{9,13},{10,... | collective-permute-start | bytes 1769480 | tf_op jit(solution)/shard_map/ppermute | solution.py:509
  151.4 26.4 %collective-permute-start.32 = (bf16[2,192,768]{2,1,0:T(8,128)(2,1)}, bf16[2,192,768]{2,1,0:T(8,128)(2,1)S(1)}, u32[]{:S(2)}, u32[]{:S(2)}) collective-permute-start(bf16[2,192,768]{2,1,0:T(8,128)(2,1)} %pad_maximum_fusion.4), channel_id=1, source_target_pairs={{0,2},{1,3},{2,0},{3,1},{4,6},{5,7},{6,4},{7,5},{8,10},{9,11},{10,... | collective-permute-start | bytes 1769480 | tf_op jit(solution)/shard_map/ppermute | solution.py:509
  193.8 31.3 %collective-permute-start.36 = (bf16[4,480,768]{2,1,0:T(8,128)(2,1)}, bf16[4,480,768]{2,1,0:T(8,128)(2,1)}, u32[]{:S(2)}, u32[]{:S(2)}) collective-permute-start(bf16[4,480,768]{2,1,0:T(8,128)(2,1)} %get-tuple-element.94), channel_id=1, source_target_pairs={{0,1},{1,0},{2,3},{3,2},{4,5},{5,4},{6,7},{7,6},{8,9},{9,8},{10,11... | collective-permute-start | bytes 8847368 | tf_op jit(solution)/shard_map/ppermute | solution.py:509
  225.1 72.2 %collective-permute-start.72 = (bf16[96,768]{1,0:T(8,128)(2,1)}, bf16[96,768]{1,0:T(8,128)(2,1)S(1)}, u32[]{:S(2)}, u32[]{:S(2)}) collective-permute-start(bf16[96,768]{1,0:T(8,128)(2,1)} %get-tuple-element.116), channel_id=1, source_target_pairs={{0,8},{8,0},{16,24},{24,16},{1,9},{9,1},{17,25},{25,17},{2,10},{10... | collective-permute-start | bytes 442376 | tf_op jit(solution)/shard_map/ppermute | solution.py:509
  227.7 34.1 %collective-permute-start.41 = (bf16[2,240,768]{2,1,0:T(8,128)(2,1)}, bf16[2,240,768]{2,1,0:T(8,128)(2,1)}, u32[]{:S(2)}, u32[]{:S(2)}) collective-permute-start(bf16[2,240,768]{2,1,0:T(8,128)(2,1)} %pad_maximum_fusion.2), channel_id=1, source_target_pairs={{0,4},{1,5},{2,6},{3,7},{4,0},{5,1},{6,2},{7,3},{8,12},{9,13},{10,... | collective-permute-start | bytes 2211848 | tf_op jit(solution)/shard_map/ppermute | solution.py:509
  230.1 31.7 %collective-permute-start.40 = (bf16[2,240,768]{2,1,0:T(8,128)(2,1)}, bf16[2,240,768]{2,1,0:T(8,128)(2,1)}, u32[]{:S(2)}, u32[]{:S(2)}) collective-permute-start(bf16[2,240,768]{2,1,0:T(8,128)(2,1)} %pad_maximum_fusion.1), channel_id=1, source_target_pairs={{0,2},{1,3},{2,0},{3,1},{4,6},{5,7},{6,4},{7,5},{8,10},{9,11},{10,... | collective-permute-start | bytes 2211848 | tf_op jit(solution)/shard_map/ppermute | solution.py:509
  264.3 37.4 %collective-permute-start.42 = (bf16[240,768]{1,0:T(8,128)(2,1)}, bf16[240,768]{1,0:T(8,128)(2,1)S(1)}, u32[]{:S(2)}, u32[]{:S(2)}) collective-permute-start(bf16[240,768]{1,0:T(8,128)(2,1)} %get-tuple-element.128), channel_id=1, source_target_pairs={{0,4},{1,5},{2,6},{3,7},{4,0},{5,1},{6,2},{7,3},{8,12},{9,13},{10,... | collective-permute-start | bytes 1105928 | tf_op jit(solution)/shard_map/ppermute | solution.py:509
  264.9 36.8 %collective-permute-start.43 = (bf16[240,768]{1,0:T(8,128)(2,1)}, bf16[240,768]{1,0:T(8,128)(2,1)}, u32[]{:S(2)}, u32[]{:S(2)}) collective-permute-start(bf16[240,768]{1,0:T(8,128)(2,1)} %get-tuple-element.127), channel_id=1, source_target_pairs={{0,2},{1,3},{2,0},{3,1},{4,6},{5,7},{6,4},{7,5},{8,10},{9,11},{10,... | collective-permute-start | bytes 1105928 | tf_op jit(solution)/shard_map/ppermute | solution.py:509
  298.0 46.7 %collective-permute-start.44 = (bf16[4,288,512]{2,1,0:T(8,128)(2,1)}, bf16[4,288,512]{2,1,0:T(8,128)(2,1)}, u32[]{:S(2)}, u32[]{:S(2)}) collective-permute-start(bf16[4,288,512]{2,1,0:T(8,128)(2,1)} %get-tuple-element.107), channel_id=1, source_target_pairs={{0,1},{1,0},{2,3},{3,2},{4,5},{5,4},{6,7},{7,6},{8,9},{9,8},{10,11... | collective-permute-start | bytes 3538952 | tf_op jit(solution)/shard_map/ppermute | solution.py:509
  306.2 20.2 %collective-permute-start.67 = (bf16[120,768]{1,0:T(8,128)(2,1)S(1)}, bf16[120,768]{1,0:T(8,128)(2,1)S(1)}, u32[]{:S(2)}, u32[]{:S(2)}) collective-permute-start(bf16[120,768]{1,0:T(8,128)(2,1)S(1)} %get-tuple-element.164), channel_id=1, source_target_pairs={{0,16},{8,24},{16,0},{24,8},{1,17},{9,25},{17,1},{25,9},{2,18},{10... | collective-permute-start | bytes 552968 | tf_op jit(solution)/shard_map/ppermute | solution.py:509
  306.2 20.2 %collective-permute-start.66 = (bf16[120,768]{1,0:T(8,128)(2,1)S(1)}, bf16[120,768]{1,0:T(8,128)(2,1)S(1)}, u32[]{:S(2)}, u32[]{:S(2)}) collective-permute-start(bf16[120,768]{1,0:T(8,128)(2,1)S(1)} %get-tuple-element.162), channel_id=1, source_target_pairs={{0,8},{8,0},{16,24},{24,16},{1,9},{9,1},{17,25},{25,17},{2,10},{10... | collective-permute-start | bytes 552968 | tf_op jit(solution)/shard_map/ppermute | solution.py:509
  365.5 19.9 %collective-permute-start.55 = (bf16[4,288,256]{2,1,0:T(8,128)(2,1)}, bf16[4,288,256]{2,1,0:T(8,128)(2,1)S(1)}, u32[]{:S(2)}, u32[]{:S(2)}) collective-permute-start(bf16[4,288,256]{2,1,0:T(8,128)(2,1)} %get-tuple-element.114), channel_id=1, source_target_pairs={{0,1},{1,0},{2,3},{3,2},{4,5},{5,4},{6,7},{7,6},{8,9},{9,8},{10,11... | collective-permute-start | bytes 1769480 | tf_op jit(solution)/shard_map/ppermute | solution.py:509
  (92 other events, 816.6 us)
